TPU v7x, 128 devices: a whole 4x4x4 slice. The times are simulated.
128 devices in a mesh: dp: 2 (over x_lo), expert: 32 (over y, z, core), tensor: 2 (over x_hi).
Axes of the slice: x: 4 (x_hi: 2, x_lo: 2; x = x_hi * 2 + x_lo), y: 4, z: 4, core: 2. Of those that a mesh axis runs over, the one named last changes fastest.
Arguments:
- tokens: bfloat16 [8192, 2048], P(('dp', 'expert')), may hold values from -6 to 6
- norm_gain: float32 [2048], replicated, may hold values from 0.1 to 1.9
- router: bfloat16 [2048, 32], replicated, may hold values from -0.125 to 0.125
- expert_ids: int32 [8192, 4], P(('dp', 'expert')), may hold values from 0 to 31, all different within a row; in each aligned block of 128 rows (0 to 127, 128 to 255, ...) at most 20 rows name the same one
- modality: int32 [8192], P(('dp', 'expert')), may hold values from 0 to 1, as said below
- expert_gate: bfloat16 [32, 2048, 1408], P('expert', None, 'tensor'), may hold values from -0.125 to 0.125
- expert_up: bfloat16 [32, 2048, 1408], P('expert', None, 'tensor'), may hold values from -0.125 to 0.125
- expert_down: bfloat16 [32, 1408, 2048], P('expert', 'tensor'), may hold values from -0.15625 to 0.15625
- shared_gate: bfloat16 [2, 2048, 704], P(None, None, ('dp', 'tensor')), may hold values from -0.125 to 0.125
- shared_up: bfloat16 [2, 2048, 704], P(None, None, ('dp', 'tensor')), may hold values from -0.125 to 0.125
- shared_down: bfloat16 [2, 704, 2048], P(None, ('dp', 'tensor')), may hold values from -0.21875 to 0.21875
Outputs:
- mixed: bfloat16 [8192, 2048], P(('dp', 'expert'), 'tensor')
Inputs may be any that keep to these rules, and one draw needn't show every extreme that they name: `expert_ids`: each token names 4 different experts; among the 128 tokens of one device (aligned blocks of rows) no expert is named by more than 20 tokens, and some expert reaches 20. `modality`: within each aligned block of 128 tokens the image patches form one run (taken cyclically) that covers from an eighth to seven eighths of the block.
All inputs are finite; a program needn't handle non-finite values.
Results may differ from a plain program's by a relative error of at most 0.0073.
Values may be sent and summed in bfloat16 or wider, within the bound.
No kernel may reach another device: no remote copies, remote signals or barrier semaphores. Data moves between devices by JAX's collectives and lax.ppermute only.
A program may use at most 128 MiB of HBM per device.

v0:
```python
import jax
import jax.numpy as jnp
from jax import lax
from jax.sharding import PartitionSpec as P

epsilon = 1e-06


def in_blocks(x, dim, size):
    lengths = x.shape
    tiles = x.reshape(*lengths[:dim], size, lengths[dim] // size, *lengths[dim + 1 :])
    return jnp.moveaxis(tiles, dim, 0)


def sent_and_summed(x, axis, dim):
    tiles = in_blocks(x, dim, lax.axis_size(axis))
    arrived = lax.all_to_all(tiles, axis, split_axis=0, concat_axis=0, tiled=True)
    return arrived.astype(jnp.float32).sum(axis=0)


def sent_to_all(x, axis):
    size = lax.axis_size(axis)
    return lax.all_to_all(jnp.broadcast_to(x[None], (size, *x.shape)), axis, 0, 0, tiled=True)


def joined_along(tiles, dim):
    lengths = list(tiles.shape[1:])
    lengths[dim] *= tiles.shape[0]
    return jnp.moveaxis(tiles, 0, dim).reshape(lengths)


def collect(x, axis, dim):
    tiles = sent_to_all(x, axis)
    return joined_along(tiles, dim)


def rms_normed(tokens, norm_gain):
    values = tokens.astype(jnp.float32)
    inv_scale = lax.rsqrt(jnp.mean(values * values, axis=-1, keepdims=True) + epsilon)
    return (values * inv_scale * norm_gain).astype(jnp.bfloat16)


def route_weights(normed, router, expert_ids):
    logits = jnp.dot(normed, router, preferred_element_type=jnp.float32)
    chosen = jnp.take_along_axis(logits, expert_ids, axis=1)
    scores = jax.nn.sigmoid(chosen)
    return scores / jnp.sum(scores, axis=1, keepdims=True)


def capacity_slots(expert_ids, expert_count, block_rows):
    row_count, top_count = expert_ids.shape
    onehot = (
        expert_ids[:, :, None] == jnp.arange(expert_count, dtype=jnp.int32)[None, None, :]
    ).astype(jnp.int32)
    grouped = onehot.reshape(row_count // block_rows, block_rows * top_count, expert_count)
    running = (jnp.cumsum(grouped, axis=1, dtype=jnp.int32) - 1).reshape(
        row_count, top_count, expert_count
    )
    return jnp.sum(running * onehot, axis=-1, dtype=jnp.int32)


def per_device(
    tokens,
    norm_gain,
    router,
    expert_ids,
    modality,
    expert_gate,
    expert_up,
    expert_down,
    shared_gate,
    shared_up,
    shared_down,
):
    normed = rms_normed(tokens, norm_gain)
    weights = route_weights(normed, router, expert_ids)
    tok_rows, model_width = normed.shape
    top_count = expert_ids.shape[1]
    groups = lax.axis_size("expert")
    pair_count = lax.axis_size("tensor")
    dp_count = lax.axis_size("dp")
    half_width = model_width // pair_count
    expert_count = groups * expert_gate.shape[0]
    capacity = pair_count * (
        (5 * tok_rows * top_count + 4 * expert_count * pair_count - 1)
        // (4 * expert_count * pair_count)
    )
    slot_rank = capacity_slots(expert_ids, expert_count, tok_rows)
    target = expert_ids * capacity + slot_rank
    positions = jnp.arange(expert_count * capacity, dtype=jnp.int32)
    placing = jnp.any(positions[:, None, None] == target[None, :, :], axis=2).astype(jnp.bfloat16)
    outgoing = jnp.dot(placing, normed, preferred_element_type=jnp.float32).astype(jnp.bfloat16)
    outgoing = outgoing.reshape(groups, capacity, model_width)
    received = lax.all_to_all(outgoing, "expert", split_axis=0, concat_axis=0, tiled=True)
    flat_rows = received.reshape(-1, model_width)
    gate_value = jnp.dot(flat_rows, expert_gate[0], preferred_element_type=jnp.float32)
    up_value = jnp.dot(flat_rows, expert_up[0], preferred_element_type=jnp.float32)
    hidden = (jax.nn.silu(gate_value) * up_value).astype(jnp.bfloat16)
    result = jnp.dot(hidden, expert_down[0], preferred_element_type=jnp.float32)
    partials = result.reshape(received.shape[0], received.shape[1], model_width)
    reduced = sent_and_summed(partials.astype(jnp.bfloat16), "tensor", 2)
    returned = lax.all_to_all(
        reduced.astype(jnp.bfloat16), "expert", split_axis=0, concat_axis=0, tiled=True
    ).astype(reduced.dtype)
    picked = returned.reshape(-1, returned.shape[2])[target]
    routed = jnp.sum(weights[:, :, None] * picked, axis=1)
    everyone, kind_flags = (collect(normed, "dp", 0), collect(modality, "dp", 0))
    image_flag = kind_flags.astype(jnp.float32)[:, None]

    def shared_hidden(modal_index, keep):
        gate_value = jnp.dot(everyone, shared_gate[modal_index], preferred_element_type=jnp.float32)
        up_value = jnp.dot(everyone, shared_up[modal_index], preferred_element_type=jnp.float32)
        return (jax.nn.silu(gate_value) * up_value * keep).astype(jnp.bfloat16)

    joined = jnp.concatenate(
        [shared_hidden(0, image_flag), shared_hidden(1, 1.0 - image_flag)], axis=1
    )
    down_blocks = shared_down.reshape(-1, pair_count, half_width)
    split_rows = joined.reshape(dp_count, tok_rows, joined.shape[1])
    shared_term = jnp.einsum(
        "pks,std->ptkd", split_rows, down_blocks, preferred_element_type=jnp.float32
    )
    shared_sum = sent_and_summed(
        shared_term.reshape(-1, half_width).astype(jnp.bfloat16), ("dp", "tensor"), 0
    )
    total = shared_sum + routed
    return total.astype(jnp.bfloat16)


def solution(mesh):
    in_specs = (
        P(("dp", "expert"), None),
        P(),
        P(),
        P(("dp", "expert"), None),
        P(("dp", "expert")),
        P("expert", None, "tensor"),
        P("expert", None, "tensor"),
        P("expert", "tensor", None),
        P(None, None, ("dp", "tensor")),
        P(None, None, ("dp", "tensor")),
        P(None, ("dp", "tensor"), None),
    )
    out_specs = P(("dp", "expert"), "tensor")
    return jax.shard_map(
        per_device, mesh=mesh, in_specs=in_specs, out_specs=out_specs, check_vma=False
    )
```

profile of v0, /device:TPU:0, one launch (start us, length us, event | category | flops | bytes accessed | tf_op | source)
XLA Modules:
  0.0 195.1 jit_solution(18191164852900598706)
XLA Ops:
  1.4 3.2 %all-to-all-start.1 = ((s32[2,1,128]{2,1,0:T(1,128)}), s32[2,1,128]{2,1,0:T(1,128)S(1)}, u32[]{:S(2)}, u32[]{:S(2)}) async-start(s32[2,1,128]{2,1,0:T(1,128)} %broadcast_in_dim.11), calls=%async_computation.1 | async-start | bytes 2048 | tf_op jit(solution)/shard_map/all_to_all | solution.py:23
  13.2 5.2 %reshape.188 = bf16[32,20,2048]{2,1,0:T(8,128)(2,1)} reshape(bf16[640,2048]{1,0:T(8,128)(2,1)} %convolution_convert_fusion.1) | data formatting | bytes 5242880 | tf_op jit(solution)/shard_map/reshape | solution.py:93
  18.4 8.6 %all-to-all-start.3 = ((bf16[32,20,2048]{2,1,0:T(8,128)(2,1)}), bf16[32,20,2048]{2,1,0:T(8,128)(2,1)}, u32[]{:S(2)}, u32[]{:S(2)}) async-start(bf16[32,20,2048]{2,1,0:T(8,128)(2,1)} %reshape.188), calls=%async_computation.3 | async-start | bytes 6291456 | tf_op jit(solution)/shard_map/all_to_all | solution.py:94
  26.9 4.7 %reshape.181 = bf16[352,2,1024]{2,1,0:T(2,128)(2,1)} reshape(bf16[2,176,2048]{2,1,0:T(8,128)(2,1)} %param.21) | data formatting | bytes 2883584 | tf_op jit(solution)/shard_map/reshape | solution.py:118
  31.7 35.4 %all-to-all-done.3 = bf16[32,20,2048]{2,1,0:T(8,128)(2,1)} async-done(((bf16[32,20,2048]{2,1,0:T(8,128)(2,1)}), bf16[32,20,2048]{2,1,0:T(8,128)(2,1)}, u32[]{:S(2)}, u32[]{:S(2)}) %all-to-all-start.3) | async-done | bytes 2621472 | tf_op jit(solution)/shard_map/all_to_all | solution.py:94
  68.3 4.4 %all-to-all-start = ((bf16[2,128,2048]{2,1,0:T(8,128)(2,1)}), bf16[2,128,2048]{2,1,0:T(8,128)(2,1)}, u32[]{:S(2)}, u32[]{:S(2)}) async-start(bf16[2,128,2048]{2,1,0:T(8,128)(2,1)} %broadcast_in_dim.10), calls=%async_computation | async-start | bytes 2097152 | tf_op jit(solution)/shard_map/all_to_all | solution.py:23
  72.7 5.2 %reshape.189 = bf16[640,2048]{1,0:T(8,128)(2,1)} reshape(bf16[32,20,2048]{2,1,0:T(8,128)(2,1)} %all-to-all-done.3) | data formatting | bytes 5242880 | tf_op jit(solution)/shard_map/reshape | solution.py:95
  77.9 5.2 %fusion.3 = f32[640,704]{0,1:T(8,128)S(1)} fusion(bf16[640,2048]{1,0:T(8,128)(2,1)} %reshape.189, bf16[1,2048,704]{1,2,0:T(8,128)(2,1)} %param.16), kind=kOutput, calls=%fused_computation.7 | convolution fusion | flops 1845493760 | bytes 7307264 | tf_op jit(solution)/shard_map/dot_general | solution.py:96
  83.1 3.4 %multiply_convert_fusion = bf16[640,704]{0,1:T(8,128)(2,1)} fusion(f32[640,704]{0,1:T(8,128)S(1)} %fusion.3, bf16[640,2048]{1,0:T(8,128)(2,1)S(1)} %copy-done.1, bf16[1,2048,704]{1,2,0:T(8,128)(2,1)S(1)} %copy-done.3), kind=kOutput, calls=%fused_computation.12 | convolution fusion | flops 1848197120 | bytes 8208384 | tf_op jit(solution)/shard_map/dot_general | solution.py:97
  90.9 3.5 %convolution_convert_fusion = bf16[32,20,2048]{2,0,1:T(8,128)(2,1)S(1)} fusion(bf16[1,704,2048]{2,1,0:T(8,128)(2,1)S(1)} %copy-done, bf16[32,20,704]{2,1,0:T(8,128)(2,1)} %dot_general.41), kind=kOutput, calls=%fused_computation.2 | convolution fusion | flops 1846804480 | bytes 6406144 | tf_op jit(solution)/shard_map/dot_general | solution.py:99
  96.2 5.2 %all-to-all-start.4 = ((bf16[2,32,20,1024]{3,1,2,0:T(8,128)(2,1)}), bf16[2,32,20,1024]{3,1,2,0:T(8,128)(2,1)}, u32[]{:S(2)}, u32[]{:S(2)}) async-start(bf16[2,32,20,1024]{3,1,2,0:T(8,128)(2,1)} %bitcast.68), calls=%async_computation.4 | async-start | bytes 5242880 | tf_op jit(solution)/shard_map/all_to_all | solution.py:17
  111.2 3.2 %convolution_convert_fusion.2 = bf16[2,128,2,1024]{3,1,2,0:T(8,128)(2,1)} fusion(bf16[352,2,1024]{2,1,0:T(2,128)(2,1)} %reshape.181, bf16[2,128,352,1]{1,0,2,3:T(2,128)(2,1)} %bitcast.71), kind=kOutput, calls=%fused_computation.13 | convolution fusion | flops 369623040 | bytes 2670592 | tf_op jit(solution)/shard_map/pks,std->ptkd/dot_general | solution.py:120
  114.4 19.1 %all-to-all-done.4 = bf16[2,32,20,1024]{3,1,2,0:T(8,128)(2,1)} async-done(((bf16[2,32,20,1024]{3,1,2,0:T(8,128)(2,1)}), bf16[2,32,20,1024]{3,1,2,0:T(8,128)(2,1)}, u32[]{:S(2)}, u32[]{:S(2)}) %all-to-all-start.4) | async-done | bytes 2621472 | tf_op jit(solution)/shard_map/all_to_all | solution.py:17
  133.6 4.2 %all-to-all-start.2 = ((bf16[4,128,1024]{2,1,0:T(8,128)(2,1)}), bf16[4,128,1024]{2,1,0:T(8,128)(2,1)}, u32[]{:S(2)}, u32[]{:S(2)}) async-start(bf16[4,128,1024]{2,1,0:T(8,128)(2,1)} %bitcast.69), calls=%async_computation.2 | async-start | bytes 2097152 | tf_op jit(solution)/shard_map/all_to_all | solution.py:17
  137.8 3.8 %reduce_sum.64 = bf16[32,20,1024]{2,0,1:T(8,128)(2,1)} reduce(bf16[2,32,20,1024]{3,1,2,0:T(8,128)(2,1)} %all-to-all-done.4, bf16[]{:T(256)} %constant.46.clone.1), dimensions={0}, to_apply=%region_7.8 | reduce | flops 655360 | bytes 3932162 | tf_op jit(solution)/shard_map/reduce_sum | solution.py:18
  141.6 3.2 %copy.101 = bf16[32,20,1024]{2,1,0:T(8,128)(2,1)} copy(bf16[32,20,1024]{2,0,1:T(8,128)(2,1)} %reduce_sum.64) | data formatting | bytes 2621440 | tf_op jit(solution)/shard_map/reduce_sum | solution.py:18
  144.8 7.3 %all-to-all-done.2 = bf16[4,128,1024]{2,1,0:T(8,128)(2,1)} async-done(((bf16[4,128,1024]{2,1,0:T(8,128)(2,1)}), bf16[4,128,1024]{2,1,0:T(8,128)(2,1)}, u32[]{:S(2)}, u32[]{:S(2)}) %all-to-all-start.2) | async-done | bytes 1048608 | tf_op jit(solution)/shard_map/all_to_all | solution.py:17
  152.1 4.7 %all-to-all-start.5 = ((bf16[32,20,1024]{2,1,0:T(8,128)(2,1)}), bf16[32,20,1024]{2,1,0:T(8,128)(2,1)}, u32[]{:S(2)}, u32[]{:S(2)}) async-start(bf16[32,20,1024]{2,1,0:T(8,128)(2,1)} %copy.101), calls=%async_computation.5 | async-start | bytes 3145728 | tf_op jit(solution)/shard_map/all_to_all | solution.py:102
  158.4 3.8 %gather_fusion.1 = f32[512]{0:T(512)S(1)} fusion(f32[128,32]{0,1:T(8,128)S(1)} %fusion.30, s32[512]{0:T(512)S(1)} %reshape.204), kind=kCustom, calls=%fused_computation.1 | custom fusion | bytes 8192 | tf_op jit(solution)/shard_map/jit(take_along_axis)/gather | solution.py:45
  164.1 15.7 %all-to-all-done.5 = bf16[32,20,1024]{2,1,0:T(8,128)(2,1)} async-done(((bf16[32,20,1024]{2,1,0:T(8,128)(2,1)}), bf16[32,20,1024]{2,1,0:T(8,128)(2,1)}, u32[]{:S(2)}, u32[]{:S(2)}) %all-to-all-start.5) | async-done | bytes 1310752 | tf_op jit(solution)/shard_map/all_to_all | solution.py:102
  179.7 3.4 %reshape.195 = f32[640,1024]{1,0:T(8,128)} reshape(bf16[32,20,1024]{2,1,0:T(8,128)(2,1)} %all-to-all-done.5) | data formatting | bytes 3932160 | tf_op jit(solution)/shard_map/reshape | solution.py:105
  183.1 5.3 %gather_fusion = f32[512,1024]{1,0:T(8,128)} fusion(f32[640,1024]{1,0:T(8,128)} %reshape.195, s32[1024]{0:T(1024)S(1)} %pad_clamp_fusion), kind=kCustom, calls=%fused_computation | custom fusion | bytes 4196352 | tf_op jit(solution)/shard_map/gather | solution.py:105
  188.4 2.9 %reshape.197 = f32[128,4,1024]{2,1,0:T(4,128)} reshape(f32[512,1024]{1,0:T(8,128)} %gather_fusion) | data formatting | bytes 4194304 | tf_op jit(solution)/shard_map/gather | solution.py:105
  191.3 3.0 %multiply_reduce_fusion = f32[128,1024]{1,0:T(8,128)S(1)} fusion(f32[128,4,1024]{2,1,0:T(4,128)} %reshape.197, f32[128,4]{1,0:T(8,128)S(1)} %copy.91), kind=kLoop, calls=%fused_computation.10 | loop fusion | flops 917504 | bytes 2623488 | tf_op jit(solution)/shard_map/reduce_sum | solution.py:106
  (59 shorter events, 31.3 us)
Async XLA Ops:
  0.0 90.9 %copy-start = (bf16[1,704,2048]{2,1,0:T(8,128)(2,1)S(1)}, bf16[1,704,2048]{2,1,0:T(8,128)(2,1)}, u32[]{:S(2)}) copy-start(bf16[1,704,2048]{2,1,0:T(8,128)(2,1)} %param.18) | copy-start | bytes 8650756
  1.4 17.0 %all-to-all-start.1 = ((s32[2,1,128]{2,1,0:T(1,128)}), s32[2,1,128]{2,1,0:T(1,128)S(1)}, u32[]{:S(2)}, u32[]{:S(2)}) async-start(s32[2,1,128]{2,1,0:T(1,128)} %broadcast_in_dim.11), calls=%async_computation.1 | async-start | bytes 2048 | tf_op jit(solution)/shard_map/all_to_all | solution.py:23
  18.4 48.7 %all-to-all-start.3 = ((bf16[32,20,2048]{2,1,0:T(8,128)(2,1)}), bf16[32,20,2048]{2,1,0:T(8,128)(2,1)}, u32[]{:S(2)}, u32[]{:S(2)}) async-start(bf16[32,20,2048]{2,1,0:T(8,128)(2,1)} %reshape.188), calls=%async_computation.3 | async-start | bytes 6291456 | tf_op jit(solution)/shard_map/all_to_all | solution.py:94
  68.3 27.9 %all-to-all-start = ((bf16[2,128,2048]{2,1,0:T(8,128)(2,1)}), bf16[2,128,2048]{2,1,0:T(8,128)(2,1)}, u32[]{:S(2)}, u32[]{:S(2)}) async-start(bf16[2,128,2048]{2,1,0:T(8,128)(2,1)} %broadcast_in_dim.10), calls=%async_computation | async-start | bytes 2097152 | tf_op jit(solution)/shard_map/all_to_all | solution.py:23
  77.9 5.2 %copy-start.1 = (bf16[640,2048]{1,0:T(8,128)(2,1)S(1)}, bf16[640,2048]{1,0:T(8,128)(2,1)}, u32[]{:S(2)}) copy-start(bf16[640,2048]{1,0:T(8,128)(2,1)} %reshape.189) | copy-start | bytes 7864324
  77.9 5.2 %copy-start.3 = (bf16[1,2048,704]{1,2,0:T(8,128)(2,1)S(1)}, bf16[1,2048,704]{1,2,0:T(8,128)(2,1)}, u32[]{:S(2)}) copy-start(bf16[1,2048,704]{1,2,0:T(8,128)(2,1)} %param.17) | copy-start | bytes 8650756
  96.2 37.3 %all-to-all-start.4 = ((bf16[2,32,20,1024]{3,1,2,0:T(8,128)(2,1)}), bf16[2,32,20,1024]{3,1,2,0:T(8,128)(2,1)}, u32[]{:S(2)}, u32[]{:S(2)}) async-start(bf16[2,32,20,1024]{3,1,2,0:T(8,128)(2,1)} %bitcast.68), calls=%async_computation.4 | async-start | bytes 5242880 | tf_op jit(solution)/shard_map/all_to_all | solution.py:17
  101.4 4.0 %copy-start.4 = (bf16[2,2048,176]{1,2,0:T(8,128)(2,1)S(1)}, bf16[2,2048,176]{1,2,0:T(8,128)(2,1)}, u32[]{:S(2)}) copy-start(bf16[2,2048,176]{1,2,0:T(8,128)(2,1)} %param.20) | copy-start | bytes 4325380
  133.6 18.5 %all-to-all-start.2 = ((bf16[4,128,1024]{2,1,0:T(8,128)(2,1)}), bf16[4,128,1024]{2,1,0:T(8,128)(2,1)}, u32[]{:S(2)}, u32[]{:S(2)}) async-start(bf16[4,128,1024]{2,1,0:T(8,128)(2,1)} %bitcast.69), calls=%async_computation.2 | async-start | bytes 2097152 | tf_op jit(solution)/shard_map/all_to_all | solution.py:17
  144.8 12.2 %copy-start.2 = (s32[128,4]{0,1:T(4,128)S(1)}, s32[128,4]{0,1:T(4,128)}, u32[]{:S(2)}) copy-start(s32[128,4]{0,1:T(4,128)} %param.14) | copy-start | bytes 6148
  152.1 27.6 %all-to-all-start.5 = ((bf16[32,20,1024]{2,1,0:T(8,128)(2,1)}), bf16[32,20,1024]{2,1,0:T(8,128)(2,1)}, u32[]{:S(2)}, u32[]{:S(2)}) async-start(bf16[32,20,1024]{2,1,0:T(8,128)(2,1)} %copy.101), calls=%async_computation.5 | async-start | bytes 3145728 | tf_op jit(solution)/shard_map/all_to_all | solution.py:102
where the time goes:
time: 197 us; the launch traced here: 195 us
  waiting for transfers between devices  77.5 us (39%)
  local copies, waits for them, and re-layouts  46.3 us (24%)
  starting transfers between devices  30.3 us (15%)
  matrix products  26.3 us (13%)
  other arithmetic  14.5 us (7%)
    all_to_all x1, waiting for transfers between devices, per_device(): lax.all_to_all(outgoing, 'expert', split_axis=0, concat_axis=0, tiled=True)  35.4 us
    all_to_all x2, waiting for transfers between devices, sent_and_summed(): lax.all_to_all(tiles, axis, split_axis=0, concat_axis=0, tiled=True)  26.4 us
    all_to_all x1, waiting for transfers between devices, per_device(): lax.all_to_all(reduced.astype(jnp.bfloat16), 'expert', split_axis=0, conc...  15.7 us
    all_to_all x2, starting transfers between devices, sent_and_summed(): lax.all_to_all(tiles, axis, split_axis=0, concat_axis=0, tiled=True)  9.41 us
    all_to_all x1, starting transfers between devices, per_device(): lax.all_to_all(outgoing, 'expert', split_axis=0, concat_axis=0, tiled=True)  8.56 us
    gather x2, local copies, waits for them, and re-layouts, per_device(): picked = returned.reshape(-1, returned.shape[2])[target]  8.21 us
    all_to_all x2, starting transfers between devices, sent_to_all(): lax.all_to_all(jnp.broadcast_to(x[None], (size, *x.shape)), axis, 0, 0, t...  7.59 us
    reduce_sum x2, other arithmetic, sent_and_summed(): return arrived.astype(jnp.float32).sum(axis=0)  5.28 us
  transfers between devices with their start and end apart: 6, of which 4 were waited for; matrix products, arithmetic and copies ran while one was open for 35% of the time, Pallas kernels for 0%

commit v1 on v0

v1 whole, which is shorter than its diff:
```python
import functools

import jax
import jax.numpy as jnp
from jax import lax
from jax.experimental import pallas as pl
from jax.experimental.pallas import tpu as pltpu
from jax.sharding import PartitionSpec as P

epsilon = 1e-06
f32 = jnp.float32
bf16 = jnp.bfloat16

EX = 32
TK = 128
MAIN = 16
REST = 4
BLK = 2 * (MAIN + REST)


def normalise(values, gain):
    values = values.astype(f32)
    inv_scale = lax.rsqrt(jnp.mean(values * values, axis=-1, keepdims=True) + epsilon)
    return (values * inv_scale * gain).astype(bf16)


def dot(a, b):
    return jnp.dot(a, b, preferred_element_type=f32)


def dot_t(a, b):
    return lax.dot_general(a, b, (((1,), (1,)), ((), ())), preferred_element_type=f32)


def place_kernel(tok_ref, gain_ref, ids_ref, out_ref, normed_ref, rank_ref):
    normed = normalise(tok_ref[...], gain_ref[...])
    normed_ref[...] = normed
    ids = ids_ref[...]
    expert = lax.broadcasted_iota(jnp.int32, (EX, TK), 0)
    named = ids[0:1] == expert
    for k in range(1, ids.shape[0]):
        named = named | (ids[k : k + 1] == expert)
    ones = jnp.where(named, 1.0, 0.0)
    before = lax.broadcasted_iota(jnp.int32, (TK, TK), 0) < lax.broadcasted_iota(
        jnp.int32, (TK, TK), 1
    )
    rank = dot(ones.astype(bf16), jnp.where(before, 1.0, 0.0).astype(bf16))
    rank = jnp.where(named, rank, -1.0)
    rank_ref[...] = rank
    half = normed.shape[1] // 2
    slot = lax.broadcasted_iota(jnp.int32, (EX, MAIN, TK), 1).astype(f32)
    main = jnp.where(rank[:, None, :] == slot, 1.0, 0.0).astype(bf16).reshape(EX * MAIN, TK)
    row = lax.broadcasted_iota(jnp.int32, (EX, 2 * REST, TK), 1)
    wanted = (row % REST + MAIN).astype(f32)
    rest = jnp.where(rank[:, None, :] == wanted, 1.0, 0.0)
    rest_lo = jnp.where(row < REST, rest, 0.0).astype(bf16).reshape(EX * 2 * REST, TK)
    rest_hi = jnp.where(row >= REST, rest, 0.0).astype(bf16).reshape(EX * 2 * REST, TK)
    step = 256
    for c in range(0, half, step):
        lo = normed[:, c : c + step]
        hi = normed[:, half + c : half + c + step]
        out_ref[:, 0:MAIN, c : c + step] = dot(main, lo).astype(bf16).reshape(EX, MAIN, step)
        out_ref[:, MAIN : 2 * MAIN, c : c + step] = (
            dot(main, hi).astype(bf16).reshape(EX, MAIN, step)
        )
        both = dot(rest_lo, lo) + dot(rest_hi, hi)
        out_ref[:, 2 * MAIN : BLK, c : c + step] = both.reshape(EX, 2 * REST, step).astype(bf16)


def weigh_kernel(normed_ref, router_ref, rank_ref, main_ref, rest_ref):
    rank = rank_ref[...]
    logits = dot_t(router_ref[...], normed_ref[...])
    scores = jnp.where(rank >= 0.0, jax.nn.sigmoid(logits), 0.0)
    weights = scores / jnp.sum(scores, axis=0, keepdims=True)
    slot = lax.broadcasted_iota(jnp.int32, (EX, MAIN, TK), 1).astype(f32)
    main = jnp.where(rank[:, None, :] == slot, weights[:, None, :], 0.0)
    main = main.reshape(EX * MAIN, TK).T
    coarse = main.astype(bf16)
    main_ref[0:TK, :] = coarse
    main_ref[TK:, :] = (main - coarse.astype(f32)).astype(bf16)
    row = lax.broadcasted_iota(jnp.int32, (EX, 2 * REST, TK), 1)
    wanted = (row % REST + MAIN).astype(f32)
    rest = jnp.where(rank[:, None, :] == wanted, weights[:, None, :], 0.0)
    for h in range(2):
        part = jnp.where((row < REST) == (h == 0), rest, 0.0)
        part = part.reshape(EX * 2 * REST, TK).T
        coarse = part.astype(bf16)
        rest_ref[h, 0:TK, :] = coarse
        rest_ref[h, TK:, :] = (part - coarse.astype(f32)).astype(bf16)


def shared_kernel(
    side_ref, normed_ref, other_ref, gain_ref, flag_ref, other_flag_ref, gate_ref, up_ref, down_ref,
    own_ref, pair_ref, near_ref, far_ref, hidden_ref,
):
    other = normalise(other_ref[...], gain_ref[...])
    kinds = gate_ref.shape[0]
    half = own_ref.shape[1]
    for r, rows, flags in ((0, normed_ref[...], flag_ref), (1, other, other_flag_ref)):
        flag = jnp.broadcast_to(flags[...].astype(f32), (TK, TK)).T[:, 0:1]
        for m in range(kinds):
            keep = flag if m == 0 else 1.0 - flag
            gate = dot_t(rows, gate_ref[m])
            up = dot_t(rows, up_ref[m])
            hidden_ref[r, m] = (jax.nn.silu(gate) * up * keep).astype(bf16)
    side = side_ref[0]
    for r in range(2):
        for s in range(2):
            at = (side if s == 0 else 1 - side) * half
            cols = pl.ds(pl.multiple_of(at, half), half)
            part = dot(hidden_ref[r, 0], down_ref[0, :, cols])
            part = part + dot(hidden_ref[r, 1], down_ref[1, :, cols])
            if r == 0 and s == 0:
                own_ref[...] = part
            else:
                target = ((None, pair_ref), (near_ref, far_ref))[r][s]
                target[...] = part.astype(bf16)


def swap4(x):
    return pltpu.roll(x, 4, 1)


def expert_kernel(
    got_ref, gate_hbm, up_hbm, down_hbm, out_hbm,
    gate_ref, up_ref, down_ref, rows_ref, hidden_ref, out_ref, in_sem, out_sem,
):
    width = 2 * got_ref.shape[2]
    half = width // 2
    hid = gate_ref.shape[0]
    cuts = [(c, min(256, hid - c)) for c in range(0, hid, 256)]
    copies = []
    for i, (c, n) in enumerate(cuts):
        copies.append(pltpu.make_async_copy(gate_hbm.at[pl.ds(c, n)], gate_ref.at[pl.ds(c, n)], in_sem.at[2 * i]))
        copies.append(pltpu.make_async_copy(up_hbm.at[pl.ds(c, n)], up_ref.at[pl.ds(c, n)], in_sem.at[2 * i + 1]))
    last = pltpu.make_async_copy(down_hbm, down_ref, in_sem.at[2 * len(cuts)])
    for copy in copies:
        copy.start()
    last.start()
    full = EX * MAIN
    rows_ref[0:full, 0:half] = got_ref[:, 0:MAIN, :].reshape(full, half)
    rows_ref[0:full, half:width] = got_ref[:, MAIN : 2 * MAIN, :].reshape(full, half)
    step = 256
    low = lax.broadcasted_iota(jnp.int32, (EX // 2, 8, step), 1) < REST
    for c in range(0, half, step):
        rest = got_ref[:, 2 * MAIN : BLK, c : c + step].astype(f32).reshape(EX // 2, 2, 8, step)
        even, odd = rest[:, 0], rest[:, 1]
        lo = jnp.where(low, even, swap4(odd))
        hi = jnp.where(low, swap4(even), odd)
        rows_ref[full:, c : c + step] = lo.reshape(EX * REST, step).astype(bf16)
        rows_ref[full:, half + c : half + c + step] = hi.reshape(EX * REST, step).astype(bf16)
    rows = rows_ref[...]
    for i, (c, n) in enumerate(cuts):
        copies[2 * i].wait()
        gate = dot_t(rows, gate_ref[c : c + n, :])
        copies[2 * i + 1].wait()
        up = dot_t(rows, up_ref[c : c + n, :])
        hidden_ref[:, c : c + n] = (jax.nn.silu(gate) * up).astype(bf16)
    last.wait()
    hidden = hidden_ref[...]
    quarter = half // 2
    low = lax.broadcasted_iota(jnp.int32, (EX // 2, 8, quarter), 1) < REST
    sends = []
    for t in range(2):
        rests = []
        for h in range(2):
            at = t * half + h * quarter
            part = dot(hidden, down_ref[:, at : at + quarter])
            out_ref[t, :, h * MAIN : (h + 1) * MAIN, :] = (
                part[0:full].astype(bf16).reshape(EX, MAIN, quarter)
            )
            rests.append(part[full:].reshape(EX // 2, 8, quarter))
        lo, hi = rests
        even = jnp.where(low, lo, swap4(hi))
        odd = jnp.where(low, swap4(lo), hi)
        joined = jnp.stack([even, odd], axis=1).reshape(EX, 8, quarter)
        out_ref[t, :, 2 * MAIN : BLK, :] = joined.astype(bf16)
        send = pltpu.make_async_copy(out_ref.at[t], out_hbm.at[:, t], out_sem.at[t])
        send.start()
        sends.append(send)
    for send in sends:
        send.wait()


def combine_kernel(back_ref, main_ref, rest_ref, own_ref, pair_ref, near_ref, far_ref, out_ref):
    quarter = back_ref.shape[3]
    base = own_ref[...] + pair_ref[...].astype(f32) + near_ref[...].astype(f32)
    base = base + far_ref[...].astype(f32)
    for h in range(2):
        total = None
        for t in range(2):
            rows = back_ref[:, t, h * MAIN : (h + 1) * MAIN, :].reshape(EX * MAIN, quarter)
            part = dot(main_ref[...], rows)
            rest = back_ref[:, t, 2 * MAIN : BLK, :].reshape(EX * 2 * REST, quarter)
            part = part + dot(rest_ref[h], rest)
            total = part if total is None else total + part
        routed = total[0:TK] + total[TK:]
        cols = slice(h * quarter, (h + 1) * quarter)
        out_ref[:, cols] = (base[:, cols] + routed).astype(bf16)


def call(body, out_shape, **kw):
    mib = kw.pop("mib", 32)
    return pl.pallas_call(
        body, out_shape=out_shape, compiler_params=pltpu.CompilerParams(vmem_limit_bytes=mib << 20), **kw
    )


vmem = pl.BlockSpec(memory_space=pltpu.VMEM)
smem = pl.BlockSpec(memory_space=pltpu.SMEM)
hbm = pl.BlockSpec(memory_space=pl.ANY)


def per_device(
    tokens, norm_gain, router, expert_ids, modality,
    expert_gate, expert_up, expert_down, shared_gate, shared_up, shared_down,
):
    sds = jax.ShapeDtypeStruct
    width = tokens.shape[1]
    half = width // 2
    side = lax.axis_index("tensor").astype(jnp.int32).reshape(1)
    gain = norm_gain.reshape(1, width)
    flags = modality.reshape(1, TK)
    swap = [(0, 1), (1, 0)]
    other_tokens = lax.ppermute(tokens, "dp", swap)
    other_flags = lax.ppermute(flags, "dp", swap)

    outgoing, normed, rank = call(
        place_kernel,
        (sds((EX, BLK, half), bf16), sds((TK, width), bf16), sds((EX, TK), f32)),
        name="place",
    )(tokens, gain, expert_ids.T)
    got = lax.all_to_all(outgoing, "expert", 0, 0, tiled=True)

    main, rest = call(
        weigh_kernel,
        (sds((2 * TK, EX * MAIN), bf16), sds((2, 2 * TK, EX * 2 * REST), bf16)),
        name="weigh",
    )(normed, router.T, rank)
    piece = sds((TK, half), bf16)
    own, pair, near, far = call(
        shared_kernel,
        (sds((TK, half), f32), piece, piece, piece),
        in_specs=[smem] + [vmem] * 8,
        scratch_shapes=[pltpu.VMEM((2, 2, TK, shared_gate.shape[2]), bf16)],
        name="shared",
    )(
        side, normed, other_tokens, gain, flags, other_flags,
        shared_gate.swapaxes(1, 2), shared_up.swapaxes(1, 2), shared_down,
    )
    four = ("dp", "tensor")
    pair = lax.ppermute(pair, four, [(i, i ^ 1) for i in range(4)])
    near = lax.ppermute(near, four, [(i, i ^ 2) for i in range(4)])
    far = lax.ppermute(far, four, [(i, i ^ 3) for i in range(4)])

    got, main, rest, own, pair, near, far = lax.optimization_barrier(
        (got, main, rest, own, pair, near, far)
    )

    hid = expert_gate.shape[2]
    rows = EX * (MAIN + REST)
    results = call(
        expert_kernel,
        sds((EX, 2, BLK, half // 2), bf16),
        in_specs=[vmem, hbm, hbm, hbm],
        out_specs=hbm,
        scratch_shapes=[
            pltpu.VMEM((hid, width), bf16),
            pltpu.VMEM((hid, width), bf16),
            pltpu.VMEM((hid, width), bf16),
            pltpu.VMEM((rows, width), bf16),
            pltpu.VMEM((rows, hid), bf16),
            pltpu.VMEM((2, EX, BLK, half // 2), bf16),
            pltpu.SemaphoreType.DMA((7,)),
            pltpu.SemaphoreType.DMA((2,)),
        ],
        mib=56,
        name="expert",
    )(got, expert_gate[0].T, expert_up[0].T, expert_down[0])
    back = lax.all_to_all(
        results.reshape(2 * EX, BLK, half // 2), ("expert", "tensor"), 0, 0, tiled=True
    ).reshape(EX, 2, BLK, half // 2)
    return call(combine_kernel, sds((TK, half), bf16), name="combine")(
        back, main, rest, own, pair, near, far
    )


def solution(mesh):
    in_specs = (
        P(("dp", "expert"), None),
        P(),
        P(),
        P(("dp", "expert"), None),
        P(("dp", "expert")),
        P("expert", None, "tensor"),
        P("expert", None, "tensor"),
        P("expert", "tensor", None),
        P(None, None, ("dp", "tensor")),
        P(None, None, ("dp", "tensor")),
        P(None, ("dp", "tensor"), None),
    )
    out_specs = P(("dp", "expert"), "tensor")
    return jax.shard_map(
        per_device, mesh=mesh, in_specs=in_specs, out_specs=out_specs, check_vma=False
    )
```

time: 197 us -> 114 us (0.58)
  waiting for transfers between devices: 77.5 us -> 22.4 us
  blocking collectives: 0 us -> 46.8 us
  local copies, waits for them, and re-layouts: 46.3 us -> 4.61 us
  matrix products: 26.3 us -> 0 us
  Pallas kernels: 0 us -> 24.1 us
  starting transfers between devices: 30.3 us -> 15.1 us
  other arithmetic: 14.5 us -> 0 us
    all_to_all x6 -> x1, waiting for transfers between devices: 77.5 us -> 0.01 us  [per_device(): got = lax.all_to_all(outgoing, 'expert', 0, 0, tiled=True)]
    all_to_all x0 -> x1, blocking collectives: none -> 46.8 us  [per_device(): lax.all_to_all(results.reshape(2 * EX, BLK, half // 2), ('expert', 'tenso...]
    dot_general x10 -> x0, matrix products: 26.3 us -> none  [the longest x1 5.18 us: per_device(): jnp.dot(flat_rows, expert_gate[0], preferred_element_type=jnp.float32)]
    pallas_call x0 -> x5, Pallas kernels: none -> 24.1 us  [the longest x1 15.6 us: per_device(): call(expert_kernel, sds((EX, 2, BLK, half // 2), bf16), in_specs=[vmem, h...]
    ppermute x0 -> x5, waiting for transfers between devices: none -> 22.4 us  [the longest x1 12.3 us: per_device(): other_flags = lax.ppermute(flags, 'dp', swap)]
    reshape x6 -> x0, local copies, waits for them, and re-layouts: 21.9 us -> none  [the longest x1 5.19 us: per_device(): flat_rows = received.reshape(-1, model_width)]
    all_to_all x6 -> x1, starting transfers between devices: 30.3 us -> 8.83 us  [per_device(): got = lax.all_to_all(outgoing, 'expert', 0, 0, tiled=True)]
    gather x7 -> x0, local copies, waits for them, and re-layouts: 12.3 us -> none  [the longest x2 8.21 us: per_device(): picked = returned.reshape(-1, returned.shape[2])[target]]
  transfers between devices with their start and end apart: 6 -> 6, of which waited for: 4 -> 3; matrix products, arithmetic and copies ran while one was open for 35% -> 0% of each run, Pallas kernels for 0% -> 4%
where the time goes in v1:
time: 114 us; the launch traced here: 113 us
  blocking collectives  46.8 us (41%)
  Pallas kernels  24.1 us (21%)
  waiting for transfers between devices  22.4 us (20%)
  starting transfers between devices  15.1 us (13%)
  local copies, waits for them, and re-layouts  4.61 us (4%)
    all_to_all x1, blocking collectives, per_device(): lax.all_to_all(results.reshape(2 * EX, BLK, half // 2), ('expert', 'tenso...  46.8 us
    pallas_call x1, Pallas kernels, per_device(): call(expert_kernel, sds((EX, 2, BLK, half // 2), bf16), in_specs=[vmem, h...  15.6 us
    ppermute x1, waiting for transfers between devices, per_device(): other_flags = lax.ppermute(flags, 'dp', swap)  12.3 us
    all_to_all x1, starting transfers between devices, per_device(): got = lax.all_to_all(outgoing, 'expert', 0, 0, tiled=True)  8.83 us
    ppermute x1, waiting for transfers between devices, per_device(): pair = lax.ppermute(pair, four, [(i, i ^ 1) for i in range(4)])  5.97 us
    unnamed x22, local copies, waits for them, and re-layouts  4.61 us
    ppermute x1, waiting for transfers between devices, per_device(): near = lax.ppermute(near, four, [(i, i ^ 2) for i in range(4)])  4.14 us
    pallas_call x1, Pallas kernels, per_device(): call(shared_kernel, (sds((TK, half), f32), piece, piece, piece), in_specs...  3.59 us
  transfers between devices with their start and end apart: 6, of which 3 were waited for; matrix products, arithmetic and copies ran while one was open for 0% of the time, Pallas kernels for 4%

profile of v1, /device:TPU:0, one launch (start us, length us, event | category | flops | bytes accessed | tf_op | source)
XLA Modules:
  0.0 113.2 jit_solution(2176296388010493075)
XLA Ops:
  0.0 1.0 copy-done.5
  1.0 0.7 copy-done.7
  1.7 0.7 copy-done.9
  2.4 2.7 %place.1 = (bf16[32,40,1024]{2,1,0:T(8,128)(2,1)}, bf16[128,2048]{1,0:T(8,128)(2,1)S(1)}, f32[32,128]{1,0:T(8,128)S(1)}) custom-call(bf16[128,2048]{1,0:T(8,128)(2,1)S(1)} %copy-done.5, f32[1,2048]{1,0:T(1,128)S(1)} %bitcast.20, s32[4,128]{1,0:T(4,128)S(1)} %bitcast.22), custom_call_target="tpu_custom_call" | custom-call | tf_op jit(solution)/shard_map/place/pallas_call | solution.py:228
  5.2 8.8 %all-to-all-start = ((bf16[32,40,1024]{2,1,0:T(8,128)(2,1)}), bf16[32,40,1024]{2,1,0:T(8,128)(2,1)}, u32[]{:S(2)}, u32[]{:S(2)}) async-start(bf16[32,40,1024]{2,1,0:T(8,128)(2,1)} %get-tuple-element.21), calls=%async_computation | async-start | bytes 5242880 | tf_op jit(solution)/shard_map/all_to_all | solution.py:233
  14.0 1.6 %collective-permute-start = (bf16[128,2048]{1,0:T(8,128)(2,1)}, bf16[128,2048]{1,0:T(8,128)(2,1)}, u32[]{:S(2)}, u32[]{:S(2)}) collective-permute-start(bf16[128,2048]{1,0:T(8,128)(2,1)} %tok_ref.1), channel_id=1, source_target_pairs={{0,64},{64,0},{1,65},{65,1},{2,66},{66,2},{3,67},{67,3},{4,68},{68... | collective-permute-start | bytes 1572872 | tf_op jit(solution)/shard_map/ppermute | solution.py:225
  15.6 0.5 collective-permute-start.1
  16.1 12.3 %collective-permute-done.1.other_flag_ref = s32[1,128]{1,0:T(1,128)S(1)} collective-permute-done((s32[1,128]{1,0:T(1,128)S(1)}, s32[1,128]{1,0:T(1,128)S(1)}, u32[]{:S(2)}, u32[]{:S(2)}) %collective-permute-start.1) | collective-permute-done | bytes 544 | tf_op jit(solution)/shard_map/ppermute | solution.py:226
  28.4 0.0 collective-permute-done.other_ref
  28.5 0.0 copy-start.2
  28.5 1.4 %copy-done.2 = bf16[2,176,2048]{2,1,0:T(8,128)(2,1)S(1)} copy-done((bf16[2,176,2048]{2,1,0:T(8,128)(2,1)S(1)}, bf16[2,176,2048]{2,1,0:T(8,128)(2,1)}, u32[]{:S(2)}) %copy-start.2) | copy-done | bytes 1441816
  29.8 3.6 %shared.1 = (f32[128,1024]{1,0:T(8,128)S(1)}, bf16[128,1024]{1,0:T(8,128)(2,1)S(1)}, bf16[128,1024]{1,0:T(8,128)(2,1)S(1)}, bf16[128,1024]{1,0:T(8,128)(2,1)S(1)}) custom-call(s32[1]{0:T(128)} %bitcast.3.side_ref, bf16[128,2048]{1,0:T(8,128)(2,1)S(1)} %get-tuple-element.22.normed_ref, bf16[128,2048]{1,0:T(8,128)(2,1)} %collective-permute-done.other_ref, ...), custom_call_target="tpu_custom_call" | custom-call | tf_op jit(solution)/shard_map/shared/pallas_call | solution.py:241
  33.4 0.8 copy-done.3
  34.2 3.0 %collective-permute-start.2 = (bf16[128,1024]{1,0:T(8,128)(2,1)S(1)}, bf16[128,1024]{1,0:T(8,128)(2,1)S(1)}, u32[]{:S(2)}, u32[]{:S(2)}) collective-permute-start(bf16[128,1024]{1,0:T(8,128)(2,1)S(1)} %get-tuple-element.27), channel_id=1, source_target_pairs={{0,1},{1,0},{64,65},{65,64},{2,3},{3,2},{66,67},{67,66},{4,5},{5,4... | collective-permute-start | bytes 786440 | tf_op jit(solution)/shard_map/ppermute | solution.py:252
  37.3 0.6 collective-permute-start.3
  37.8 0.6 collective-permute-start.4
  38.4 0.5 weigh.1
  38.9 6.0 %collective-permute-done.2.pair_ref = bf16[128,1024]{1,0:T(8,128)(2,1)S(1)} collective-permute-done((bf16[128,1024]{1,0:T(8,128)(2,1)S(1)}, bf16[128,1024]{1,0:T(8,128)(2,1)S(1)}, u32[]{:S(2)}, u32[]{:S(2)}) %collective-permute-start.2) | collective-permute-done | bytes 262176 | tf_op jit(solution)/shard_map/ppermute | solution.py:252
  44.9 4.1 %collective-permute-done.3.near_ref = bf16[128,1024]{1,0:T(8,128)(2,1)S(1)} collective-permute-done((bf16[128,1024]{1,0:T(8,128)(2,1)S(1)}, bf16[128,1024]{1,0:T(8,128)(2,1)S(1)}, u32[]{:S(2)}, u32[]{:S(2)}) %collective-permute-start.3) | collective-permute-done | bytes 262176 | tf_op jit(solution)/shard_map/ppermute | solution.py:253
  49.1 0.0 collective-permute-done.4.far_ref
  49.1 0.0 all-to-all-done.got_ref
  49.1 15.6 %expert.1 = bf16[32,2,40,512]{3,2,1,0:T(8,128)(2,1)} custom-call(bf16[32,40,1024]{2,1,0:T(8,128)(2,1)} %all-to-all-done.got_ref, bf16[704,2048]{1,0:T(8,128)(2,1)} %bitcast.26, bf16[704,2048]{1,0:T(8,128)(2,1)} %bitcast.27, bf16[704,2048]{1,0:T(8,128)(2,1)} %bitcast.28), custom_call_target="tpu_custom_call" | custom-call | tf_op jit(solution)/shard_map/expert/pallas_call | solution.py:262
  64.6 46.8 %all_to_all.10 = bf16[64,40,512]{2,1,0:T(8,128)(2,1)S(1)} all-to-all(bf16[64,40,512]{2,1,0:T(8,128)(2,1)} %bitcast.25), channel_id=1, replica_groups=mesh['dp'=2,'expert'=32,'tensor'=2] {'expert','tensor'}, dimensions={0} | all-to-all | bytes 5242880 | tf_op jit(solution)/shard_map/all_to_all | solution.py:280
  111.5 1.7 %combine.1 = bf16[128,1024]{1,0:T(8,128)(2,1)} custom-call(bf16[32,2,40,512]{3,2,1,0:T(8,128)(2,1)S(1)} %bitcast.16, bf16[256,512]{1,0:T(8,128)(2,1)S(1)} %get-tuple-element.31.main_ref, bf16[2,256,256]{2,1,0:T(8,128)(2,1)S(1)} %get-tuple-element.32.rest_ref, f32[128,1024]{1,0:T(8,128)S(1)} %copy-done.4, ...), custom_call_target="tpu_custom_call" | custom-call | tf_op jit(solution)/shard_map/combine/pallas_call | solution.py:283
  (16 shorter events, 0.0 us)
Async XLA Ops:
  0.0 1.0 copy-start.5
  1.0 0.7 copy-start.7
  1.7 0.7 copy-start.9
  5.1 10.4 %copy-start.10 = (s32[128]{0:T(128)S(1)}, s32[128]{0:T(128)}, u32[]{:S(2)}) copy-start(s32[128]{0:T(128)} %param.15) | copy-start | bytes 1540
  5.1 23.3 %copy-start = (bf16[2,2048,176]{1,2,0:T(8,128)(2,1)S(1)}, bf16[2,2048,176]{1,2,0:T(8,128)(2,1)}, u32[]{:S(2)}) copy-start(bf16[2,2048,176]{1,2,0:T(8,128)(2,1)} %param.19) | copy-start | bytes 4325380
  5.1 23.3 %copy-start.1 = (bf16[2,2048,176]{1,2,0:T(8,128)(2,1)S(1)}, bf16[2,2048,176]{1,2,0:T(8,128)(2,1)}, u32[]{:S(2)}) copy-start(bf16[2,2048,176]{1,2,0:T(8,128)(2,1)} %param.20) | copy-start | bytes 4325380
  5.1 23.3 %copy-start.8 = (f32[2048]{0:T(1024)S(1)}, f32[2048]{0:T(1024)}, u32[]{:S(2)}) copy-start(f32[2048]{0:T(1024)} %param.12) | copy-start | bytes 24580
  5.2 43.9 %all-to-all-start = ((bf16[32,40,1024]{2,1,0:T(8,128)(2,1)}), bf16[32,40,1024]{2,1,0:T(8,128)(2,1)}, u32[]{:S(2)}, u32[]{:S(2)}) async-start(bf16[32,40,1024]{2,1,0:T(8,128)(2,1)} %get-tuple-element.21), calls=%async_computation | async-start | bytes 5242880 | tf_op jit(solution)/shard_map/all_to_all | solution.py:233
  14.0 14.4 %collective-permute-start = (bf16[128,2048]{1,0:T(8,128)(2,1)}, bf16[128,2048]{1,0:T(8,128)(2,1)}, u32[]{:S(2)}, u32[]{:S(2)}) collective-permute-start(bf16[128,2048]{1,0:T(8,128)(2,1)} %tok_ref.1), channel_id=1, source_target_pairs={{0,64},{64,0},{1,65},{65,1},{2,66},{66,2},{3,67},{67,3},{4,68},{68... | collective-permute-start | bytes 1572872 | tf_op jit(solution)/shard_map/ppermute | solution.py:225
  15.6 12.9 %collective-permute-start.1 = (s32[1,128]{1,0:T(1,128)S(1)}, s32[1,128]{1,0:T(1,128)S(1)}, u32[]{:S(2)}, u32[]{:S(2)}) collective-permute-start(s32[1,128]{1,0:T(1,128)S(1)} %bitcast.23), channel_id=1, source_target_pairs={{0,64},{64,0},{1,65},{65,1},{2,66},{66,2},{3,67},{67,3},{4,68},{68... | collective-permute-start | bytes 1544 | tf_op jit(solution)/shard_map/ppermute | solution.py:226
  28.5 1.4 %copy-start.2 = (bf16[2,176,2048]{2,1,0:T(8,128)(2,1)S(1)}, bf16[2,176,2048]{2,1,0:T(8,128)(2,1)}, u32[]{:S(2)}) copy-start(bf16[2,176,2048]{2,1,0:T(8,128)(2,1)} %down_ref.1) | copy-start | bytes 4325380
  29.8 8.6 %copy-start.6 = (bf16[2048,32]{0,1:T(8,128)(2,1)S(1)}, bf16[2048,32]{0,1:T(8,128)(2,1)}, u32[]{:S(2)}) copy-start(bf16[2048,32]{0,1:T(8,128)(2,1)} %param.13) | copy-start | bytes 393220
  33.4 0.8 copy-start.3
  34.2 10.7 %collective-permute-start.2 = (bf16[128,1024]{1,0:T(8,128)(2,1)S(1)}, bf16[128,1024]{1,0:T(8,128)(2,1)S(1)}, u32[]{:S(2)}, u32[]{:S(2)}) collective-permute-start(bf16[128,1024]{1,0:T(8,128)(2,1)S(1)} %get-tuple-element.27), channel_id=1, source_target_pairs={{0,1},{1,0},{64,65},{65,64},{2,3},{3,2},{66,67},{67,66},{4,5},{5,4... | collective-permute-start | bytes 786440 | tf_op jit(solution)/shard_map/ppermute | solution.py:252
  37.3 11.8 %collective-permute-start.3 = (bf16[128,1024]{1,0:T(8,128)(2,1)S(1)}, bf16[128,1024]{1,0:T(8,128)(2,1)S(1)}, u32[]{:S(2)}, u32[]{:S(2)}) collective-permute-start(bf16[128,1024]{1,0:T(8,128)(2,1)S(1)} %get-tuple-element.28), channel_id=1, source_target_pairs={{0,64},{1,65},{64,0},{65,1},{2,66},{3,67},{66,2},{67,3},{4,68},{5,... | collective-permute-start | bytes 786440 | tf_op jit(solution)/shard_map/ppermute | solution.py:253
  37.8 11.2 %collective-permute-start.4 = (bf16[128,1024]{1,0:T(8,128)(2,1)S(1)}, bf16[128,1024]{1,0:T(8,128)(2,1)S(1)}, u32[]{:S(2)}, u32[]{:S(2)}) collective-permute-start(bf16[128,1024]{1,0:T(8,128)(2,1)S(1)} %get-tuple-element.29), channel_id=1, source_target_pairs={{0,65},{1,64},{64,1},{65,0},{2,67},{3,66},{66,3},{67,2},{4,69},{5,... | collective-permute-start | bytes 786440 | tf_op jit(solution)/shard_map/ppermute | solution.py:254
  64.6 46.8 %copy-start.4 = (f32[128,1024]{1,0:T(8,128)S(1)}, f32[128,1024]{1,0:T(8,128)}, u32[]{:S(2)}) copy-start(f32[128,1024]{1,0:T(8,128)} %copy-done.3) | copy-start | bytes 1572868

commit v2 on v1

--- a/solution.py
+++ b/solution.py
@@ -18,6 +18,9 @@
 BLK = 2 * (MAIN + REST)
 
 
+CUTS = (0, 256, 1 << 20)
+
+
 def normalise(values, gain):
     values = values.astype(f32)
     inv_scale = lax.rsqrt(jnp.mean(values * values, axis=-1, keepdims=True) + epsilon)
@@ -32,7 +35,16 @@
     return lax.dot_general(a, b, (((1,), (1,)), ((), ())), preferred_element_type=f32)
 
 
-def place_kernel(tok_ref, gain_ref, ids_ref, out_ref, normed_ref, rank_ref):
+def place_kernel(
+    tok_hbm, gain_hbm, ids_hbm, out_hbm, normed_ref, rank_ref,
+    tok_ref, gain_ref, ids_ref, out_ref, sem, out_sem,
+):
+    pairs = ((ids_hbm, ids_ref), (tok_hbm, tok_ref), (gain_hbm, gain_ref))
+    copies = [pltpu.make_async_copy(a, b, sem.at[i]) for i, (a, b) in enumerate(pairs)]
+    for copy in copies:
+        copy.start()
+    for copy in copies:
+        copy.wait()
     normed = normalise(tok_ref[...], gain_ref[...])
     normed_ref[...] = normed
     ids = ids_ref[...]
@@ -56,6 +68,7 @@
     rest_lo = jnp.where(row < REST, rest, 0.0).astype(bf16).reshape(EX * 2 * REST, TK)
     rest_hi = jnp.where(row >= REST, rest, 0.0).astype(bf16).reshape(EX * 2 * REST, TK)
     step = 256
+    sends = []
     for c in range(0, half, step):
         lo = normed[:, c : c + step]
         hi = normed[:, half + c : half + c + step]
@@ -65,6 +78,14 @@
         )
         both = dot(rest_lo, lo) + dot(rest_hi, hi)
         out_ref[:, 2 * MAIN : BLK, c : c + step] = both.reshape(EX, 2 * REST, step).astype(bf16)
+        cols = pl.ds(c, step)
+        send = pltpu.make_async_copy(
+            out_ref.at[:, :, cols], out_hbm.at[:, :, cols], out_sem.at[len(sends)]
+        )
+        send.start()
+        sends.append(send)
+    for send in sends:
+        send.wait()
 
 
 def weigh_kernel(normed_ref, router_ref, rank_ref, main_ref, rest_ref):
@@ -123,21 +144,28 @@
 
 def expert_kernel(
     got_ref, gate_hbm, up_hbm, down_hbm, out_hbm,
-    gate_ref, up_ref, down_ref, rows_ref, hidden_ref, out_ref, in_sem, out_sem,
+    gate_ref, up_ref, down_ref, rows_ref, hidden_ref, out_ref, in_sem, sem,
 ):
     width = 2 * got_ref.shape[2]
     half = width // 2
     hid = gate_ref.shape[0]
-    cuts = [(c, min(256, hid - c)) for c in range(0, hid, 256)]
-    copies = []
-    for i, (c, n) in enumerate(cuts):
-        copies.append(pltpu.make_async_copy(gate_hbm.at[pl.ds(c, n)], gate_ref.at[pl.ds(c, n)], in_sem.at[2 * i]))
-        copies.append(pltpu.make_async_copy(up_hbm.at[pl.ds(c, n)], up_ref.at[pl.ds(c, n)], in_sem.at[2 * i + 1]))
-    last = pltpu.make_async_copy(down_hbm, down_ref, in_sem.at[2 * len(cuts)])
-    for copy in copies:
-        copy.start()
-    last.start()
     full = EX * MAIN
+    quarter = half // 2
+    cuts = [(c, min(CUTS[i + 1], hid) - c) for i, c in enumerate(CUTS[:-1])]
+    loads = []
+    for c, n in cuts:
+        cut = pl.ds(c, n)
+        loads.append([(gate_hbm.at[cut], gate_ref.at[cut]), (up_hbm.at[cut], up_ref.at[cut])])
+    loads.append([(down_hbm, down_ref)])
+    count = 0
+    for i, group in enumerate(loads):
+        for j, (source, target) in enumerate(group):
+            group[j] = pltpu.make_async_copy(source, target, in_sem.at[count])
+            count += 1
+
+    for group in loads:
+        for copy in group:
+            copy.start()
     rows_ref[0:full, 0:half] = got_ref[:, 0:MAIN, :].reshape(full, half)
     rows_ref[0:full, half:width] = got_ref[:, MAIN : 2 * MAIN, :].reshape(full, half)
     step = 256
@@ -149,43 +177,59 @@
         hi = jnp.where(low, swap4(even), odd)
         rows_ref[full:, c : c + step] = lo.reshape(EX * REST, step).astype(bf16)
         rows_ref[full:, half + c : half + c + step] = hi.reshape(EX * REST, step).astype(bf16)
-    rows = rows_ref[...]
-    for i, (c, n) in enumerate(cuts):
-        copies[2 * i].wait()
-        gate = dot_t(rows, gate_ref[c : c + n, :])
-        copies[2 * i + 1].wait()
-        up = dot_t(rows, up_ref[c : c + n, :])
+    for (c, n), group in zip(cuts, loads):
+        for copy in group:
+            copy.wait()
+        gate = dot_t(rows_ref[...], gate_ref[c : c + n, :])
+        up = dot_t(rows_ref[...], up_ref[c : c + n, :])
         hidden_ref[:, c : c + n] = (jax.nn.silu(gate) * up).astype(bf16)
-    last.wait()
-    hidden = hidden_ref[...]
-    quarter = half // 2
+    loads[-1][0].wait()
     low = lax.broadcasted_iota(jnp.int32, (EX // 2, 8, quarter), 1) < REST
     sends = []
+
+    def send(t, first, count):
+        rows = pl.ds(first, count)
+        copy = pltpu.make_async_copy(
+            out_ref.at[:, t, rows, :], out_hbm.at[:, t, rows, :], sem.at[len(sends)]
+        )
+        copy.start()
+        sends.append(copy)
+
     for t in range(2):
         rests = []
         for h in range(2):
             at = t * half + h * quarter
-            part = dot(hidden, down_ref[:, at : at + quarter])
-            out_ref[t, :, h * MAIN : (h + 1) * MAIN, :] = (
+            part = dot(hidden_ref[...], down_ref[:, at : at + quarter])
+            out_ref[:, t, h * MAIN : (h + 1) * MAIN, :] = (
                 part[0:full].astype(bf16).reshape(EX, MAIN, quarter)
             )
+            if h == 0:
+                send(t, 0, MAIN)
             rests.append(part[full:].reshape(EX // 2, 8, quarter))
         lo, hi = rests
         even = jnp.where(low, lo, swap4(hi))
         odd = jnp.where(low, swap4(lo), hi)
         joined = jnp.stack([even, odd], axis=1).reshape(EX, 8, quarter)
-        out_ref[t, :, 2 * MAIN : BLK, :] = joined.astype(bf16)
-        send = pltpu.make_async_copy(out_ref.at[t], out_hbm.at[:, t], out_sem.at[t])
-        send.start()
-        sends.append(send)
-    for send in sends:
-        send.wait()
-
-
-def combine_kernel(back_ref, main_ref, rest_ref, own_ref, pair_ref, near_ref, far_ref, out_ref):
+        out_ref[:, t, 2 * MAIN : BLK, :] = joined.astype(bf16)
+        send(t, MAIN, BLK - MAIN)
+    for copy in sends:
+        copy.wait()
+
+
+def combine_kernel(
+    back_ref, main_hbm, rest_hbm, own_hbm, pair_hbm, near_hbm, far_hbm, out_ref,
+    main_ref, rest_ref, own_ref, pair_ref, near_ref, far_ref, sem,
+):
+    sources = (main_hbm, rest_hbm, own_hbm, pair_hbm, near_hbm, far_hbm)
+    targets = (main_ref, rest_ref, own_ref, pair_ref, near_ref, far_ref)
+    copies = []
+    for i, (source, target) in enumerate(zip(sources, targets)):
+        copies.append(pltpu.make_async_copy(source, target, sem.at[i]))
+        copies[i].start()
     quarter = back_ref.shape[3]
-    base = own_ref[...] + pair_ref[...].astype(f32) + near_ref[...].astype(f32)
-    base = base + far_ref[...].astype(f32)
+    copies[0].wait()
+    copies[1].wait()
+    routed = []
     for h in range(2):
         total = None
         for t in range(2):
@@ -194,13 +238,18 @@
             rest = back_ref[:, t, 2 * MAIN : BLK, :].reshape(EX * 2 * REST, quarter)
             part = part + dot(rest_ref[h], rest)
             total = part if total is None else total + part
-        routed = total[0:TK] + total[TK:]
+        routed.append(total[0:TK] + total[TK:])
+    for copy in copies[2:]:
+        copy.wait()
+    base = own_ref[...] + pair_ref[...].astype(f32) + near_ref[...].astype(f32)
+    base = base + far_ref[...].astype(f32)
+    for h in range(2):
         cols = slice(h * quarter, (h + 1) * quarter)
-        out_ref[:, cols] = (base[:, cols] + routed).astype(bf16)
+        out_ref[:, cols] = (base[:, cols] + routed[h]).astype(bf16)
 
 
 def call(body, out_shape, **kw):
-    mib = kw.pop("mib", 32)
+    mib = kw.pop("mib", 16)
     return pl.pallas_call(
         body, out_shape=out_shape, compiler_params=pltpu.CompilerParams(vmem_limit_bytes=mib << 20), **kw
     )
@@ -209,6 +258,10 @@
 vmem = pl.BlockSpec(memory_space=pltpu.VMEM)
 smem = pl.BlockSpec(memory_space=pltpu.SMEM)
 hbm = pl.BlockSpec(memory_space=pl.ANY)
+
+
+def in_hbm(x):
+    return pltpu.with_memory_space_constraint(x, pltpu.HBM)
 
 
 def per_device(
@@ -227,20 +280,34 @@
 
     outgoing, normed, rank = call(
         place_kernel,
-        (sds((EX, BLK, half), bf16), sds((TK, width), bf16), sds((EX, TK), f32)),
+        (pltpu.HBM((EX, BLK, half), bf16), sds((TK, width), bf16), sds((EX, TK), f32)),
+        in_specs=[hbm] * 3,
+        out_specs=[hbm, vmem, vmem],
+        scratch_shapes=[
+            pltpu.VMEM((TK, width), bf16),
+            pltpu.VMEM((1, width), f32),
+            pltpu.VMEM((expert_ids.shape[1], TK), jnp.int32),
+            pltpu.VMEM((EX, BLK, half), bf16),
+            pltpu.SemaphoreType.DMA((3,)),
+            pltpu.SemaphoreType.DMA((4,)),
+        ],
         name="place",
-    )(tokens, gain, expert_ids.T)
+    )(in_hbm(tokens), in_hbm(gain), in_hbm(expert_ids.T))
     got = lax.all_to_all(outgoing, "expert", 0, 0, tiled=True)
 
+    hid = expert_gate.shape[2]
     main, rest = call(
         weigh_kernel,
-        (sds((2 * TK, EX * MAIN), bf16), sds((2, 2 * TK, EX * 2 * REST), bf16)),
+        (
+            pltpu.HBM((2 * TK, EX * MAIN), bf16),
+            pltpu.HBM((2, 2 * TK, EX * 2 * REST), bf16),
+        ),
         name="weigh",
     )(normed, router.T, rank)
-    piece = sds((TK, half), bf16)
+    piece = pltpu.HBM((TK, half), bf16)
     own, pair, near, far = call(
         shared_kernel,
-        (sds((TK, half), f32), piece, piece, piece),
+        (pltpu.HBM((TK, half), f32), piece, piece, piece),
         in_specs=[smem] + [vmem] * 8,
         scratch_shapes=[pltpu.VMEM((2, 2, TK, shared_gate.shape[2]), bf16)],
         name="shared",
@@ -248,20 +315,19 @@
         side, normed, other_tokens, gain, flags, other_flags,
         shared_gate.swapaxes(1, 2), shared_up.swapaxes(1, 2), shared_down,
     )
+    got, main, rest, own, pair, near, far = lax.optimization_barrier(
+        (got, main, rest, own, pair, near, far)
+    )
     four = ("dp", "tensor")
     pair = lax.ppermute(pair, four, [(i, i ^ 1) for i in range(4)])
     near = lax.ppermute(near, four, [(i, i ^ 2) for i in range(4)])
     far = lax.ppermute(far, four, [(i, i ^ 3) for i in range(4)])
 
-    got, main, rest, own, pair, near, far = lax.optimization_barrier(
-        (got, main, rest, own, pair, near, far)
-    )
-
     hid = expert_gate.shape[2]
     rows = EX * (MAIN + REST)
     results = call(
         expert_kernel,
-        sds((EX, 2, BLK, half // 2), bf16),
+        pltpu.HBM((EX, 2, BLK, half // 2), bf16),
         in_specs=[vmem, hbm, hbm, hbm],
         out_specs=hbm,
         scratch_shapes=[
@@ -270,19 +336,25 @@
             pltpu.VMEM((hid, width), bf16),
             pltpu.VMEM((rows, width), bf16),
             pltpu.VMEM((rows, hid), bf16),
-            pltpu.VMEM((2, EX, BLK, half // 2), bf16),
-            pltpu.SemaphoreType.DMA((7,)),
-            pltpu.SemaphoreType.DMA((2,)),
+            pltpu.VMEM((EX, 2, BLK, half // 2), bf16),
+            pltpu.SemaphoreType.DMA((2 * len(CUTS) - 1,)),
+            pltpu.SemaphoreType.DMA((4,)),
         ],
-        mib=56,
+        mib=32,
         name="expert",
-    )(got, expert_gate[0].T, expert_up[0].T, expert_down[0])
+    )(got, in_hbm(expert_gate[0].T), in_hbm(expert_up[0].T), in_hbm(expert_down[0]))
     back = lax.all_to_all(
         results.reshape(2 * EX, BLK, half // 2), ("expert", "tensor"), 0, 0, tiled=True
     ).reshape(EX, 2, BLK, half // 2)
-    return call(combine_kernel, sds((TK, half), bf16), name="combine")(
-        back, main, rest, own, pair, near, far
-    )
+    fixed = (main, rest, own, pair, near, far)
+    return call(
+        combine_kernel,
+        sds((TK, half), bf16),
+        in_specs=[vmem] + [hbm] * 6,
+        scratch_shapes=[pltpu.VMEM(x.shape, x.dtype) for x in fixed]
+        + [pltpu.SemaphoreType.DMA((6,))],
+        name="combine",
+    )(back, *[in_hbm(x) for x in fixed])
 
 
 def solution(mesh):

time: 114 us -> 110 us (0.965)
  blocking collectives: 46.8 us -> 0 us
  waiting for transfers between devices: 22.4 us -> 61.9 us
  starting transfers between devices: 15.1 us -> 21.3 us
  Pallas kernels: 24.1 us -> 21.1 us
    all_to_all x1 -> x0, blocking collectives: 46.8 us -> none  [per_device(): lax.all_to_all(results.reshape(2 * EX, BLK, half // 2), ('expert', 'tenso...]
    ppermute x1, waiting for transfers between devices: 5.97 us -> 34 us  [per_device(): pair = lax.ppermute(pair, four, [(i, i ^ 1) for i in range(4)])]
    all_to_all x1, waiting for transfers between devices: 0.01 us -> 11.7 us  [per_device(): got = lax.all_to_all(outgoing, 'expert', 0, 0, tiled=True)]
    all_to_all x0 -> x1, starting transfers between devices: none -> 6.42 us  [per_device(): lax.all_to_all(results.reshape(2 * EX, BLK, half // 2), ('expert', 'tenso...]
    pallas_call x5, Pallas kernels: 24.1 us -> 21.1 us  [the longest x1 9.26 us: per_device(): call(expert_kernel, pltpu.HBM((EX, 2, BLK, half // 2), bf16), in_specs=[v...]
    ppermute x1, waiting for transfers between devices: 0.01 us -> 2.49 us  [per_device(): far = lax.ppermute(far, four, [(i, i ^ 3) for i in range(4)])]
    ppermute x1, waiting for transfers between devices: 4.14 us -> 2.5 us  [per_device(): near = lax.ppermute(near, four, [(i, i ^ 2) for i in range(4)])]
    ppermute x1, waiting for transfers between devices: 12.3 us -> 11.1 us  [per_device(): other_flags = lax.ppermute(flags, 'dp', swap)]
  transfers between devices with their start and end apart: 6 -> 7, of which waited for: 3 -> 5; matrix products, arithmetic and copies ran while one was open for 0% -> 0% of each run, Pallas kernels for 4% -> 5%
where the time goes in v2:
time: 110 us; the launch traced here: 109 us
  waiting for transfers between devices  61.9 us (56%)
  starting transfers between devices  21.3 us (19%)
  Pallas kernels  21.1 us (19%)
  local copies, waits for them, and re-layouts  4.82 us (4%)
    ppermute x1, waiting for transfers between devices, per_device(): pair = lax.ppermute(pair, four, [(i, i ^ 1) for i in range(4)])  34 us
    all_to_all x1, waiting for transfers between devices, per_device(): got = lax.all_to_all(outgoing, 'expert', 0, 0, tiled=True)  11.7 us
    ppermute x1, waiting for transfers between devices, per_device(): other_flags = lax.ppermute(flags, 'dp', swap)  11.1 us
    pallas_call x1, Pallas kernels, per_device(): call(expert_kernel, pltpu.HBM((EX, 2, BLK, half // 2), bf16), in_specs=[v...  9.26 us
    all_to_all x1, starting transfers between devices, per_device(): got = lax.all_to_all(outgoing, 'expert', 0, 0, tiled=True)  8.59 us
    all_to_all x1, starting transfers between devices, per_device(): lax.all_to_all(results.reshape(2 * EX, BLK, half // 2), ('expert', 'tenso...  6.42 us
    unnamed x18, local copies, waits for them, and re-layouts  4.82 us
    pallas_call x1, Pallas kernels, per_device(): call(shared_kernel, (pltpu.HBM((TK, half), f32), piece, piece, piece), in...  4.29 us
  transfers between devices with their start and end apart: 7, of which 5 were waited for; matrix products, arithmetic and copies ran while one was open for 0% of the time, Pallas kernels for 5%

profile of v2, /device:TPU:0, one launch (start us, length us, event | category | flops | bytes accessed | tf_op | source)
XLA Modules:
  0.0 109.1 jit_solution(18416090725066710855)
XLA Ops:
  0.0 3.4 %place.1 = (bf16[32,40,1024]{2,1,0:T(8,128)(2,1)}, bf16[128,2048]{1,0:T(8,128)(2,1)S(1)}, f32[32,128]{1,0:T(8,128)S(1)}) custom-call(bf16[128,2048]{1,0:T(8,128)(2,1)} %tok_hbm.1, f32[1,2048]{1,0:T(1,128)} %bitcast.20, s32[4,128]{1,0:T(4,128)} %bitcast.28), custom_call_target="tpu_custom_call" | custom-call | tf_op jit(solution)/shard_map/place/pallas_call | solution.py:281
  3.4 0.0 copy-start.5
  3.4 0.0 copy-start.3
  3.4 0.0 copy-start.4
  3.4 8.6 %all-to-all-start = ((bf16[32,40,1024]{2,1,0:T(8,128)(2,1)}), bf16[32,40,1024]{2,1,0:T(8,128)(2,1)S(1)}, u32[]{:S(2)}, u32[]{:S(2)}) async-start(bf16[32,40,1024]{2,1,0:T(8,128)(2,1)} %get-tuple-element.21), calls=%async_computation | async-start | bytes 5242880 | tf_op jit(solution)/shard_map/all_to_all | solution.py:296
  12.0 1.6 %collective-permute-start = (bf16[128,2048]{1,0:T(8,128)(2,1)}, bf16[128,2048]{1,0:T(8,128)(2,1)}, u32[]{:S(2)}, u32[]{:S(2)}) collective-permute-start(bf16[128,2048]{1,0:T(8,128)(2,1)} %tok_hbm.1), channel_id=1, source_target_pairs={{0,64},{64,0},{1,65},{65,1},{2,66},{66,2},{3,67},{67,3},{4,68},{68... | collective-permute-start | bytes 1572872 | tf_op jit(solution)/shard_map/ppermute | solution.py:278
  13.6 0.5 collective-permute-start.1
  14.1 1.3 %weigh.1 = (bf16[256,512]{1,0:T(8,128)(2,1)}, bf16[2,256,256]{2,1,0:T(8,128)(2,1)}) custom-call(bf16[128,2048]{1,0:T(8,128)(2,1)S(1)} %get-tuple-element.22.normed_ref, bf16[32,2048]{1,0:T(8,128)(2,1)S(1)} %bitcast.19, f32[32,128]{1,0:T(8,128)S(1)} %get-tuple-element.23.rank_ref), custom_call_target="tpu_custom_call" | custom-call | tf_op jit(solution)/shard_map/weigh/pallas_call | solution.py:299
  15.4 11.1 %collective-permute-done.1.other_flag_ref = s32[1,128]{1,0:T(1,128)S(1)} collective-permute-done((s32[1,128]{1,0:T(1,128)S(1)}, s32[1,128]{1,0:T(1,128)S(1)}, u32[]{:S(2)}, u32[]{:S(2)}) %collective-permute-start.1) | collective-permute-done | bytes 544 | tf_op jit(solution)/shard_map/ppermute | solution.py:279
  26.5 1.4 %copy-done = bf16[2,2048,176]{1,2,0:T(8,128)(2,1)S(1)} copy-done((bf16[2,2048,176]{1,2,0:T(8,128)(2,1)S(1)}, bf16[2,2048,176]{1,2,0:T(8,128)(2,1)}, u32[]{:S(2)}) %copy-start) | copy-done | bytes 1441816
  27.9 1.4 %copy-done.1 = bf16[2,2048,176]{1,2,0:T(8,128)(2,1)S(1)} copy-done((bf16[2,2048,176]{1,2,0:T(8,128)(2,1)S(1)}, bf16[2,2048,176]{1,2,0:T(8,128)(2,1)}, u32[]{:S(2)}) %copy-start.1) | copy-done | bytes 1441816
  29.3 1.4 %copy-done.2 = bf16[2,176,2048]{2,1,0:T(8,128)(2,1)S(1)} copy-done((bf16[2,176,2048]{2,1,0:T(8,128)(2,1)S(1)}, bf16[2,176,2048]{2,1,0:T(8,128)(2,1)}, u32[]{:S(2)}) %copy-start.2) | copy-done | bytes 1441816
  30.6 4.3 %shared.1 = (f32[128,1024]{1,0:T(8,128)}, bf16[128,1024]{1,0:T(8,128)(2,1)}, bf16[128,1024]{1,0:T(8,128)(2,1)}, bf16[128,1024]{1,0:T(8,128)(2,1)}) custom-call(s32[1]{0:T(128)} %bitcast.3.side_ref, bf16[128,2048]{1,0:T(8,128)(2,1)S(1)} %get-tuple-element.22.normed_ref, bf16[128,2048]{1,0:T(8,128)(2,1)} %collective-permute-done.other_ref, ...), custom_call_target="tpu_custom_call" | custom-call | tf_op jit(solution)/shard_map/shared/pallas_call | solution.py:308
  34.9 11.7 %all-to-all-done.got_ref = bf16[32,40,1024]{2,1,0:T(8,128)(2,1)S(1)} async-done(((bf16[32,40,1024]{2,1,0:T(8,128)(2,1)}), bf16[32,40,1024]{2,1,0:T(8,128)(2,1)S(1)}, u32[]{:S(2)}, u32[]{:S(2)}) %all-to-all-start) | async-done | bytes 2621472 | tf_op jit(solution)/shard_map/all_to_all | solution.py:296
  46.6 9.3 %expert.1 = bf16[32,2,40,512]{3,2,1,0:T(8,128)(2,1)} custom-call(bf16[32,40,1024]{2,1,0:T(8,128)(2,1)S(1)} %all-to-all-done.got_ref, bf16[704,2048]{1,0:T(8,128)(2,1)} %bitcast.25, bf16[704,2048]{1,0:T(8,128)(2,1)} %bitcast.26, bf16[704,2048]{1,0:T(8,128)(2,1)} %bitcast.27), custom_call_target="tpu_custom_call" | custom-call | tf_op jit(solution)/shard_map/expert/pallas_call | solution.py:328
  55.9 6.4 %all-to-all-start.1 = ((bf16[64,40,512]{2,1,0:T(8,128)(2,1)}), bf16[64,40,512]{2,1,0:T(8,128)(2,1)S(1)}, u32[]{:S(2)}, u32[]{:S(2)}) async-start(bf16[64,40,512]{2,1,0:T(8,128)(2,1)} %bitcast.24), calls=%async_computation.1 | async-start | bytes 5242880 | tf_op jit(solution)/shard_map/all_to_all | solution.py:346
  62.3 3.2 %collective-permute-start.2 = (bf16[128,1024]{1,0:T(8,128)(2,1)}, bf16[128,1024]{1,0:T(8,128)(2,1)S(1)}, u32[]{:S(2)}, u32[]{:S(2)}) collective-permute-start(bf16[128,1024]{1,0:T(8,128)(2,1)} %get-tuple-element.34), channel_id=1, source_target_pairs={{0,1},{1,0},{64,65},{65,64},{2,3},{3,2},{66,67},{67,66},{4,5},{5,4... | collective-permute-start | bytes 786440 | tf_op jit(solution)/shard_map/ppermute | solution.py:322
  65.4 0.6 collective-permute-start.3
  66.0 0.4 collective-permute-start.4
  66.5 34.0 %collective-permute-done.2.pair_hbm = bf16[128,1024]{1,0:T(8,128)(2,1)S(1)} collective-permute-done((bf16[128,1024]{1,0:T(8,128)(2,1)}, bf16[128,1024]{1,0:T(8,128)(2,1)S(1)}, u32[]{:S(2)}, u32[]{:S(2)}) %collective-permute-start.2) | collective-permute-done | bytes 262176 | tf_op jit(solution)/shard_map/ppermute | solution.py:322
  100.5 2.5 %collective-permute-done.3.near_hbm = bf16[128,1024]{1,0:T(8,128)(2,1)S(1)} collective-permute-done((bf16[128,1024]{1,0:T(8,128)(2,1)}, bf16[128,1024]{1,0:T(8,128)(2,1)S(1)}, u32[]{:S(2)}, u32[]{:S(2)}) %collective-permute-start.3) | collective-permute-done | bytes 262176 | tf_op jit(solution)/shard_map/ppermute | solution.py:323
  103.0 2.5 %collective-permute-done.4.far_hbm = bf16[128,1024]{1,0:T(8,128)(2,1)S(1)} collective-permute-done((bf16[128,1024]{1,0:T(8,128)(2,1)}, bf16[128,1024]{1,0:T(8,128)(2,1)S(1)}, u32[]{:S(2)}, u32[]{:S(2)}) %collective-permute-start.4) | collective-permute-done | bytes 262176 | tf_op jit(solution)/shard_map/ppermute | solution.py:324
  105.5 0.7 copy-done.8
  106.2 2.9 %combine.1 = bf16[128,1024]{1,0:T(8,128)(2,1)} custom-call(bf16[32,2,40,512]{3,2,1,0:T(8,128)(2,1)S(1)} %bitcast.16, bf16[256,512]{1,0:T(8,128)(2,1)} %get-tuple-element.31.main_hbm, bf16[2,256,256]{2,1,0:T(8,128)(2,1)} %get-tuple-element.32.rest_hbm, f32[128,1024]{1,0:T(8,128)} %get-tuple-element.33.own_hbm, bf16[128,1024]{1,0:T(8,128)(2,1)} %copy-done.6, ...), custom_call_target="tpu_custom_call" | custom-call | tf_op jit(solution)/shard_map/combine/pallas_call | solution.py:350
  (13 shorter events, 0.0 us)
Async XLA Ops:
  3.4 10.2 %copy-start.5 = (s32[128]{0:T(128)S(1)}, s32[128]{0:T(128)}, u32[]{:S(2)}) copy-start(s32[128]{0:T(128)} %param.15) | copy-start | bytes 1540
  3.4 10.7 %copy-start.3 = (bf16[2048,32]{0,1:T(8,128)(2,1)S(1)}, bf16[2048,32]{0,1:T(8,128)(2,1)}, u32[]{:S(2)}) copy-start(bf16[2048,32]{0,1:T(8,128)(2,1)} %param.13) | copy-start | bytes 393220
  3.4 23.1 %copy-start.4 = (f32[2048]{0:T(1024)S(1)}, f32[2048]{0:T(1024)}, u32[]{:S(2)}) copy-start(f32[2048]{0:T(1024)} %param.12) | copy-start | bytes 24580
  3.4 43.2 %all-to-all-start = ((bf16[32,40,1024]{2,1,0:T(8,128)(2,1)}), bf16[32,40,1024]{2,1,0:T(8,128)(2,1)S(1)}, u32[]{:S(2)}, u32[]{:S(2)}) async-start(bf16[32,40,1024]{2,1,0:T(8,128)(2,1)} %get-tuple-element.21), calls=%async_computation | async-start | bytes 5242880 | tf_op jit(solution)/shard_map/all_to_all | solution.py:296
  12.0 14.5 %collective-permute-start = (bf16[128,2048]{1,0:T(8,128)(2,1)}, bf16[128,2048]{1,0:T(8,128)(2,1)}, u32[]{:S(2)}, u32[]{:S(2)}) collective-permute-start(bf16[128,2048]{1,0:T(8,128)(2,1)} %tok_hbm.1), channel_id=1, source_target_pairs={{0,64},{64,0},{1,65},{65,1},{2,66},{66,2},{3,67},{67,3},{4,68},{68... | collective-permute-start | bytes 1572872 | tf_op jit(solution)/shard_map/ppermute | solution.py:278
  13.6 12.9 %collective-permute-start.1 = (s32[1,128]{1,0:T(1,128)S(1)}, s32[1,128]{1,0:T(1,128)S(1)}, u32[]{:S(2)}, u32[]{:S(2)}) collective-permute-start(s32[1,128]{1,0:T(1,128)S(1)} %bitcast.22), channel_id=1, source_target_pairs={{0,64},{64,0},{1,65},{65,1},{2,66},{66,2},{3,67},{67,3},{4,68},{68... | collective-permute-start | bytes 1544 | tf_op jit(solution)/shard_map/ppermute | solution.py:279
  26.5 1.4 %copy-start = (bf16[2,2048,176]{1,2,0:T(8,128)(2,1)S(1)}, bf16[2,2048,176]{1,2,0:T(8,128)(2,1)}, u32[]{:S(2)}) copy-start(bf16[2,2048,176]{1,2,0:T(8,128)(2,1)} %param.19) | copy-start | bytes 4325380
  27.9 1.4 %copy-start.1 = (bf16[2,2048,176]{1,2,0:T(8,128)(2,1)S(1)}, bf16[2,2048,176]{1,2,0:T(8,128)(2,1)}, u32[]{:S(2)}) copy-start(bf16[2,2048,176]{1,2,0:T(8,128)(2,1)} %param.20) | copy-start | bytes 4325380
  29.3 1.4 %copy-start.2 = (bf16[2,176,2048]{2,1,0:T(8,128)(2,1)S(1)}, bf16[2,176,2048]{2,1,0:T(8,128)(2,1)}, u32[]{:S(2)}) copy-start(bf16[2,176,2048]{2,1,0:T(8,128)(2,1)} %down_ref.1) | copy-start | bytes 4325380
  55.9 49.6 %all-to-all-start.1 = ((bf16[64,40,512]{2,1,0:T(8,128)(2,1)}), bf16[64,40,512]{2,1,0:T(8,128)(2,1)S(1)}, u32[]{:S(2)}, u32[]{:S(2)}) async-start(bf16[64,40,512]{2,1,0:T(8,128)(2,1)} %bitcast.24), calls=%async_computation.1 | async-start | bytes 5242880 | tf_op jit(solution)/shard_map/all_to_all | solution.py:346
  62.3 38.2 %collective-permute-start.2 = (bf16[128,1024]{1,0:T(8,128)(2,1)}, bf16[128,1024]{1,0:T(8,128)(2,1)S(1)}, u32[]{:S(2)}, u32[]{:S(2)}) collective-permute-start(bf16[128,1024]{1,0:T(8,128)(2,1)} %get-tuple-element.34), channel_id=1, source_target_pairs={{0,1},{1,0},{64,65},{65,64},{2,3},{3,2},{66,67},{67,66},{4,5},{5,4... | collective-permute-start | bytes 786440 | tf_op jit(solution)/shard_map/ppermute | solution.py:322
  65.4 37.6 %collective-permute-start.3 = (bf16[128,1024]{1,0:T(8,128)(2,1)}, bf16[128,1024]{1,0:T(8,128)(2,1)S(1)}, u32[]{:S(2)}, u32[]{:S(2)}) collective-permute-start(bf16[128,1024]{1,0:T(8,128)(2,1)} %get-tuple-element.35), channel_id=1, source_target_pairs={{0,64},{1,65},{64,0},{65,1},{2,66},{3,67},{66,2},{67,3},{4,68},{5,... | collective-permute-start | bytes 786440 | tf_op jit(solution)/shard_map/ppermute | solution.py:323
  66.0 39.5 %collective-permute-start.4 = (bf16[128,1024]{1,0:T(8,128)(2,1)}, bf16[128,1024]{1,0:T(8,128)(2,1)S(1)}, u32[]{:S(2)}, u32[]{:S(2)}) collective-permute-start(bf16[128,1024]{1,0:T(8,128)(2,1)} %get-tuple-element.36), channel_id=1, source_target_pairs={{0,65},{1,64},{64,1},{65,0},{2,67},{3,66},{66,3},{67,2},{4,69},{5,... | collective-permute-start | bytes 786440 | tf_op jit(solution)/shard_map/ppermute | solution.py:324
  100.5 5.0 %copy-start.6 = (bf16[128,1024]{1,0:T(8,128)(2,1)}, bf16[128,1024]{1,0:T(8,128)(2,1)S(1)}, u32[]{:S(2)}) copy-start(bf16[128,1024]{1,0:T(8,128)(2,1)S(1)} %collective-permute-done.2.pair_hbm) | copy-start | bytes 786436
  103.0 2.5 %copy-start.7 = (bf16[128,1024]{1,0:T(8,128)(2,1)}, bf16[128,1024]{1,0:T(8,128)(2,1)S(1)}, u32[]{:S(2)}) copy-start(bf16[128,1024]{1,0:T(8,128)(2,1)S(1)} %collective-permute-done.3.near_hbm) | copy-start | bytes 786436
  105.5 0.7 copy-start.8

commit v3 on v2

--- a/solution.py
+++ b/solution.py
@@ -35,19 +35,7 @@
     return lax.dot_general(a, b, (((1,), (1,)), ((), ())), preferred_element_type=f32)
 
 
-def place_kernel(
-    tok_hbm, gain_hbm, ids_hbm, out_hbm, normed_ref, rank_ref,
-    tok_ref, gain_ref, ids_ref, out_ref, sem, out_sem,
-):
-    pairs = ((ids_hbm, ids_ref), (tok_hbm, tok_ref), (gain_hbm, gain_ref))
-    copies = [pltpu.make_async_copy(a, b, sem.at[i]) for i, (a, b) in enumerate(pairs)]
-    for copy in copies:
-        copy.start()
-    for copy in copies:
-        copy.wait()
-    normed = normalise(tok_ref[...], gain_ref[...])
-    normed_ref[...] = normed
-    ids = ids_ref[...]
+def slot_ranks(ids):
     expert = lax.broadcasted_iota(jnp.int32, (EX, TK), 0)
     named = ids[0:1] == expert
     for k in range(1, ids.shape[0]):
@@ -57,8 +45,20 @@
         jnp.int32, (TK, TK), 1
     )
     rank = dot(ones.astype(bf16), jnp.where(before, 1.0, 0.0).astype(bf16))
-    rank = jnp.where(named, rank, -1.0)
-    rank_ref[...] = rank
+    return jnp.where(named, rank, -1.0)
+
+
+def place_kernel(
+    tok_hbm, gain_hbm, ids_hbm, out_hbm, tok_ref, gain_ref, ids_ref, out_ref, sem, out_sem
+):
+    pairs = ((ids_hbm, ids_ref), (gain_hbm, gain_ref), (tok_hbm, tok_ref))
+    copies = [pltpu.make_async_copy(a, b, sem.at[i]) for i, (a, b) in enumerate(pairs)]
+    for copy in copies:
+        copy.start()
+    for copy in copies:
+        copy.wait()
+    rank = slot_ranks(ids_ref[...])
+    normed = normalise(tok_ref[...], gain_ref[...])
     half = normed.shape[1] // 2
     slot = lax.broadcasted_iota(jnp.int32, (EX, MAIN, TK), 1).astype(f32)
     main = jnp.where(rank[:, None, :] == slot, 1.0, 0.0).astype(bf16).reshape(EX * MAIN, TK)
@@ -88,9 +88,17 @@
         send.wait()
 
 
-def weigh_kernel(normed_ref, router_ref, rank_ref, main_ref, rest_ref):
-    rank = rank_ref[...]
-    logits = dot_t(router_ref[...], normed_ref[...])
+def weigh_kernel(
+    side_ref, tok_ref, gain_ref, ids_ref, router_ref, flag_ref, gate_hbm, up_hbm, down_hbm,
+    main_ref, rest_ref, own_ref, pair_ref, gate_ref, up_ref, down_ref, hidden_ref, sem,
+):
+    pairs = ((gate_hbm, gate_ref), (up_hbm, up_ref), (down_hbm, down_ref))
+    copies = [pltpu.make_async_copy(a, b, sem.at[i]) for i, (a, b) in enumerate(pairs)]
+    for copy in copies:
+        copy.start()
+    rank = slot_ranks(ids_ref[...])
+    normed = normalise(tok_ref[...], gain_ref[...])
+    logits = dot_t(router_ref[...], normed)
     scores = jnp.where(rank >= 0.0, jax.nn.sigmoid(logits), 0.0)
     weights = scores / jnp.sum(scores, axis=0, keepdims=True)
     slot = lax.broadcasted_iota(jnp.int32, (EX, MAIN, TK), 1).astype(f32)
@@ -108,34 +116,40 @@
         coarse = part.astype(bf16)
         rest_ref[h, 0:TK, :] = coarse
         rest_ref[h, TK:, :] = (part - coarse.astype(f32)).astype(bf16)
+    for copy in copies:
+        copy.wait()
+    shared_terms(
+        side_ref, normed, flag_ref, gate_ref, up_ref, down_ref, hidden_ref,
+        own_ref, pair_ref,
+    )
+
+
+def shared_terms(
+    side_ref, rows, flag_ref, gate_ref, up_ref, down_ref, hidden_ref, same_ref, cross_ref
+):
+    flag = jnp.broadcast_to(flag_ref[...].astype(f32), (TK, TK)).T[:, 0:1]
+    for m in range(gate_ref.shape[0]):
+        keep = flag if m == 0 else 1.0 - flag
+        gate = dot_t(rows, gate_ref[m])
+        up = dot_t(rows, up_ref[m])
+        hidden_ref[m] = (jax.nn.silu(gate) * up * keep).astype(bf16)
+    side = side_ref[0]
+    half = same_ref.shape[1]
+    for target, at in ((cross_ref, 1 - side), (same_ref, side)):
+        cols = pl.ds(pl.multiple_of(at * half, half), half)
+        part = dot(hidden_ref[0], down_ref[0, :, cols])
+        part = part + dot(hidden_ref[1], down_ref[1, :, cols])
+        target[...] = part.astype(target.dtype)
 
 
 def shared_kernel(
-    side_ref, normed_ref, other_ref, gain_ref, flag_ref, other_flag_ref, gate_ref, up_ref, down_ref,
-    own_ref, pair_ref, near_ref, far_ref, hidden_ref,
-):
-    other = normalise(other_ref[...], gain_ref[...])
-    kinds = gate_ref.shape[0]
-    half = own_ref.shape[1]
-    for r, rows, flags in ((0, normed_ref[...], flag_ref), (1, other, other_flag_ref)):
-        flag = jnp.broadcast_to(flags[...].astype(f32), (TK, TK)).T[:, 0:1]
-        for m in range(kinds):
-            keep = flag if m == 0 else 1.0 - flag
-            gate = dot_t(rows, gate_ref[m])
-            up = dot_t(rows, up_ref[m])
-            hidden_ref[r, m] = (jax.nn.silu(gate) * up * keep).astype(bf16)
-    side = side_ref[0]
-    for r in range(2):
-        for s in range(2):
-            at = (side if s == 0 else 1 - side) * half
-            cols = pl.ds(pl.multiple_of(at, half), half)
-            part = dot(hidden_ref[r, 0], down_ref[0, :, cols])
-            part = part + dot(hidden_ref[r, 1], down_ref[1, :, cols])
-            if r == 0 and s == 0:
-                own_ref[...] = part
-            else:
-                target = ((None, pair_ref), (near_ref, far_ref))[r][s]
-                target[...] = part.astype(bf16)
+    side_ref, other_ref, gain_ref, flag_ref, gate_ref, up_ref, down_ref,
+    near_ref, far_ref, hidden_ref,
+):
+    rows = normalise(other_ref[...], gain_ref[...])
+    shared_terms(
+        side_ref, rows, flag_ref, gate_ref, up_ref, down_ref, hidden_ref, near_ref, far_ref
+    )
 
 
 def swap4(x):
@@ -216,19 +230,10 @@
         copy.wait()
 
 
-def combine_kernel(
-    back_ref, main_hbm, rest_hbm, own_hbm, pair_hbm, near_hbm, far_hbm, out_ref,
-    main_ref, rest_ref, own_ref, pair_ref, near_ref, far_ref, sem,
-):
-    sources = (main_hbm, rest_hbm, own_hbm, pair_hbm, near_hbm, far_hbm)
-    targets = (main_ref, rest_ref, own_ref, pair_ref, near_ref, far_ref)
-    copies = []
-    for i, (source, target) in enumerate(zip(sources, targets)):
-        copies.append(pltpu.make_async_copy(source, target, sem.at[i]))
-        copies[i].start()
+def combine_kernel(back_ref, main_ref, rest_ref, base_hbm, out_ref, base_ref, sem):
+    copy = pltpu.make_async_copy(base_hbm, base_ref, sem)
+    copy.start()
     quarter = back_ref.shape[3]
-    copies[0].wait()
-    copies[1].wait()
     routed = []
     for h in range(2):
         total = None
@@ -239,13 +244,10 @@
             part = part + dot(rest_ref[h], rest)
             total = part if total is None else total + part
         routed.append(total[0:TK] + total[TK:])
-    for copy in copies[2:]:
-        copy.wait()
-    base = own_ref[...] + pair_ref[...].astype(f32) + near_ref[...].astype(f32)
-    base = base + far_ref[...].astype(f32)
+    copy.wait()
     for h in range(2):
         cols = slice(h * quarter, (h + 1) * quarter)
-        out_ref[:, cols] = (base[:, cols] + routed[h]).astype(bf16)
+        out_ref[:, cols] = (base_ref[:, cols] + routed[h]).astype(bf16)
 
 
 def call(body, out_shape, **kw):
@@ -262,6 +264,10 @@
 
 def in_hbm(x):
     return pltpu.with_memory_space_constraint(x, pltpu.HBM)
+
+
+def in_vmem(x):
+    return pltpu.with_memory_space_constraint(x, pltpu.VMEM)
 
 
 def per_device(
@@ -278,11 +284,11 @@
     other_tokens = lax.ppermute(tokens, "dp", swap)
     other_flags = lax.ppermute(flags, "dp", swap)
 
-    outgoing, normed, rank = call(
+    outgoing = call(
         place_kernel,
-        (pltpu.HBM((EX, BLK, half), bf16), sds((TK, width), bf16), sds((EX, TK), f32)),
+        pltpu.HBM((EX, BLK, half), bf16),
         in_specs=[hbm] * 3,
-        out_specs=[hbm, vmem, vmem],
+        out_specs=hbm,
         scratch_shapes=[
             pltpu.VMEM((TK, width), bf16),
             pltpu.VMEM((1, width), f32),
@@ -296,32 +302,42 @@
     got = lax.all_to_all(outgoing, "expert", 0, 0, tiled=True)
 
     hid = expert_gate.shape[2]
-    main, rest = call(
+    piece = pltpu.HBM((TK, half), bf16)
+    hidden = pltpu.VMEM((2, TK, shared_gate.shape[2]), bf16)
+    part = pltpu.VMEM(shared_down.shape, bf16)
+    main, rest, own, pair, *weights = call(
         weigh_kernel,
         (
-            pltpu.HBM((2 * TK, EX * MAIN), bf16),
-            pltpu.HBM((2, 2 * TK, EX * 2 * REST), bf16),
+            sds((2 * TK, EX * MAIN), bf16),
+            sds((2, 2 * TK, EX * 2 * REST), bf16),
+            pltpu.HBM((TK, half), f32),
+            piece,
+            part,
+            part,
+            part,
         ),
+        in_specs=[smem] + [vmem] * 5 + [hbm] * 3,
+        scratch_shapes=[hidden, pltpu.SemaphoreType.DMA((3,))],
         name="weigh",
-    )(normed, router.T, rank)
-    piece = pltpu.HBM((TK, half), bf16)
-    own, pair, near, far = call(
+    )(
+        side, tokens, gain, expert_ids.T, router.T, flags,
+        in_hbm(shared_gate.swapaxes(1, 2)), in_hbm(shared_up.swapaxes(1, 2)), in_hbm(shared_down),
+    )
+    four = ("dp", "tensor")
+    pair = lax.ppermute(pair, four, [(i, i ^ 1) for i in range(4)])
+    near, far = call(
         shared_kernel,
-        (pltpu.HBM((TK, half), f32), piece, piece, piece),
-        in_specs=[smem] + [vmem] * 8,
-        scratch_shapes=[pltpu.VMEM((2, 2, TK, shared_gate.shape[2]), bf16)],
+        (piece, piece),
+        in_specs=[smem] + [vmem] * 6,
+        scratch_shapes=[hidden],
         name="shared",
-    )(
-        side, normed, other_tokens, gain, flags, other_flags,
-        shared_gate.swapaxes(1, 2), shared_up.swapaxes(1, 2), shared_down,
-    )
+    )(side, other_tokens, gain, other_flags, *[in_vmem(x) for x in weights])
+    near = lax.ppermute(near, four, [(i, i ^ 2) for i in range(4)])
+    far = lax.ppermute(far, four, [(i, i ^ 3) for i in range(4)])
     got, main, rest, own, pair, near, far = lax.optimization_barrier(
         (got, main, rest, own, pair, near, far)
     )
-    four = ("dp", "tensor")
-    pair = lax.ppermute(pair, four, [(i, i ^ 1) for i in range(4)])
-    near = lax.ppermute(near, four, [(i, i ^ 2) for i in range(4)])
-    far = lax.ppermute(far, four, [(i, i ^ 3) for i in range(4)])
+    base = own + pair.astype(f32) + near.astype(f32) + far.astype(f32)
 
     hid = expert_gate.shape[2]
     rows = EX * (MAIN + REST)
@@ -346,15 +362,13 @@
     back = lax.all_to_all(
         results.reshape(2 * EX, BLK, half // 2), ("expert", "tensor"), 0, 0, tiled=True
     ).reshape(EX, 2, BLK, half // 2)
-    fixed = (main, rest, own, pair, near, far)
     return call(
         combine_kernel,
         sds((TK, half), bf16),
-        in_specs=[vmem] + [hbm] * 6,
-        scratch_shapes=[pltpu.VMEM(x.shape, x.dtype) for x in fixed]
-        + [pltpu.SemaphoreType.DMA((6,))],
+        in_specs=[vmem] * 3 + [hbm],
+        scratch_shapes=[pltpu.VMEM((TK, half), f32), pltpu.SemaphoreType.DMA],
         name="combine",
-    )(back, *[in_hbm(x) for x in fixed])
+    )(back, main, rest, in_hbm(base))
 
 
 def solution(mesh):

time: 110 us -> 102 us (0.927)
  waiting for transfers between devices: 61.9 us -> 51.2 us
  local copies, waits for them, and re-layouts: 4.82 us -> 0.74 us
  starting transfers between devices: 21.3 us -> 23.8 us
  other arithmetic: 0 us -> 2.13 us
  Pallas kernels: 21.1 us -> 23.2 us
    all_to_all x1, waiting for transfers between devices: 0.01 us -> 34.1 us  [per_device(): lax.all_to_all(results.reshape(2 * EX, BLK, half // 2), ('expert', 'tenso...]
    ppermute x1, waiting for transfers between devices: 34 us -> 0.05 us  [per_device(): pair = lax.ppermute(pair, four, [(i, i ^ 1) for i in range(4)])]
    ppermute x1, waiting for transfers between devices: 11.1 us -> 4.52 us  [per_device(): other_flags = lax.ppermute(flags, 'dp', swap)]
    all_to_all x1, waiting for transfers between devices: 11.7 us -> 6.63 us  [per_device(): got = lax.all_to_all(outgoing, 'expert', 0, 0, tiled=True)]
    unnamed x18 -> x22, local copies, waits for them, and re-layouts: 4.82 us -> 0.74 us
    add x0 -> x1, other arithmetic: none -> 2.13 us  [per_device(): base = own + pair.astype(f32) + near.astype(f32) + far.astype(f32)]
    pallas_call x4, Pallas kernels: 11.8 us -> 13.9 us  [the longest x1 4.62 us: per_device(): call(weigh_kernel, (sds((2 * TK, EX * MAIN), bf16), sds((2, 2 * TK, EX *...]
    ppermute x1, starting transfers between devices: 0.42 us -> 2.1 us  [per_device(): far = lax.ppermute(far, four, [(i, i ^ 3) for i in range(4)])]
  transfers between devices with their start and end apart: 7 -> 7, of which waited for: 5 -> 6; matrix products, arithmetic and copies ran while one was open for 0% -> 2% of each run, Pallas kernels for 5% -> 8%
where the time goes in v3:
time: 102 us; the launch traced here: 101 us
  waiting for transfers between devices  51.2 us (50%)
  starting transfers between devices  23.8 us (23%)
  Pallas kernels  23.2 us (23%)
  other arithmetic  2.13 us (2%)
    all_to_all x1, waiting for transfers between devices, per_device(): lax.all_to_all(results.reshape(2 * EX, BLK, half // 2), ('expert', 'tenso...  34.1 us
    pallas_call x1, Pallas kernels, per_device(): call(expert_kernel, pltpu.HBM((EX, 2, BLK, half // 2), bf16), in_specs=[v...  9.28 us
    all_to_all x1, starting transfers between devices, per_device(): got = lax.all_to_all(outgoing, 'expert', 0, 0, tiled=True)  8.59 us
    all_to_all x1, waiting for transfers between devices, per_device(): got = lax.all_to_all(outgoing, 'expert', 0, 0, tiled=True)  6.63 us
    all_to_all x1, starting transfers between devices, per_device(): lax.all_to_all(results.reshape(2 * EX, BLK, half // 2), ('expert', 'tenso...  6.54 us
    pallas_call x1, Pallas kernels, per_device(): call(weigh_kernel, (sds((2 * TK, EX * MAIN), bf16), sds((2, 2 * TK, EX *...  4.62 us
    ppermute x1, waiting for transfers between devices, per_device(): other_flags = lax.ppermute(flags, 'dp', swap)  4.52 us
    ppermute x1, waiting for transfers between devices, per_device(): near = lax.ppermute(near, four, [(i, i ^ 2) for i in range(4)])  3.5 us
  transfers between devices with their start and end apart: 7, of which 6 were waited for; matrix products, arithmetic and copies ran while one was open for 2% of the time, Pallas kernels for 8%

profile of v3, /device:TPU:0, one launch (start us, length us, event | category | flops | bytes accessed | tf_op | source)
XLA Modules:
  0.0 101.3 jit_solution(10500225457118810048)
XLA Ops:
  0.0 3.4 %place.1 = bf16[32,40,1024]{2,1,0:T(8,128)(2,1)} custom-call(bf16[128,2048]{1,0:T(8,128)(2,1)} %tok_ref.1, f32[1,2048]{1,0:T(1,128)} %bitcast.18, s32[4,128]{1,0:T(4,128)} %bitcast.21), custom_call_target="tpu_custom_call" | custom-call | tf_op jit(solution)/shard_map/place/pallas_call | solution.py:287
  3.4 0.0 copy-start
  3.4 0.0 copy-start.6
  3.4 0.0 copy-start.3
  3.4 0.0 copy-start.4
  3.4 8.6 %all-to-all-start = ((bf16[32,40,1024]{2,1,0:T(8,128)(2,1)}), bf16[32,40,1024]{2,1,0:T(8,128)(2,1)S(1)}, u32[]{:S(2)}, u32[]{:S(2)}) async-start(bf16[32,40,1024]{2,1,0:T(8,128)(2,1)} %place.1), calls=%async_computation | async-start | bytes 5242880 | tf_op jit(solution)/shard_map/all_to_all | solution.py:302
  12.0 1.6 %collective-permute-start.1 = (bf16[128,2048]{1,0:T(8,128)(2,1)S(1)}, bf16[128,2048]{1,0:T(8,128)(2,1)}, u32[]{:S(2)}, u32[]{:S(2)}) collective-permute-start(bf16[128,2048]{1,0:T(8,128)(2,1)S(1)} %copy-done), channel_id=1, source_target_pairs={{0,64},{64,0},{1,65},{65,1},{2,66},{66,2},{3,67},{67,3},{4,68},{68... | collective-permute-start | bytes 1572872 | tf_op jit(solution)/shard_map/ppermute | solution.py:284
  13.6 0.5 collective-permute-start.2
  14.2 4.6 %weigh.1 = (bf16[256,512]{1,0:T(8,128)(2,1)S(1)}, bf16[2,256,256]{2,1,0:T(8,128)(2,1)S(1)}, f32[128,1024]{1,0:T(8,128)}, bf16[128,1024]{1,0:T(8,128)(2,1)}, bf16...) custom-call(s32[1]{0:T(128)} %bitcast.2.side_ref, ...), custom_call_target="tpu_custom_call" | custom-call | tf_op jit(solution)/shard_map/weigh/pallas_call | solution.py:308
  18.8 0.7 copy-done.1
  19.5 3.0 %collective-permute-start = (bf16[128,1024]{1,0:T(8,128)(2,1)}, bf16[128,1024]{1,0:T(8,128)(2,1)S(1)}, u32[]{:S(2)}, u32[]{:S(2)}) collective-permute-start(bf16[128,1024]{1,0:T(8,128)(2,1)} %get-tuple-element.24), channel_id=1, source_target_pairs={{0,1},{1,0},{64,65},{65,64},{2,3},{3,2},{66,67},{67,66},{4,5},{5,4... | collective-permute-start | bytes 786440 | tf_op jit(solution)/shard_map/ppermute | solution.py:327
  22.5 4.5 %collective-permute-done.2.flag_ref = s32[1,128]{1,0:T(1,128)} collective-permute-done((s32[1,128]{1,0:T(1,128)S(1)}, s32[1,128]{1,0:T(1,128)}, u32[]{:S(2)}, u32[]{:S(2)}) %collective-permute-start.2) | collective-permute-done | bytes 544 | tf_op jit(solution)/shard_map/ppermute | solution.py:285
  27.0 3.4 %shared.1 = (bf16[128,1024]{1,0:T(8,128)(2,1)}, bf16[128,1024]{1,0:T(8,128)(2,1)}) custom-call(s32[1]{0:T(128)} %bitcast.2.side_ref, bf16[128,2048]{1,0:T(8,128)(2,1)} %collective-permute-done.1.other_ref, f32[1,2048]{1,0:T(1,128)S(1)} %bitcast.20, s32[1,128]{1,0:T(1,128)} %collective-permute-done.2.flag_ref, ...), custom_call_target="tpu_custom_call" | custom-call | tf_op jit(solution)/shard_map/shared/pallas_call | solution.py:328
  30.4 1.5 %collective-permute-start.3 = (bf16[128,1024]{1,0:T(8,128)(2,1)}, bf16[128,1024]{1,0:T(8,128)(2,1)S(1)}, u32[]{:S(2)}, u32[]{:S(2)}) collective-permute-start(bf16[128,1024]{1,0:T(8,128)(2,1)} %get-tuple-element.28), channel_id=1, source_target_pairs={{0,64},{1,65},{64,0},{65,1},{2,66},{3,67},{66,2},{67,3},{4,68},{5,... | collective-permute-start | bytes 786440 | tf_op jit(solution)/shard_map/ppermute | solution.py:335
  31.9 2.1 %collective-permute-start.4 = (bf16[128,1024]{1,0:T(8,128)(2,1)}, bf16[128,1024]{1,0:T(8,128)(2,1)S(1)}, u32[]{:S(2)}, u32[]{:S(2)}) collective-permute-start(bf16[128,1024]{1,0:T(8,128)(2,1)} %get-tuple-element.29), channel_id=1, source_target_pairs={{0,65},{1,64},{64,1},{65,0},{2,67},{3,66},{66,3},{67,2},{4,69},{5,... | collective-permute-start | bytes 786440 | tf_op jit(solution)/shard_map/ppermute | solution.py:336
  34.0 0.1 collective-permute-done
  34.0 3.5 %collective-permute-done.3 = bf16[128,1024]{1,0:T(8,128)(2,1)S(1)} collective-permute-done((bf16[128,1024]{1,0:T(8,128)(2,1)}, bf16[128,1024]{1,0:T(8,128)(2,1)S(1)}, u32[]{:S(2)}, u32[]{:S(2)}) %collective-permute-start.3) | collective-permute-done | bytes 262176 | tf_op jit(solution)/shard_map/ppermute | solution.py:335
  37.6 2.4 %collective-permute-done.4 = bf16[128,1024]{1,0:T(8,128)(2,1)S(1)} collective-permute-done((bf16[128,1024]{1,0:T(8,128)(2,1)}, bf16[128,1024]{1,0:T(8,128)(2,1)S(1)}, u32[]{:S(2)}, u32[]{:S(2)}) %collective-permute-start.4) | collective-permute-done | bytes 262176 | tf_op jit(solution)/shard_map/ppermute | solution.py:336
  40.0 6.6 %all-to-all-done.got_ref = bf16[32,40,1024]{2,1,0:T(8,128)(2,1)S(1)} async-done(((bf16[32,40,1024]{2,1,0:T(8,128)(2,1)}), bf16[32,40,1024]{2,1,0:T(8,128)(2,1)S(1)}, u32[]{:S(2)}, u32[]{:S(2)}) %all-to-all-start) | async-done | bytes 2621472 | tf_op jit(solution)/shard_map/all_to_all | solution.py:302
  46.6 9.3 %expert.1 = bf16[32,2,40,512]{3,2,1,0:T(8,128)(2,1)} custom-call(bf16[32,40,1024]{2,1,0:T(8,128)(2,1)S(1)} %all-to-all-done.got_ref, bf16[704,2048]{1,0:T(8,128)(2,1)} %bitcast.26, bf16[704,2048]{1,0:T(8,128)(2,1)} %bitcast.27, bf16[704,2048]{1,0:T(8,128)(2,1)} %bitcast.28), custom_call_target="tpu_custom_call" | custom-call | tf_op jit(solution)/shard_map/expert/pallas_call | solution.py:344
  55.9 6.5 %all-to-all-start.1 = ((bf16[64,40,512]{2,1,0:T(8,128)(2,1)}), bf16[64,40,512]{2,1,0:T(8,128)(2,1)S(1)}, u32[]{:S(2)}, u32[]{:S(2)}) async-start(bf16[64,40,512]{2,1,0:T(8,128)(2,1)} %bitcast.25), calls=%async_computation.1 | async-start | bytes 5242880 | tf_op jit(solution)/shard_map/all_to_all | solution.py:362
  62.5 2.1 %convert_add_fusion.base_hbm = f32[128,1024]{1,0:T(8,128)} fusion(bf16[128,1024]{1,0:T(8,128)(2,1)} %copy-done.10, bf16[128,1024]{1,0:T(8,128)(2,1)} %copy-done.9, f32[128,1024]{1,0:T(8,128)} %get-tuple-element.33, bf16[128,1024]{1,0:T(8,128)(2,1)S(1)} %copy-done.8), kind=kLoop, calls=%fused_computation | loop fusion | flops 786432 | bytes 1835008 | tf_op jit(solution)/shard_map/add | solution.py:340
  64.6 34.1 %all-to-all-done.1 = bf16[64,40,512]{2,1,0:T(8,128)(2,1)S(1)} async-done(((bf16[64,40,512]{2,1,0:T(8,128)(2,1)}), bf16[64,40,512]{2,1,0:T(8,128)(2,1)S(1)}, u32[]{:S(2)}, u32[]{:S(2)}) %all-to-all-start.1) | async-done | bytes 2621472 | tf_op jit(solution)/shard_map/all_to_all | solution.py:362
  98.7 2.6 %combine.1 = bf16[128,1024]{1,0:T(8,128)(2,1)} custom-call(bf16[32,2,40,512]{3,2,1,0:T(8,128)(2,1)S(1)} %bitcast.16, bf16[256,512]{1,0:T(8,128)(2,1)S(1)} %get-tuple-element.31.main_ref, bf16[2,256,256]{2,1,0:T(8,128)(2,1)S(1)} %copy-done.2, f32[128,1024]{1,0:T(8,128)} %convert_add_fusion.base_hbm), custom_call_target="tpu_custom_call" | custom-call | tf_op jit(solution)/shard_map/combine/pallas_call | solution.py:365
  (18 shorter events, 0.0 us)
Async XLA Ops:
  3.4 8.7 %copy-start = (bf16[128,2048]{1,0:T(8,128)(2,1)S(1)}, bf16[128,2048]{1,0:T(8,128)(2,1)}, u32[]{:S(2)}) copy-start(bf16[128,2048]{1,0:T(8,128)(2,1)} %tok_ref.1) | copy-start | bytes 1572868
  3.4 10.2 %copy-start.6 = (s32[128]{0:T(128)S(1)}, s32[128]{0:T(128)}, u32[]{:S(2)}) copy-start(s32[128]{0:T(128)} %param.15) | copy-start | bytes 1540
  3.4 10.8 %copy-start.3 = (bf16[2048,32]{0,1:T(8,128)(2,1)S(1)}, bf16[2048,32]{0,1:T(8,128)(2,1)}, u32[]{:S(2)}) copy-start(bf16[2048,32]{0,1:T(8,128)(2,1)} %param.13) | copy-start | bytes 393220
  3.4 10.7 %copy-start.4 = (f32[2048]{0:T(1024)S(1)}, f32[2048]{0:T(1024)}, u32[]{:S(2)}) copy-start(f32[2048]{0:T(1024)} %param.12) | copy-start | bytes 24580
  3.4 10.7 %copy-start.5 = (s32[128,4]{0,1:T(4,128)S(1)}, s32[128,4]{0,1:T(4,128)}, u32[]{:S(2)}) copy-start(s32[128,4]{0,1:T(4,128)} %param.14) | copy-start | bytes 6148
  3.4 43.2 %all-to-all-start = ((bf16[32,40,1024]{2,1,0:T(8,128)(2,1)}), bf16[32,40,1024]{2,1,0:T(8,128)(2,1)S(1)}, u32[]{:S(2)}, u32[]{:S(2)}) async-start(bf16[32,40,1024]{2,1,0:T(8,128)(2,1)} %place.1), calls=%async_computation | async-start | bytes 5242880 | tf_op jit(solution)/shard_map/all_to_all | solution.py:302
  12.0 15.0 %collective-permute-start.1 = (bf16[128,2048]{1,0:T(8,128)(2,1)S(1)}, bf16[128,2048]{1,0:T(8,128)(2,1)}, u32[]{:S(2)}, u32[]{:S(2)}) collective-permute-start(bf16[128,2048]{1,0:T(8,128)(2,1)S(1)} %copy-done), channel_id=1, source_target_pairs={{0,64},{64,0},{1,65},{65,1},{2,66},{66,2},{3,67},{67,3},{4,68},{68... | collective-permute-start | bytes 1572872 | tf_op jit(solution)/shard_map/ppermute | solution.py:284
  13.6 13.4 %collective-permute-start.2 = (s32[1,128]{1,0:T(1,128)S(1)}, s32[1,128]{1,0:T(1,128)}, u32[]{:S(2)}, u32[]{:S(2)}) collective-permute-start(s32[1,128]{1,0:T(1,128)S(1)} %bitcast.23), channel_id=1, source_target_pairs={{0,64},{64,0},{1,65},{65,1},{2,66},{66,2},{3,67},{67,3},{4,68},{68... | collective-permute-start | bytes 1544 | tf_op jit(solution)/shard_map/ppermute | solution.py:285
  18.8 0.7 copy-start.1
  19.5 14.6 %collective-permute-start = (bf16[128,1024]{1,0:T(8,128)(2,1)}, bf16[128,1024]{1,0:T(8,128)(2,1)S(1)}, u32[]{:S(2)}, u32[]{:S(2)}) collective-permute-start(bf16[128,1024]{1,0:T(8,128)(2,1)} %get-tuple-element.24), channel_id=1, source_target_pairs={{0,1},{1,0},{64,65},{65,64},{2,3},{3,2},{66,67},{67,66},{4,5},{5,4... | collective-permute-start | bytes 786440 | tf_op jit(solution)/shard_map/ppermute | solution.py:327
  30.4 7.1 %collective-permute-start.3 = (bf16[128,1024]{1,0:T(8,128)(2,1)}, bf16[128,1024]{1,0:T(8,128)(2,1)S(1)}, u32[]{:S(2)}, u32[]{:S(2)}) collective-permute-start(bf16[128,1024]{1,0:T(8,128)(2,1)} %get-tuple-element.28), channel_id=1, source_target_pairs={{0,64},{1,65},{64,0},{65,1},{2,66},{3,67},{66,2},{67,3},{4,68},{5,... | collective-permute-start | bytes 786440 | tf_op jit(solution)/shard_map/ppermute | solution.py:335
  31.9 8.1 %collective-permute-start.4 = (bf16[128,1024]{1,0:T(8,128)(2,1)}, bf16[128,1024]{1,0:T(8,128)(2,1)S(1)}, u32[]{:S(2)}, u32[]{:S(2)}) collective-permute-start(bf16[128,1024]{1,0:T(8,128)(2,1)} %get-tuple-element.29), channel_id=1, source_target_pairs={{0,65},{1,64},{64,1},{65,0},{2,67},{3,66},{66,3},{67,2},{4,69},{5,... | collective-permute-start | bytes 786440 | tf_op jit(solution)/shard_map/ppermute | solution.py:336
  34.0 3.5 %copy-start.7 = (bf16[128,1024]{1,0:T(8,128)(2,1)}, bf16[128,1024]{1,0:T(8,128)(2,1)S(1)}, u32[]{:S(2)}) copy-start(bf16[128,1024]{1,0:T(8,128)(2,1)S(1)} %collective-permute-done) | copy-start | bytes 786436
  37.5 18.3 %copy-start.9 = (bf16[128,1024]{1,0:T(8,128)(2,1)}, bf16[128,1024]{1,0:T(8,128)(2,1)S(1)}, u32[]{:S(2)}) copy-start(bf16[128,1024]{1,0:T(8,128)(2,1)S(1)} %collective-permute-done.3) | copy-start | bytes 786436
  40.0 15.9 %copy-start.10 = (bf16[128,1024]{1,0:T(8,128)(2,1)}, bf16[128,1024]{1,0:T(8,128)(2,1)S(1)}, u32[]{:S(2)}) copy-start(bf16[128,1024]{1,0:T(8,128)(2,1)S(1)} %collective-permute-done.4) | copy-start | bytes 786436
  55.9 6.6 %copy-start.8 = (bf16[128,1024]{1,0:T(8,128)(2,1)S(1)}, bf16[128,1024]{1,0:T(8,128)(2,1)}, u32[]{:S(2)}) copy-start(bf16[128,1024]{1,0:T(8,128)(2,1)} %copy-done.7) | copy-start | bytes 786436
  55.9 42.8 %copy-start.2 = (bf16[2,256,256]{2,1,0:T(8,128)(2,1)S(1)}, bf16[2,256,256]{2,1,0:T(8,128)(2,1)}, u32[]{:S(2)}) copy-start(bf16[2,256,256]{2,1,0:T(8,128)(2,1)} %copy-done.1) | copy-start | bytes 786436
  55.9 42.8 %all-to-all-start.1 = ((bf16[64,40,512]{2,1,0:T(8,128)(2,1)}), bf16[64,40,512]{2,1,0:T(8,128)(2,1)S(1)}, u32[]{:S(2)}, u32[]{:S(2)}) async-start(bf16[64,40,512]{2,1,0:T(8,128)(2,1)} %bitcast.25), calls=%async_computation.1 | async-start | bytes 5242880 | tf_op jit(solution)/shard_map/all_to_all | solution.py:362

commit v4 on v3

--- a/solution.py
+++ b/solution.py
@@ -55,11 +55,9 @@
     copies = [pltpu.make_async_copy(a, b, sem.at[i]) for i, (a, b) in enumerate(pairs)]
     for copy in copies:
         copy.start()
-    for copy in copies:
-        copy.wait()
+    copies[0].wait()
     rank = slot_ranks(ids_ref[...])
-    normed = normalise(tok_ref[...], gain_ref[...])
-    half = normed.shape[1] // 2
+    half = tok_ref.shape[1] // 2
     slot = lax.broadcasted_iota(jnp.int32, (EX, MAIN, TK), 1).astype(f32)
     main = jnp.where(rank[:, None, :] == slot, 1.0, 0.0).astype(bf16).reshape(EX * MAIN, TK)
     row = lax.broadcasted_iota(jnp.int32, (EX, 2 * REST, TK), 1)
@@ -67,6 +65,10 @@
     rest = jnp.where(rank[:, None, :] == wanted, 1.0, 0.0)
     rest_lo = jnp.where(row < REST, rest, 0.0).astype(bf16).reshape(EX * 2 * REST, TK)
     rest_hi = jnp.where(row >= REST, rest, 0.0).astype(bf16).reshape(EX * 2 * REST, TK)
+    rest = jnp.concatenate([rest_lo, rest_hi], axis=1)
+    for copy in copies[1:]:
+        copy.wait()
+    normed = normalise(tok_ref[...], gain_ref[...])
     step = 256
     sends = []
     for c in range(0, half, step):
@@ -76,7 +78,7 @@
         out_ref[:, MAIN : 2 * MAIN, c : c + step] = (
             dot(main, hi).astype(bf16).reshape(EX, MAIN, step)
         )
-        both = dot(rest_lo, lo) + dot(rest_hi, hi)
+        both = dot(rest, jnp.concatenate([lo, hi], axis=0))
         out_ref[:, 2 * MAIN : BLK, c : c + step] = both.reshape(EX, 2 * REST, step).astype(bf16)
         cols = pl.ds(c, step)
         send = pltpu.make_async_copy(
@@ -110,12 +112,10 @@
     row = lax.broadcasted_iota(jnp.int32, (EX, 2 * REST, TK), 1)
     wanted = (row % REST + MAIN).astype(f32)
     rest = jnp.where(rank[:, None, :] == wanted, weights[:, None, :], 0.0)
-    for h in range(2):
-        part = jnp.where((row < REST) == (h == 0), rest, 0.0)
-        part = part.reshape(EX * 2 * REST, TK).T
-        coarse = part.astype(bf16)
-        rest_ref[h, 0:TK, :] = coarse
-        rest_ref[h, TK:, :] = (part - coarse.astype(f32)).astype(bf16)
+    rest = rest.reshape(EX * 2 * REST, TK).T
+    coarse = rest.astype(bf16)
+    rest_ref[0:TK, :] = coarse
+    rest_ref[TK:, :] = (rest - coarse.astype(f32)).astype(bf16)
     for copy in copies:
         copy.wait()
     shared_terms(
@@ -230,24 +230,21 @@
         copy.wait()
 
 
-def combine_kernel(back_ref, main_ref, rest_ref, base_hbm, out_ref, base_ref, sem):
-    copy = pltpu.make_async_copy(base_hbm, base_ref, sem)
-    copy.start()
+def combine_kernel(back_ref, main_ref, rest_ref, base_ref, out_ref):
     quarter = back_ref.shape[3]
-    routed = []
+    lane = lax.broadcasted_iota(jnp.int32, rest_ref.shape, 1)
     for h in range(2):
+        mine = (lane % (2 * REST) < REST) == (h == 0)
+        few = jnp.where(mine, rest_ref[...].astype(f32), 0.0).astype(bf16)
         total = None
         for t in range(2):
             rows = back_ref[:, t, h * MAIN : (h + 1) * MAIN, :].reshape(EX * MAIN, quarter)
             part = dot(main_ref[...], rows)
             rest = back_ref[:, t, 2 * MAIN : BLK, :].reshape(EX * 2 * REST, quarter)
-            part = part + dot(rest_ref[h], rest)
+            part = part + dot(few, rest)
             total = part if total is None else total + part
-        routed.append(total[0:TK] + total[TK:])
-    copy.wait()
-    for h in range(2):
         cols = slice(h * quarter, (h + 1) * quarter)
-        out_ref[:, cols] = (base_ref[:, cols] + routed[h]).astype(bf16)
+        out_ref[:, cols] = (base_ref[:, cols] + total[0:TK] + total[TK:]).astype(bf16)
 
 
 def call(body, out_shape, **kw):
@@ -309,7 +306,7 @@
         weigh_kernel,
         (
             sds((2 * TK, EX * MAIN), bf16),
-            sds((2, 2 * TK, EX * 2 * REST), bf16),
+            sds((2 * TK, EX * 2 * REST), bf16),
             pltpu.HBM((TK, half), f32),
             piece,
             part,
@@ -362,13 +359,7 @@
     back = lax.all_to_all(
         results.reshape(2 * EX, BLK, half // 2), ("expert", "tensor"), 0, 0, tiled=True
     ).reshape(EX, 2, BLK, half // 2)
-    return call(
-        combine_kernel,
-        sds((TK, half), bf16),
-        in_specs=[vmem] * 3 + [hbm],
-        scratch_shapes=[pltpu.VMEM((TK, half), f32), pltpu.SemaphoreType.DMA],
-        name="combine",
-    )(back, main, rest, in_hbm(base))
+    return call(combine_kernel, sds((TK, half), bf16), name="combine")(back, main, rest, base)
 
 
 def solution(mesh):

time: 102 us -> 101 us (level)
  waiting for transfers between devices: 51.2 us -> 52.6 us
  Pallas kernels: 23.2 us -> 22.1 us
  transfers between devices with their start and end apart: 7 -> 7, of which waited for: 6 -> 6; matrix products, arithmetic and copies ran while one was open for 2% -> 1% of each run, Pallas kernels for 8% -> 8%
where the time goes in v4:
time: 101 us; the launch traced here: 100 us
  waiting for transfers between devices  52.6 us (52%)
  starting transfers between devices  23.9 us (24%)
  Pallas kernels  22.1 us (22%)
  other arithmetic  1.4 us (1%)
    all_to_all x1, waiting for transfers between devices, per_device(): lax.all_to_all(results.reshape(2 * EX, BLK, half // 2), ('expert', 'tenso...  34.8 us
    pallas_call x1, Pallas kernels, per_device(): call(expert_kernel, pltpu.HBM((EX, 2, BLK, half // 2), bf16), in_specs=[v...  9.24 us
    all_to_all x1, starting transfers between devices, per_device(): got = lax.all_to_all(outgoing, 'expert', 0, 0, tiled=True)  8.59 us
    all_to_all x1, waiting for transfers between devices, per_device(): got = lax.all_to_all(outgoing, 'expert', 0, 0, tiled=True)  6.62 us
    all_to_all x1, starting transfers between devices, per_device(): lax.all_to_all(results.reshape(2 * EX, BLK, half // 2), ('expert', 'tenso...  6.56 us
    ppermute x1, waiting for transfers between devices, per_device(): other_flags = lax.ppermute(flags, 'dp', swap)  5.12 us
    pallas_call x1, Pallas kernels, per_device(): call(weigh_kernel, (sds((2 * TK, EX * MAIN), bf16), sds((2 * TK, EX * 2 *...  4.62 us
    ppermute x1, waiting for transfers between devices, per_device(): near = lax.ppermute(near, four, [(i, i ^ 2) for i in range(4)])  3.4 us
  transfers between devices with their start and end apart: 7, of which 6 were waited for; matrix products, arithmetic and copies ran while one was open for 1% of the time, Pallas kernels for 8%

profile of v4, /device:TPU:0, one launch (start us, length us, event | category | flops | bytes accessed | tf_op | source)
XLA Modules:
  0.0 100.2 jit_solution(9862941874957029514)
XLA Ops:
  0.0 3.2 %place.1 = bf16[32,40,1024]{2,1,0:T(8,128)(2,1)} custom-call(bf16[128,2048]{1,0:T(8,128)(2,1)} %tok_ref.1, f32[1,2048]{1,0:T(1,128)} %bitcast.18, s32[4,128]{1,0:T(4,128)} %bitcast.21), custom_call_target="tpu_custom_call" | custom-call | tf_op jit(solution)/shard_map/place/pallas_call | solution.py:284
  3.2 0.0 copy-start
  3.2 0.0 copy-start.6
  3.2 0.0 copy-start.1
  3.3 0.0 copy-start.4
  3.3 0.0 copy-start.5
  3.3 8.6 %all-to-all-start = ((bf16[32,40,1024]{2,1,0:T(8,128)(2,1)}), bf16[32,40,1024]{2,1,0:T(8,128)(2,1)S(1)}, u32[]{:S(2)}, u32[]{:S(2)}) async-start(bf16[32,40,1024]{2,1,0:T(8,128)(2,1)} %place.1), calls=%async_computation | async-start | bytes 5242880 | tf_op jit(solution)/shard_map/all_to_all | solution.py:299
  11.9 1.6 %collective-permute-start.1 = (bf16[128,2048]{1,0:T(8,128)(2,1)S(1)}, bf16[128,2048]{1,0:T(8,128)(2,1)}, u32[]{:S(2)}, u32[]{:S(2)}) collective-permute-start(bf16[128,2048]{1,0:T(8,128)(2,1)S(1)} %copy-done), channel_id=1, source_target_pairs={{0,64},{64,0},{1,65},{65,1},{2,66},{66,2},{3,67},{67,3},{4,68},{68... | collective-permute-start | bytes 1572872 | tf_op jit(solution)/shard_map/ppermute | solution.py:281
  13.5 0.5 collective-permute-start.2
  14.0 4.6 %weigh.1 = (bf16[256,512]{1,0:T(8,128)(2,1)S(1)}, bf16[256,256]{1,0:T(8,128)(2,1)S(1)}, f32[128,1024]{1,0:T(8,128)}, bf16[128,1024]{1,0:T(8,128)(2,1)}, bf16[2,1...) custom-call(s32[1]{0:T(128)} %bitcast.2.side_ref, ...), custom_call_target="tpu_custom_call" | custom-call | tf_op jit(solution)/shard_map/weigh/pallas_call | solution.py:305
  18.6 3.1 %collective-permute-start = (bf16[128,1024]{1,0:T(8,128)(2,1)}, bf16[128,1024]{1,0:T(8,128)(2,1)}, u32[]{:S(2)}, u32[]{:S(2)}) collective-permute-start(bf16[128,1024]{1,0:T(8,128)(2,1)} %get-tuple-element.24), channel_id=1, source_target_pairs={{0,1},{1,0},{64,65},{65,64},{2,3},{3,2},{66,67},{67,66},{4,5},{5,4... | collective-permute-start | bytes 786440 | tf_op jit(solution)/shard_map/ppermute | solution.py:324
  21.7 5.1 %collective-permute-done.2.flag_ref = s32[1,128]{1,0:T(1,128)} collective-permute-done((s32[1,128]{1,0:T(1,128)S(1)}, s32[1,128]{1,0:T(1,128)}, u32[]{:S(2)}, u32[]{:S(2)}) %collective-permute-start.2) | collective-permute-done | bytes 544 | tf_op jit(solution)/shard_map/ppermute | solution.py:282
  26.9 3.4 %shared.1 = (bf16[128,1024]{1,0:T(8,128)(2,1)}, bf16[128,1024]{1,0:T(8,128)(2,1)}) custom-call(s32[1]{0:T(128)} %bitcast.2.side_ref, bf16[128,2048]{1,0:T(8,128)(2,1)} %collective-permute-done.1.other_ref, f32[1,2048]{1,0:T(1,128)S(1)} %bitcast.20, s32[1,128]{1,0:T(1,128)} %collective-permute-done.2.flag_ref, ...), custom_call_target="tpu_custom_call" | custom-call | tf_op jit(solution)/shard_map/shared/pallas_call | solution.py:325
  30.2 1.5 %collective-permute-start.3 = (bf16[128,1024]{1,0:T(8,128)(2,1)}, bf16[128,1024]{1,0:T(8,128)(2,1)S(1)}, u32[]{:S(2)}, u32[]{:S(2)}) collective-permute-start(bf16[128,1024]{1,0:T(8,128)(2,1)} %get-tuple-element.28), channel_id=1, source_target_pairs={{0,64},{1,65},{64,0},{65,1},{2,66},{3,67},{66,2},{67,3},{4,68},{5,... | collective-permute-start | bytes 786440 | tf_op jit(solution)/shard_map/ppermute | solution.py:332
  31.7 2.1 %collective-permute-start.4 = (bf16[128,1024]{1,0:T(8,128)(2,1)}, bf16[128,1024]{1,0:T(8,128)(2,1)S(1)}, u32[]{:S(2)}, u32[]{:S(2)}) collective-permute-start(bf16[128,1024]{1,0:T(8,128)(2,1)} %get-tuple-element.29), channel_id=1, source_target_pairs={{0,65},{1,64},{64,1},{65,0},{2,67},{3,66},{66,3},{67,2},{4,69},{5,... | collective-permute-start | bytes 786440 | tf_op jit(solution)/shard_map/ppermute | solution.py:333
  33.8 0.2 collective-permute-done
  34.0 3.4 %collective-permute-done.3 = bf16[128,1024]{1,0:T(8,128)(2,1)S(1)} collective-permute-done((bf16[128,1024]{1,0:T(8,128)(2,1)}, bf16[128,1024]{1,0:T(8,128)(2,1)S(1)}, u32[]{:S(2)}, u32[]{:S(2)}) %collective-permute-start.3) | collective-permute-done | bytes 262176 | tf_op jit(solution)/shard_map/ppermute | solution.py:332
  37.4 2.4 %collective-permute-done.4 = bf16[128,1024]{1,0:T(8,128)(2,1)S(1)} collective-permute-done((bf16[128,1024]{1,0:T(8,128)(2,1)}, bf16[128,1024]{1,0:T(8,128)(2,1)S(1)}, u32[]{:S(2)}, u32[]{:S(2)}) %collective-permute-start.4) | collective-permute-done | bytes 262176 | tf_op jit(solution)/shard_map/ppermute | solution.py:333
  39.8 6.6 %all-to-all-done.got_ref = bf16[32,40,1024]{2,1,0:T(8,128)(2,1)S(1)} async-done(((bf16[32,40,1024]{2,1,0:T(8,128)(2,1)}), bf16[32,40,1024]{2,1,0:T(8,128)(2,1)S(1)}, u32[]{:S(2)}, u32[]{:S(2)}) %all-to-all-start) | async-done | bytes 2621472 | tf_op jit(solution)/shard_map/all_to_all | solution.py:299
  46.4 9.2 %expert.1 = bf16[32,2,40,512]{3,2,1,0:T(8,128)(2,1)} custom-call(bf16[32,40,1024]{2,1,0:T(8,128)(2,1)S(1)} %all-to-all-done.got_ref, bf16[704,2048]{1,0:T(8,128)(2,1)} %bitcast.26, bf16[704,2048]{1,0:T(8,128)(2,1)} %bitcast.27, bf16[704,2048]{1,0:T(8,128)(2,1)} %bitcast.28), custom_call_target="tpu_custom_call" | custom-call | tf_op jit(solution)/shard_map/expert/pallas_call | solution.py:341
  55.7 6.6 %all-to-all-start.1 = ((bf16[64,40,512]{2,1,0:T(8,128)(2,1)}), bf16[64,40,512]{2,1,0:T(8,128)(2,1)S(1)}, u32[]{:S(2)}, u32[]{:S(2)}) async-start(bf16[64,40,512]{2,1,0:T(8,128)(2,1)} %bitcast.25), calls=%async_computation.1 | async-start | bytes 5242880 | tf_op jit(solution)/shard_map/all_to_all | solution.py:359
  62.3 1.4 %convert_add_fusion.base_ref = f32[128,1024]{1,0:T(8,128)S(1)} fusion(bf16[128,1024]{1,0:T(8,128)(2,1)} %copy-done.8, bf16[128,1024]{1,0:T(8,128)(2,1)} %copy-done.7, f32[128,1024]{1,0:T(8,128)} %get-tuple-element.33, bf16[128,1024]{1,0:T(8,128)(2,1)} %collective-permute-done), kind=kLoop, calls=%fused_computation | loop fusion | flops 786432 | bytes 1835008 | tf_op jit(solution)/shard_map/add | solution.py:337
  63.7 34.8 %all-to-all-done.1 = bf16[64,40,512]{2,1,0:T(8,128)(2,1)S(1)} async-done(((bf16[64,40,512]{2,1,0:T(8,128)(2,1)}), bf16[64,40,512]{2,1,0:T(8,128)(2,1)S(1)}, u32[]{:S(2)}, u32[]{:S(2)}) %all-to-all-start.1) | async-done | bytes 2621472 | tf_op jit(solution)/shard_map/all_to_all | solution.py:359
  98.5 1.7 %combine.1 = bf16[128,1024]{1,0:T(8,128)(2,1)} custom-call(bf16[32,2,40,512]{3,2,1,0:T(8,128)(2,1)S(1)} %bitcast.16, bf16[256,512]{1,0:T(8,128)(2,1)S(1)} %get-tuple-element.31.main_ref, bf16[256,256]{1,0:T(8,128)(2,1)S(1)} %copy-done.3, f32[128,1024]{1,0:T(8,128)S(1)} %convert_add_fusion.base_ref), custom_call_target="tpu_custom_call" | custom-call | tf_op jit(solution)/shard_map/combine/pallas_call | solution.py:362
  (14 shorter events, 0.0 us)
Async XLA Ops:
  3.2 8.7 %copy-start = (bf16[128,2048]{1,0:T(8,128)(2,1)S(1)}, bf16[128,2048]{1,0:T(8,128)(2,1)}, u32[]{:S(2)}) copy-start(bf16[128,2048]{1,0:T(8,128)(2,1)} %tok_ref.1) | copy-start | bytes 1572868
  3.2 10.2 %copy-start.6 = (s32[128]{0:T(128)S(1)}, s32[128]{0:T(128)}, u32[]{:S(2)}) copy-start(s32[128]{0:T(128)} %param.15) | copy-start | bytes 1540
  3.2 10.8 %copy-start.1 = (bf16[2048,32]{0,1:T(8,128)(2,1)S(1)}, bf16[2048,32]{0,1:T(8,128)(2,1)}, u32[]{:S(2)}) copy-start(bf16[2048,32]{0,1:T(8,128)(2,1)} %param.13) | copy-start | bytes 393220
  3.3 10.7 %copy-start.4 = (f32[2048]{0:T(1024)S(1)}, f32[2048]{0:T(1024)}, u32[]{:S(2)}) copy-start(f32[2048]{0:T(1024)} %param.12) | copy-start | bytes 24580
  3.3 10.7 %copy-start.5 = (s32[128,4]{0,1:T(4,128)S(1)}, s32[128,4]{0,1:T(4,128)}, u32[]{:S(2)}) copy-start(s32[128,4]{0,1:T(4,128)} %param.14) | copy-start | bytes 6148
  3.3 43.2 %all-to-all-start = ((bf16[32,40,1024]{2,1,0:T(8,128)(2,1)}), bf16[32,40,1024]{2,1,0:T(8,128)(2,1)S(1)}, u32[]{:S(2)}, u32[]{:S(2)}) async-start(bf16[32,40,1024]{2,1,0:T(8,128)(2,1)} %place.1), calls=%async_computation | async-start | bytes 5242880 | tf_op jit(solution)/shard_map/all_to_all | solution.py:299
  11.9 15.0 %collective-permute-start.1 = (bf16[128,2048]{1,0:T(8,128)(2,1)S(1)}, bf16[128,2048]{1,0:T(8,128)(2,1)}, u32[]{:S(2)}, u32[]{:S(2)}) collective-permute-start(bf16[128,2048]{1,0:T(8,128)(2,1)S(1)} %copy-done), channel_id=1, source_target_pairs={{0,64},{64,0},{1,65},{65,1},{2,66},{66,2},{3,67},{67,3},{4,68},{68... | collective-permute-start | bytes 1572872 | tf_op jit(solution)/shard_map/ppermute | solution.py:281
  13.5 13.4 %collective-permute-start.2 = (s32[1,128]{1,0:T(1,128)S(1)}, s32[1,128]{1,0:T(1,128)}, u32[]{:S(2)}, u32[]{:S(2)}) collective-permute-start(s32[1,128]{1,0:T(1,128)S(1)} %bitcast.23), channel_id=1, source_target_pairs={{0,64},{64,0},{1,65},{65,1},{2,66},{66,2},{3,67},{67,3},{4,68},{68... | collective-permute-start | bytes 1544 | tf_op jit(solution)/shard_map/ppermute | solution.py:282
  18.6 18.8 %copy-start.2 = (bf16[256,256]{1,0:T(8,128)(2,1)}, bf16[256,256]{1,0:T(8,128)(2,1)S(1)}, u32[]{:S(2)}) copy-start(bf16[256,256]{1,0:T(8,128)(2,1)S(1)} %get-tuple-element.32.rest_ref) | copy-start | bytes 393220
  18.6 15.4 %collective-permute-start = (bf16[128,1024]{1,0:T(8,128)(2,1)}, bf16[128,1024]{1,0:T(8,128)(2,1)}, u32[]{:S(2)}, u32[]{:S(2)}) collective-permute-start(bf16[128,1024]{1,0:T(8,128)(2,1)} %get-tuple-element.24), channel_id=1, source_target_pairs={{0,1},{1,0},{64,65},{65,64},{2,3},{3,2},{66,67},{67,66},{4,5},{5,4... | collective-permute-start | bytes 786440 | tf_op jit(solution)/shard_map/ppermute | solution.py:324
  30.2 7.2 %collective-permute-start.3 = (bf16[128,1024]{1,0:T(8,128)(2,1)}, bf16[128,1024]{1,0:T(8,128)(2,1)S(1)}, u32[]{:S(2)}, u32[]{:S(2)}) collective-permute-start(bf16[128,1024]{1,0:T(8,128)(2,1)} %get-tuple-element.28), channel_id=1, source_target_pairs={{0,64},{1,65},{64,0},{65,1},{2,66},{3,67},{66,2},{67,3},{4,68},{5,... | collective-permute-start | bytes 786440 | tf_op jit(solution)/shard_map/ppermute | solution.py:332
  31.7 8.1 %collective-permute-start.4 = (bf16[128,1024]{1,0:T(8,128)(2,1)}, bf16[128,1024]{1,0:T(8,128)(2,1)S(1)}, u32[]{:S(2)}, u32[]{:S(2)}) collective-permute-start(bf16[128,1024]{1,0:T(8,128)(2,1)} %get-tuple-element.29), channel_id=1, source_target_pairs={{0,65},{1,64},{64,1},{65,0},{2,67},{3,66},{66,3},{67,2},{4,69},{5,... | collective-permute-start | bytes 786440 | tf_op jit(solution)/shard_map/ppermute | solution.py:333
  37.4 18.3 %copy-start.7 = (bf16[128,1024]{1,0:T(8,128)(2,1)}, bf16[128,1024]{1,0:T(8,128)(2,1)S(1)}, u32[]{:S(2)}) copy-start(bf16[128,1024]{1,0:T(8,128)(2,1)S(1)} %collective-permute-done.3) | copy-start | bytes 786436
  39.8 15.9 %copy-start.8 = (bf16[128,1024]{1,0:T(8,128)(2,1)}, bf16[128,1024]{1,0:T(8,128)(2,1)S(1)}, u32[]{:S(2)}) copy-start(bf16[128,1024]{1,0:T(8,128)(2,1)S(1)} %collective-permute-done.4) | copy-start | bytes 786436
  55.7 42.8 %copy-start.3 = (bf16[256,256]{1,0:T(8,128)(2,1)S(1)}, bf16[256,256]{1,0:T(8,128)(2,1)}, u32[]{:S(2)}) copy-start(bf16[256,256]{1,0:T(8,128)(2,1)} %copy-done.2) | copy-start | bytes 393220
  55.7 42.8 %all-to-all-start.1 = ((bf16[64,40,512]{2,1,0:T(8,128)(2,1)}), bf16[64,40,512]{2,1,0:T(8,128)(2,1)S(1)}, u32[]{:S(2)}, u32[]{:S(2)}) async-start(bf16[64,40,512]{2,1,0:T(8,128)(2,1)} %bitcast.25), calls=%async_computation.1 | async-start | bytes 5242880 | tf_op jit(solution)/shard_map/all_to_all | solution.py:359

commit v5 on v4

--- a/solution.py
+++ b/solution.py
@@ -105,17 +105,11 @@
     weights = scores / jnp.sum(scores, axis=0, keepdims=True)
     slot = lax.broadcasted_iota(jnp.int32, (EX, MAIN, TK), 1).astype(f32)
     main = jnp.where(rank[:, None, :] == slot, weights[:, None, :], 0.0)
-    main = main.reshape(EX * MAIN, TK).T
-    coarse = main.astype(bf16)
-    main_ref[0:TK, :] = coarse
-    main_ref[TK:, :] = (main - coarse.astype(f32)).astype(bf16)
+    main_ref[...] = main.reshape(EX * MAIN, TK).T.astype(bf16)
     row = lax.broadcasted_iota(jnp.int32, (EX, 2 * REST, TK), 1)
     wanted = (row % REST + MAIN).astype(f32)
     rest = jnp.where(rank[:, None, :] == wanted, weights[:, None, :], 0.0)
-    rest = rest.reshape(EX * 2 * REST, TK).T
-    coarse = rest.astype(bf16)
-    rest_ref[0:TK, :] = coarse
-    rest_ref[TK:, :] = (rest - coarse.astype(f32)).astype(bf16)
+    rest_ref[...] = rest.reshape(EX * 2 * REST, TK).T.astype(bf16)
     for copy in copies:
         copy.wait()
     shared_terms(
@@ -244,7 +238,7 @@
             part = part + dot(few, rest)
             total = part if total is None else total + part
         cols = slice(h * quarter, (h + 1) * quarter)
-        out_ref[:, cols] = (base_ref[:, cols] + total[0:TK] + total[TK:]).astype(bf16)
+        out_ref[:, cols] = (base_ref[:, cols] + total).astype(bf16)
 
 
 def call(body, out_shape, **kw):
@@ -305,8 +299,8 @@
     main, rest, own, pair, *weights = call(
         weigh_kernel,
         (
-            sds((2 * TK, EX * MAIN), bf16),
-            sds((2 * TK, EX * 2 * REST), bf16),
+            sds((TK, EX * MAIN), bf16),
+            sds((TK, EX * 2 * REST), bf16),
             pltpu.HBM((TK, half), f32),
             piece,
             part,

time: 101 us -> 100 us (0.990)
  no operation moved by 1% of the time
where the time goes in v5:
time: 100 us; the launch traced here: 99.6 us
  waiting for transfers between devices  52 us (52%)
  starting transfers between devices  23.8 us (24%)
  Pallas kernels  21.6 us (22%)
  other arithmetic  1.4 us (1%)
    all_to_all x1, waiting for transfers between devices, per_device(): lax.all_to_all(results.reshape(2 * EX, BLK, half // 2), ('expert', 'tenso...  34.8 us
    pallas_call x1, Pallas kernels, per_device(): call(expert_kernel, pltpu.HBM((EX, 2, BLK, half // 2), bf16), in_specs=[v...  9.2 us
    all_to_all x1, starting transfers between devices, per_device(): got = lax.all_to_all(outgoing, 'expert', 0, 0, tiled=True)  8.59 us
    all_to_all x1, waiting for transfers between devices, per_device(): got = lax.all_to_all(outgoing, 'expert', 0, 0, tiled=True)  6.61 us
    all_to_all x1, starting transfers between devices, per_device(): lax.all_to_all(results.reshape(2 * EX, BLK, half // 2), ('expert', 'tenso...  6.42 us
    ppermute x1, waiting for transfers between devices, per_device(): other_flags = lax.ppermute(flags, 'dp', swap)  5.13 us
    pallas_call x1, Pallas kernels, per_device(): call(weigh_kernel, (sds((TK, EX * MAIN), bf16), sds((TK, EX * 2 * REST),...  4.62 us
    ppermute x1, waiting for transfers between devices, per_device(): near = lax.ppermute(near, four, [(i, i ^ 2) for i in range(4)])  3.46 us
  transfers between devices with their start and end apart: 7, of which 6 were waited for; matrix products, arithmetic and copies ran while one was open for 1% of the time, Pallas kernels for 8%

profile of v5, /device:TPU:0, one launch (start us, length us, event | category | flops | bytes accessed | tf_op | source)
XLA Modules:
  0.0 99.6 jit_solution(3311894164814554680)
XLA Ops:
  0.0 3.2 %place.1 = bf16[32,40,1024]{2,1,0:T(8,128)(2,1)} custom-call(bf16[128,2048]{1,0:T(8,128)(2,1)} %tok_ref.1, f32[1,2048]{1,0:T(1,128)} %bitcast.18, s32[4,128]{1,0:T(4,128)} %bitcast.21), custom_call_target="tpu_custom_call" | custom-call | tf_op jit(solution)/shard_map/place/pallas_call | solution.py:278
  3.2 0.0 copy-start
  3.2 0.0 copy-start.4
  3.3 0.0 copy-start.1
  3.3 0.0 copy-start.3
  3.3 8.6 %all-to-all-start = ((bf16[32,40,1024]{2,1,0:T(8,128)(2,1)}), bf16[32,40,1024]{2,1,0:T(8,128)(2,1)S(1)}, u32[]{:S(2)}, u32[]{:S(2)}) async-start(bf16[32,40,1024]{2,1,0:T(8,128)(2,1)} %place.1), calls=%async_computation | async-start | bytes 5242880 | tf_op jit(solution)/shard_map/all_to_all | solution.py:293
  11.9 1.6 %collective-permute-start.1 = (bf16[128,2048]{1,0:T(8,128)(2,1)S(1)}, bf16[128,2048]{1,0:T(8,128)(2,1)}, u32[]{:S(2)}, u32[]{:S(2)}) collective-permute-start(bf16[128,2048]{1,0:T(8,128)(2,1)S(1)} %copy-done), channel_id=1, source_target_pairs={{0,64},{64,0},{1,65},{65,1},{2,66},{66,2},{3,67},{67,3},{4,68},{68... | collective-permute-start | bytes 1572872 | tf_op jit(solution)/shard_map/ppermute | solution.py:275
  13.5 0.5 collective-permute-start.2
  14.0 4.6 %weigh.1 = (bf16[128,512]{1,0:T(8,128)(2,1)S(1)}, bf16[128,256]{1,0:T(8,128)(2,1)S(1)}, f32[128,1024]{1,0:T(8,128)}, bf16[128,1024]{1,0:T(8,128)(2,1)}, bf16[2,1...) custom-call(s32[1]{0:T(128)} %bitcast.2.side_ref, ...), custom_call_target="tpu_custom_call" | custom-call | tf_op jit(solution)/shard_map/weigh/pallas_call | solution.py:299
  18.6 3.1 %collective-permute-start = (bf16[128,1024]{1,0:T(8,128)(2,1)}, bf16[128,1024]{1,0:T(8,128)(2,1)S(1)}, u32[]{:S(2)}, u32[]{:S(2)}) collective-permute-start(bf16[128,1024]{1,0:T(8,128)(2,1)} %get-tuple-element.24), channel_id=1, source_target_pairs={{0,1},{1,0},{64,65},{65,64},{2,3},{3,2},{66,67},{67,66},{4,5},{5,4... | collective-permute-start | bytes 786440 | tf_op jit(solution)/shard_map/ppermute | solution.py:318
  21.7 5.1 %collective-permute-done.2.flag_ref = s32[1,128]{1,0:T(1,128)S(1)} collective-permute-done((s32[1,128]{1,0:T(1,128)S(1)}, s32[1,128]{1,0:T(1,128)S(1)}, u32[]{:S(2)}, u32[]{:S(2)}) %collective-permute-start.2) | collective-permute-done | bytes 544 | tf_op jit(solution)/shard_map/ppermute | solution.py:276
  26.9 3.3 %shared.1 = (bf16[128,1024]{1,0:T(8,128)(2,1)}, bf16[128,1024]{1,0:T(8,128)(2,1)}) custom-call(s32[1]{0:T(128)} %bitcast.2.side_ref, bf16[128,2048]{1,0:T(8,128)(2,1)} %collective-permute-done.1.other_ref, f32[1,2048]{1,0:T(1,128)S(1)} %bitcast.20, s32[1,128]{1,0:T(1,128)S(1)} %collective-permute-done.2.flag_ref, ...), custom_call_target="tpu_custom_call" | custom-call | tf_op jit(solution)/shard_map/shared/pallas_call | solution.py:319
  30.2 1.5 %collective-permute-start.3 = (bf16[128,1024]{1,0:T(8,128)(2,1)}, bf16[128,1024]{1,0:T(8,128)(2,1)S(1)}, u32[]{:S(2)}, u32[]{:S(2)}) collective-permute-start(bf16[128,1024]{1,0:T(8,128)(2,1)} %get-tuple-element.28), channel_id=1, source_target_pairs={{0,64},{1,65},{64,0},{65,1},{2,66},{3,67},{66,2},{67,3},{4,68},{5,... | collective-permute-start | bytes 786440 | tf_op jit(solution)/shard_map/ppermute | solution.py:326
  31.6 2.1 %collective-permute-start.4 = (bf16[128,1024]{1,0:T(8,128)(2,1)}, bf16[128,1024]{1,0:T(8,128)(2,1)}, u32[]{:S(2)}, u32[]{:S(2)}) collective-permute-start(bf16[128,1024]{1,0:T(8,128)(2,1)} %get-tuple-element.29), channel_id=1, source_target_pairs={{0,65},{1,64},{64,1},{65,0},{2,67},{3,66},{66,3},{67,2},{4,69},{5,... | collective-permute-start | bytes 786440 | tf_op jit(solution)/shard_map/ppermute | solution.py:327
  33.7 0.2 collective-permute-done
  33.9 3.5 %collective-permute-done.3 = bf16[128,1024]{1,0:T(8,128)(2,1)S(1)} collective-permute-done((bf16[128,1024]{1,0:T(8,128)(2,1)}, bf16[128,1024]{1,0:T(8,128)(2,1)S(1)}, u32[]{:S(2)}, u32[]{:S(2)}) %collective-permute-start.3) | collective-permute-done | bytes 262176 | tf_op jit(solution)/shard_map/ppermute | solution.py:326
  37.4 0.7 copy-done.6
  38.1 1.8 %collective-permute-done.4 = bf16[128,1024]{1,0:T(8,128)(2,1)} collective-permute-done((bf16[128,1024]{1,0:T(8,128)(2,1)}, bf16[128,1024]{1,0:T(8,128)(2,1)}, u32[]{:S(2)}, u32[]{:S(2)}) %collective-permute-start.4) | collective-permute-done | bytes 262176 | tf_op jit(solution)/shard_map/ppermute | solution.py:327
  39.8 6.6 %all-to-all-done.got_ref = bf16[32,40,1024]{2,1,0:T(8,128)(2,1)S(1)} async-done(((bf16[32,40,1024]{2,1,0:T(8,128)(2,1)}), bf16[32,40,1024]{2,1,0:T(8,128)(2,1)S(1)}, u32[]{:S(2)}, u32[]{:S(2)}) %all-to-all-start) | async-done | bytes 2621472 | tf_op jit(solution)/shard_map/all_to_all | solution.py:293
  46.5 9.2 %expert.1 = bf16[32,2,40,512]{3,2,1,0:T(8,128)(2,1)} custom-call(bf16[32,40,1024]{2,1,0:T(8,128)(2,1)S(1)} %all-to-all-done.got_ref, bf16[704,2048]{1,0:T(8,128)(2,1)} %bitcast.26, bf16[704,2048]{1,0:T(8,128)(2,1)} %bitcast.27, bf16[704,2048]{1,0:T(8,128)(2,1)} %bitcast.28), custom_call_target="tpu_custom_call" | custom-call | tf_op jit(solution)/shard_map/expert/pallas_call | solution.py:335
  55.7 6.4 %all-to-all-start.1 = ((bf16[64,40,512]{2,1,0:T(8,128)(2,1)}), bf16[64,40,512]{2,1,0:T(8,128)(2,1)S(1)}, u32[]{:S(2)}, u32[]{:S(2)}) async-start(bf16[64,40,512]{2,1,0:T(8,128)(2,1)} %bitcast.25), calls=%async_computation.1 | async-start | bytes 5242880 | tf_op jit(solution)/shard_map/all_to_all | solution.py:353
  62.1 1.4 %convert_add_fusion.base_ref = f32[128,1024]{1,0:T(8,128)S(1)} fusion(bf16[128,1024]{1,0:T(8,128)(2,1)} %collective-permute-done.4, bf16[128,1024]{1,0:T(8,128)(2,1)} %copy-done.6, f32[128,1024]{1,0:T(8,128)} %get-tuple-element.33, bf16[128,1024]{1,0:T(8,128)(2,1)} %copy-done.5), kind=kLoop, calls=%fused_computation | loop fusion | flops 786432 | bytes 1835008 | tf_op jit(solution)/shard_map/add | solution.py:331
  63.5 34.8 %all-to-all-done.1 = bf16[64,40,512]{2,1,0:T(8,128)(2,1)S(1)} async-done(((bf16[64,40,512]{2,1,0:T(8,128)(2,1)}), bf16[64,40,512]{2,1,0:T(8,128)(2,1)S(1)}, u32[]{:S(2)}, u32[]{:S(2)}) %all-to-all-start.1) | async-done | bytes 2621472 | tf_op jit(solution)/shard_map/all_to_all | solution.py:353
  98.3 1.3 %combine.1 = bf16[128,1024]{1,0:T(8,128)(2,1)} custom-call(bf16[32,2,40,512]{3,2,1,0:T(8,128)(2,1)S(1)} %bitcast.16, bf16[128,512]{1,0:T(8,128)(2,1)S(1)} %get-tuple-element.31.main_ref, bf16[128,256]{1,0:T(8,128)(2,1)S(1)} %get-tuple-element.32.rest_ref, f32[128,1024]{1,0:T(8,128)S(1)} %convert_add_fusion.base_ref), custom_call_target="tpu_custom_call" | custom-call | tf_op jit(solution)/shard_map/combine/pallas_call | solution.py:356
  (10 shorter events, 0.0 us)
Async XLA Ops:
  3.2 8.7 %copy-start = (bf16[128,2048]{1,0:T(8,128)(2,1)S(1)}, bf16[128,2048]{1,0:T(8,128)(2,1)}, u32[]{:S(2)}) copy-start(bf16[128,2048]{1,0:T(8,128)(2,1)} %tok_ref.1) | copy-start | bytes 1572868
  3.2 10.2 %copy-start.4 = (s32[128]{0:T(128)S(1)}, s32[128]{0:T(128)}, u32[]{:S(2)}) copy-start(s32[128]{0:T(128)} %param.15) | copy-start | bytes 1540
  3.3 10.8 %copy-start.1 = (bf16[2048,32]{0,1:T(8,128)(2,1)S(1)}, bf16[2048,32]{0,1:T(8,128)(2,1)}, u32[]{:S(2)}) copy-start(bf16[2048,32]{0,1:T(8,128)(2,1)} %param.13) | copy-start | bytes 393220
  3.3 10.7 %copy-start.2 = (f32[2048]{0:T(1024)S(1)}, f32[2048]{0:T(1024)}, u32[]{:S(2)}) copy-start(f32[2048]{0:T(1024)} %param.12) | copy-start | bytes 24580
  3.3 10.7 %copy-start.3 = (s32[128,4]{0,1:T(4,128)S(1)}, s32[128,4]{0,1:T(4,128)}, u32[]{:S(2)}) copy-start(s32[128,4]{0,1:T(4,128)} %param.14) | copy-start | bytes 6148
  3.3 43.2 %all-to-all-start = ((bf16[32,40,1024]{2,1,0:T(8,128)(2,1)}), bf16[32,40,1024]{2,1,0:T(8,128)(2,1)S(1)}, u32[]{:S(2)}, u32[]{:S(2)}) async-start(bf16[32,40,1024]{2,1,0:T(8,128)(2,1)} %place.1), calls=%async_computation | async-start | bytes 5242880 | tf_op jit(solution)/shard_map/all_to_all | solution.py:293
  11.9 15.0 %collective-permute-start.1 = (bf16[128,2048]{1,0:T(8,128)(2,1)S(1)}, bf16[128,2048]{1,0:T(8,128)(2,1)}, u32[]{:S(2)}, u32[]{:S(2)}) collective-permute-start(bf16[128,2048]{1,0:T(8,128)(2,1)S(1)} %copy-done), channel_id=1, source_target_pairs={{0,64},{64,0},{1,65},{65,1},{2,66},{66,2},{3,67},{67,3},{4,68},{68... | collective-permute-start | bytes 1572872 | tf_op jit(solution)/shard_map/ppermute | solution.py:275
  13.5 13.4 %collective-permute-start.2 = (s32[1,128]{1,0:T(1,128)S(1)}, s32[1,128]{1,0:T(1,128)S(1)}, u32[]{:S(2)}, u32[]{:S(2)}) collective-permute-start(s32[1,128]{1,0:T(1,128)S(1)} %bitcast.23), channel_id=1, source_target_pairs={{0,64},{64,0},{1,65},{65,1},{2,66},{66,2},{3,67},{67,3},{4,68},{68... | collective-permute-start | bytes 1544 | tf_op jit(solution)/shard_map/ppermute | solution.py:276
  18.6 15.3 %collective-permute-start = (bf16[128,1024]{1,0:T(8,128)(2,1)}, bf16[128,1024]{1,0:T(8,128)(2,1)S(1)}, u32[]{:S(2)}, u32[]{:S(2)}) collective-permute-start(bf16[128,1024]{1,0:T(8,128)(2,1)} %get-tuple-element.24), channel_id=1, source_target_pairs={{0,1},{1,0},{64,65},{65,64},{2,3},{3,2},{66,67},{67,66},{4,5},{5,4... | collective-permute-start | bytes 786440 | tf_op jit(solution)/shard_map/ppermute | solution.py:318
  30.2 7.2 %collective-permute-start.3 = (bf16[128,1024]{1,0:T(8,128)(2,1)}, bf16[128,1024]{1,0:T(8,128)(2,1)S(1)}, u32[]{:S(2)}, u32[]{:S(2)}) collective-permute-start(bf16[128,1024]{1,0:T(8,128)(2,1)} %get-tuple-element.28), channel_id=1, source_target_pairs={{0,64},{1,65},{64,0},{65,1},{2,66},{3,67},{66,2},{67,3},{4,68},{5,... | collective-permute-start | bytes 786440 | tf_op jit(solution)/shard_map/ppermute | solution.py:326
  31.6 8.2 %collective-permute-start.4 = (bf16[128,1024]{1,0:T(8,128)(2,1)}, bf16[128,1024]{1,0:T(8,128)(2,1)}, u32[]{:S(2)}, u32[]{:S(2)}) collective-permute-start(bf16[128,1024]{1,0:T(8,128)(2,1)} %get-tuple-element.29), channel_id=1, source_target_pairs={{0,65},{1,64},{64,1},{65,0},{2,67},{3,66},{66,3},{67,2},{4,69},{5,... | collective-permute-start | bytes 786440 | tf_op jit(solution)/shard_map/ppermute | solution.py:327
  33.9 3.5 %copy-start.5 = (bf16[128,1024]{1,0:T(8,128)(2,1)}, bf16[128,1024]{1,0:T(8,128)(2,1)S(1)}, u32[]{:S(2)}) copy-start(bf16[128,1024]{1,0:T(8,128)(2,1)S(1)} %collective-permute-done) | copy-start | bytes 786436
  37.4 0.7 copy-start.6
  55.7 42.7 %all-to-all-start.1 = ((bf16[64,40,512]{2,1,0:T(8,128)(2,1)}), bf16[64,40,512]{2,1,0:T(8,128)(2,1)S(1)}, u32[]{:S(2)}, u32[]{:S(2)}) async-start(bf16[64,40,512]{2,1,0:T(8,128)(2,1)} %bitcast.25), calls=%async_computation.1 | async-start | bytes 5242880 | tf_op jit(solution)/shard_map/all_to_all | solution.py:353

commit v6 on v5

--- a/solution.py
+++ b/solution.py
@@ -18,7 +18,7 @@
 BLK = 2 * (MAIN + REST)
 
 
-CUTS = (0, 256, 1 << 20)
+CUTS = (0, 320, 1 << 20)
 
 
 def normalise(values, gain):
@@ -69,9 +69,10 @@
     for copy in copies[1:]:
         copy.wait()
     normed = normalise(tok_ref[...], gain_ref[...])
-    step = 256
     sends = []
-    for c in range(0, half, step):
+    edges = [half * i // 8 for i in (0, 2, 4, 6, 7, 8)]
+    for c, end in zip(edges, edges[1:]):
+        step = end - c
         lo = normed[:, c : c + step]
         hi = normed[:, half + c : half + c + step]
         out_ref[:, 0:MAIN, c : c + step] = dot(main, lo).astype(bf16).reshape(EX, MAIN, step)
@@ -109,7 +110,9 @@
     row = lax.broadcasted_iota(jnp.int32, (EX, 2 * REST, TK), 1)
     wanted = (row % REST + MAIN).astype(f32)
     rest = jnp.where(rank[:, None, :] == wanted, weights[:, None, :], 0.0)
-    rest_ref[...] = rest.reshape(EX * 2 * REST, TK).T.astype(bf16)
+    for h in range(2):
+        part = jnp.where((row < REST) == (h == 0), rest, 0.0)
+        rest_ref[h] = part.reshape(EX * 2 * REST, TK).T.astype(bf16)
     for copy in copies:
         copy.wait()
     shared_terms(
@@ -226,16 +229,13 @@
 
 def combine_kernel(back_ref, main_ref, rest_ref, base_ref, out_ref):
     quarter = back_ref.shape[3]
-    lane = lax.broadcasted_iota(jnp.int32, rest_ref.shape, 1)
     for h in range(2):
-        mine = (lane % (2 * REST) < REST) == (h == 0)
-        few = jnp.where(mine, rest_ref[...].astype(f32), 0.0).astype(bf16)
         total = None
         for t in range(2):
             rows = back_ref[:, t, h * MAIN : (h + 1) * MAIN, :].reshape(EX * MAIN, quarter)
             part = dot(main_ref[...], rows)
             rest = back_ref[:, t, 2 * MAIN : BLK, :].reshape(EX * 2 * REST, quarter)
-            part = part + dot(few, rest)
+            part = part + dot(rest_ref[h], rest)
             total = part if total is None else total + part
         cols = slice(h * quarter, (h + 1) * quarter)
         out_ref[:, cols] = (base_ref[:, cols] + total).astype(bf16)
@@ -286,7 +286,7 @@
             pltpu.VMEM((expert_ids.shape[1], TK), jnp.int32),
             pltpu.VMEM((EX, BLK, half), bf16),
             pltpu.SemaphoreType.DMA((3,)),
-            pltpu.SemaphoreType.DMA((4,)),
+            pltpu.SemaphoreType.DMA((5,)),
         ],
         name="place",
     )(in_hbm(tokens), in_hbm(gain), in_hbm(expert_ids.T))
@@ -300,7 +300,7 @@
         weigh_kernel,
         (
             sds((TK, EX * MAIN), bf16),
-            sds((TK, EX * 2 * REST), bf16),
+            sds((2, TK, EX * 2 * REST), bf16),
             pltpu.HBM((TK, half), f32),
             piece,
             part,

time: 100 us -> 102 us (1.020)
  Pallas kernels: 21.6 us -> 23.2 us
    pallas_call x1, Pallas kernels: 9.2 us -> 10.8 us  [per_device(): call(expert_kernel, pltpu.HBM((EX, 2, BLK, half // 2), bf16), in_specs=[v...]
  transfers between devices with their start and end apart: 7 -> 7, of which waited for: 6 -> 5; matrix products, arithmetic and copies ran while one was open for 1% -> 1% of each run, Pallas kernels for 8% -> 8%
where the time goes in v6:
time: 102 us; the launch traced here: 101 us
  waiting for transfers between devices  51.9 us (51%)
  starting transfers between devices  23.8 us (23%)
  Pallas kernels  23.2 us (23%)
  other arithmetic  1.4 us (1%)
    all_to_all x1, waiting for transfers between devices, per_device(): lax.all_to_all(results.reshape(2 * EX, BLK, half // 2), ('expert', 'tenso...  34.8 us
    pallas_call x1, Pallas kernels, per_device(): call(expert_kernel, pltpu.HBM((EX, 2, BLK, half // 2), bf16), in_specs=[v...  10.8 us
    all_to_all x1, starting transfers between devices, per_device(): got = lax.all_to_all(outgoing, 'expert', 0, 0, tiled=True)  8.59 us
    all_to_all x1, waiting for transfers between devices, per_device(): got = lax.all_to_all(outgoing, 'expert', 0, 0, tiled=True)  6.61 us
    all_to_all x1, starting transfers between devices, per_device(): lax.all_to_all(results.reshape(2 * EX, BLK, half // 2), ('expert', 'tenso...  6.42 us
    ppermute x1, waiting for transfers between devices, per_device(): other_flags = lax.ppermute(flags, 'dp', swap)  5.23 us
    pallas_call x1, Pallas kernels, per_device(): call(weigh_kernel, (sds((TK, EX * MAIN), bf16), sds((2, TK, EX * 2 * REST...  4.62 us
    ppermute x1, waiting for transfers between devices, per_device(): near = lax.ppermute(near, four, [(i, i ^ 2) for i in range(4)])  3.42 us
  transfers between devices with their start and end apart: 7, of which 5 were waited for; matrix products, arithmetic and copies ran while one was open for 1% of the time, Pallas kernels for 8%

profile of v6, /device:TPU:0, one launch (start us, length us, event | category | flops | bytes accessed | tf_op | source)
XLA Modules:
  0.0 101.2 jit_solution(17896641201531233769)
XLA Ops:
  0.0 3.2 %place.1 = bf16[32,40,1024]{2,1,0:T(8,128)(2,1)} custom-call(bf16[128,2048]{1,0:T(8,128)(2,1)} %tok_ref.1, f32[1,2048]{1,0:T(1,128)} %bitcast.18, s32[4,128]{1,0:T(4,128)} %bitcast.21), custom_call_target="tpu_custom_call" | custom-call | tf_op jit(solution)/shard_map/place/pallas_call | solution.py:278
  3.2 0.0 copy-start
  3.2 0.0 copy-start.4
  3.2 0.0 copy-start.1
  3.3 0.0 copy-start.2
  3.3 0.0 copy-start.3
  3.3 8.6 %all-to-all-start = ((bf16[32,40,1024]{2,1,0:T(8,128)(2,1)}), bf16[32,40,1024]{2,1,0:T(8,128)(2,1)S(1)}, u32[]{:S(2)}, u32[]{:S(2)}) async-start(bf16[32,40,1024]{2,1,0:T(8,128)(2,1)} %place.1), calls=%async_computation | async-start | bytes 5242880 | tf_op jit(solution)/shard_map/all_to_all | solution.py:293
  11.9 1.6 %collective-permute-start.1 = (bf16[128,2048]{1,0:T(8,128)(2,1)S(1)}, bf16[128,2048]{1,0:T(8,128)(2,1)}, u32[]{:S(2)}, u32[]{:S(2)}) collective-permute-start(bf16[128,2048]{1,0:T(8,128)(2,1)S(1)} %copy-done), channel_id=1, source_target_pairs={{0,64},{64,0},{1,65},{65,1},{2,66},{66,2},{3,67},{67,3},{4,68},{68... | collective-permute-start | bytes 1572872 | tf_op jit(solution)/shard_map/ppermute | solution.py:275
  13.5 0.5 collective-permute-start.2
  14.0 4.6 %weigh.1 = (bf16[128,512]{1,0:T(8,128)(2,1)S(1)}, bf16[2,128,256]{2,1,0:T(8,128)(2,1)S(1)}, f32[128,1024]{1,0:T(8,128)}, bf16[128,1024]{1,0:T(8,128)(2,1)}, bf16...) custom-call(s32[1]{0:T(128)} %bitcast.2.side_ref, ...), custom_call_target="tpu_custom_call" | custom-call | tf_op jit(solution)/shard_map/weigh/pallas_call | solution.py:299
  18.6 3.1 %collective-permute-start = (bf16[128,1024]{1,0:T(8,128)(2,1)}, bf16[128,1024]{1,0:T(8,128)(2,1)S(1)}, u32[]{:S(2)}, u32[]{:S(2)}) collective-permute-start(bf16[128,1024]{1,0:T(8,128)(2,1)} %get-tuple-element.24), channel_id=1, source_target_pairs={{0,1},{1,0},{64,65},{65,64},{2,3},{3,2},{66,67},{67,66},{4,5},{5,4... | collective-permute-start | bytes 786440 | tf_op jit(solution)/shard_map/ppermute | solution.py:318
  21.7 5.2 %collective-permute-done.2.flag_ref = s32[1,128]{1,0:T(1,128)} collective-permute-done((s32[1,128]{1,0:T(1,128)S(1)}, s32[1,128]{1,0:T(1,128)}, u32[]{:S(2)}, u32[]{:S(2)}) %collective-permute-start.2) | collective-permute-done | bytes 544 | tf_op jit(solution)/shard_map/ppermute | solution.py:276
  27.0 3.3 %shared.1 = (bf16[128,1024]{1,0:T(8,128)(2,1)}, bf16[128,1024]{1,0:T(8,128)(2,1)}) custom-call(s32[1]{0:T(128)} %bitcast.2.side_ref, bf16[128,2048]{1,0:T(8,128)(2,1)} %collective-permute-done.1.other_ref, f32[1,2048]{1,0:T(1,128)S(1)} %bitcast.20, s32[1,128]{1,0:T(1,128)} %collective-permute-done.2.flag_ref, ...), custom_call_target="tpu_custom_call" | custom-call | tf_op jit(solution)/shard_map/shared/pallas_call | solution.py:319
  30.3 1.5 %collective-permute-start.3 = (bf16[128,1024]{1,0:T(8,128)(2,1)}, bf16[128,1024]{1,0:T(8,128)(2,1)S(1)}, u32[]{:S(2)}, u32[]{:S(2)}) collective-permute-start(bf16[128,1024]{1,0:T(8,128)(2,1)} %get-tuple-element.28), channel_id=1, source_target_pairs={{0,64},{1,65},{64,0},{65,1},{2,66},{3,67},{66,2},{67,3},{4,68},{5,... | collective-permute-start | bytes 786440 | tf_op jit(solution)/shard_map/ppermute | solution.py:326
  31.8 2.1 %collective-permute-start.4 = (bf16[128,1024]{1,0:T(8,128)(2,1)}, bf16[128,1024]{1,0:T(8,128)(2,1)}, u32[]{:S(2)}, u32[]{:S(2)}) collective-permute-start(bf16[128,1024]{1,0:T(8,128)(2,1)} %get-tuple-element.29), channel_id=1, source_target_pairs={{0,65},{1,64},{64,1},{65,0},{2,67},{3,66},{66,3},{67,2},{4,69},{5,... | collective-permute-start | bytes 786440 | tf_op jit(solution)/shard_map/ppermute | solution.py:327
  33.9 3.4 %collective-permute-done.3 = bf16[128,1024]{1,0:T(8,128)(2,1)S(1)} collective-permute-done((bf16[128,1024]{1,0:T(8,128)(2,1)}, bf16[128,1024]{1,0:T(8,128)(2,1)S(1)}, u32[]{:S(2)}, u32[]{:S(2)}) %collective-permute-start.3) | collective-permute-done | bytes 262176 | tf_op jit(solution)/shard_map/ppermute | solution.py:326
  37.3 0.7 copy-done.6
  38.0 1.8 %collective-permute-done.4 = bf16[128,1024]{1,0:T(8,128)(2,1)} collective-permute-done((bf16[128,1024]{1,0:T(8,128)(2,1)}, bf16[128,1024]{1,0:T(8,128)(2,1)}, u32[]{:S(2)}, u32[]{:S(2)}) %collective-permute-start.4) | collective-permute-done | bytes 262176 | tf_op jit(solution)/shard_map/ppermute | solution.py:327
  39.8 6.6 %all-to-all-done.got_ref = bf16[32,40,1024]{2,1,0:T(8,128)(2,1)S(1)} async-done(((bf16[32,40,1024]{2,1,0:T(8,128)(2,1)}), bf16[32,40,1024]{2,1,0:T(8,128)(2,1)S(1)}, u32[]{:S(2)}, u32[]{:S(2)}) %all-to-all-start) | async-done | bytes 2621472 | tf_op jit(solution)/shard_map/all_to_all | solution.py:293
  46.5 10.8 %expert.1 = bf16[32,2,40,512]{3,2,1,0:T(8,128)(2,1)} custom-call(bf16[32,40,1024]{2,1,0:T(8,128)(2,1)S(1)} %all-to-all-done.got_ref, bf16[704,2048]{1,0:T(8,128)(2,1)} %bitcast.26, bf16[704,2048]{1,0:T(8,128)(2,1)} %bitcast.27, bf16[704,2048]{1,0:T(8,128)(2,1)} %bitcast.28), custom_call_target="tpu_custom_call" | custom-call | tf_op jit(solution)/shard_map/expert/pallas_call | solution.py:335
  57.2 6.4 %all-to-all-start.1 = ((bf16[64,40,512]{2,1,0:T(8,128)(2,1)}), bf16[64,40,512]{2,1,0:T(8,128)(2,1)S(1)}, u32[]{:S(2)}, u32[]{:S(2)}) async-start(bf16[64,40,512]{2,1,0:T(8,128)(2,1)} %bitcast.25), calls=%async_computation.1 | async-start | bytes 5242880 | tf_op jit(solution)/shard_map/all_to_all | solution.py:353
  63.7 1.4 %convert_add_fusion.base_ref = f32[128,1024]{1,0:T(8,128)S(1)} fusion(bf16[128,1024]{1,0:T(8,128)(2,1)} %collective-permute-done.4, bf16[128,1024]{1,0:T(8,128)(2,1)} %copy-done.6, f32[128,1024]{1,0:T(8,128)} %get-tuple-element.33, bf16[128,1024]{1,0:T(8,128)(2,1)} %copy-done.5), kind=kLoop, calls=%fused_computation | loop fusion | flops 786432 | bytes 1835008 | tf_op jit(solution)/shard_map/add | solution.py:331
  65.1 34.8 %all-to-all-done.1 = bf16[64,40,512]{2,1,0:T(8,128)(2,1)S(1)} async-done(((bf16[64,40,512]{2,1,0:T(8,128)(2,1)}), bf16[64,40,512]{2,1,0:T(8,128)(2,1)S(1)}, u32[]{:S(2)}, u32[]{:S(2)}) %all-to-all-start.1) | async-done | bytes 2621472 | tf_op jit(solution)/shard_map/all_to_all | solution.py:353
  99.9 1.3 %combine.1 = bf16[128,1024]{1,0:T(8,128)(2,1)} custom-call(bf16[32,2,40,512]{3,2,1,0:T(8,128)(2,1)S(1)} %bitcast.16, bf16[128,512]{1,0:T(8,128)(2,1)S(1)} %get-tuple-element.31.main_ref, bf16[2,128,256]{2,1,0:T(8,128)(2,1)S(1)} %get-tuple-element.32.rest_ref, f32[128,1024]{1,0:T(8,128)S(1)} %convert_add_fusion.base_ref), custom_call_target="tpu_custom_call" | custom-call | tf_op jit(solution)/shard_map/combine/pallas_call | solution.py:356
  (10 shorter events, 0.0 us)
Async XLA Ops:
  3.2 8.7 %copy-start = (bf16[128,2048]{1,0:T(8,128)(2,1)S(1)}, bf16[128,2048]{1,0:T(8,128)(2,1)}, u32[]{:S(2)}) copy-start(bf16[128,2048]{1,0:T(8,128)(2,1)} %tok_ref.1) | copy-start | bytes 1572868
  3.2 10.2 %copy-start.4 = (s32[128]{0:T(128)S(1)}, s32[128]{0:T(128)}, u32[]{:S(2)}) copy-start(s32[128]{0:T(128)} %param.15) | copy-start | bytes 1540
  3.2 10.8 %copy-start.1 = (bf16[2048,32]{0,1:T(8,128)(2,1)S(1)}, bf16[2048,32]{0,1:T(8,128)(2,1)}, u32[]{:S(2)}) copy-start(bf16[2048,32]{0,1:T(8,128)(2,1)} %param.13) | copy-start | bytes 393220
  3.3 10.7 %copy-start.2 = (f32[2048]{0:T(1024)S(1)}, f32[2048]{0:T(1024)}, u32[]{:S(2)}) copy-start(f32[2048]{0:T(1024)} %param.12) | copy-start | bytes 24580
  3.3 10.7 %copy-start.3 = (s32[128,4]{0,1:T(4,128)S(1)}, s32[128,4]{0,1:T(4,128)}, u32[]{:S(2)}) copy-start(s32[128,4]{0,1:T(4,128)} %param.14) | copy-start | bytes 6148
  3.3 43.2 %all-to-all-start = ((bf16[32,40,1024]{2,1,0:T(8,128)(2,1)}), bf16[32,40,1024]{2,1,0:T(8,128)(2,1)S(1)}, u32[]{:S(2)}, u32[]{:S(2)}) async-start(bf16[32,40,1024]{2,1,0:T(8,128)(2,1)} %place.1), calls=%async_computation | async-start | bytes 5242880 | tf_op jit(solution)/shard_map/all_to_all | solution.py:293
  11.9 15.1 %collective-permute-start.1 = (bf16[128,2048]{1,0:T(8,128)(2,1)S(1)}, bf16[128,2048]{1,0:T(8,128)(2,1)}, u32[]{:S(2)}, u32[]{:S(2)}) collective-permute-start(bf16[128,2048]{1,0:T(8,128)(2,1)S(1)} %copy-done), channel_id=1, source_target_pairs={{0,64},{64,0},{1,65},{65,1},{2,66},{66,2},{3,67},{67,3},{4,68},{68... | collective-permute-start | bytes 1572872 | tf_op jit(solution)/shard_map/ppermute | solution.py:275
  13.5 13.5 %collective-permute-start.2 = (s32[1,128]{1,0:T(1,128)S(1)}, s32[1,128]{1,0:T(1,128)}, u32[]{:S(2)}, u32[]{:S(2)}) collective-permute-start(s32[1,128]{1,0:T(1,128)S(1)} %bitcast.23), channel_id=1, source_target_pairs={{0,64},{64,0},{1,65},{65,1},{2,66},{66,2},{3,67},{67,3},{4,68},{68... | collective-permute-start | bytes 1544 | tf_op jit(solution)/shard_map/ppermute | solution.py:276
  18.6 15.3 %collective-permute-start = (bf16[128,1024]{1,0:T(8,128)(2,1)}, bf16[128,1024]{1,0:T(8,128)(2,1)S(1)}, u32[]{:S(2)}, u32[]{:S(2)}) collective-permute-start(bf16[128,1024]{1,0:T(8,128)(2,1)} %get-tuple-element.24), channel_id=1, source_target_pairs={{0,1},{1,0},{64,65},{65,64},{2,3},{3,2},{66,67},{67,66},{4,5},{5,4... | collective-permute-start | bytes 786440 | tf_op jit(solution)/shard_map/ppermute | solution.py:318
  30.3 7.0 %collective-permute-start.3 = (bf16[128,1024]{1,0:T(8,128)(2,1)}, bf16[128,1024]{1,0:T(8,128)(2,1)S(1)}, u32[]{:S(2)}, u32[]{:S(2)}) collective-permute-start(bf16[128,1024]{1,0:T(8,128)(2,1)} %get-tuple-element.28), channel_id=1, source_target_pairs={{0,64},{1,65},{64,0},{65,1},{2,66},{3,67},{66,2},{67,3},{4,68},{5,... | collective-permute-start | bytes 786440 | tf_op jit(solution)/shard_map/ppermute | solution.py:326
  31.8 8.0 %collective-permute-start.4 = (bf16[128,1024]{1,0:T(8,128)(2,1)}, bf16[128,1024]{1,0:T(8,128)(2,1)}, u32[]{:S(2)}, u32[]{:S(2)}) collective-permute-start(bf16[128,1024]{1,0:T(8,128)(2,1)} %get-tuple-element.29), channel_id=1, source_target_pairs={{0,65},{1,64},{64,1},{65,0},{2,67},{3,66},{66,3},{67,2},{4,69},{5,... | collective-permute-start | bytes 786440 | tf_op jit(solution)/shard_map/ppermute | solution.py:327
  33.9 3.4 %copy-start.5 = (bf16[128,1024]{1,0:T(8,128)(2,1)}, bf16[128,1024]{1,0:T(8,128)(2,1)S(1)}, u32[]{:S(2)}) copy-start(bf16[128,1024]{1,0:T(8,128)(2,1)S(1)} %collective-permute-done) | copy-start | bytes 786436
  37.3 0.7 copy-start.6
  57.2 42.7 %all-to-all-start.1 = ((bf16[64,40,512]{2,1,0:T(8,128)(2,1)}), bf16[64,40,512]{2,1,0:T(8,128)(2,1)S(1)}, u32[]{:S(2)}, u32[]{:S(2)}) async-start(bf16[64,40,512]{2,1,0:T(8,128)(2,1)} %bitcast.25), calls=%async_computation.1 | async-start | bytes 5242880 | tf_op jit(solution)/shard_map/all_to_all | solution.py:353

commit v7 on v5

--- a/solution.py
+++ b/solution.py
@@ -190,7 +190,8 @@
             copy.wait()
         gate = dot_t(rows_ref[...], gate_ref[c : c + n, :])
         up = dot_t(rows_ref[...], up_ref[c : c + n, :])
-        hidden_ref[:, c : c + n] = (jax.nn.silu(gate) * up).astype(bf16)
+        gate = 0.5 * gate
+        hidden_ref[:, c : c + n] = ((gate + gate * jnp.tanh(gate)) * up).astype(bf16)
     loads[-1][0].wait()
     low = lax.broadcasted_iota(jnp.int32, (EX // 2, 8, quarter), 1) < REST
     sends = []

time: 100 us -> 100 us (level)
  no operation moved by 1% of the time
where the time goes in v7:
time: 100 us; the launch traced here: 99.7 us
  waiting for transfers between devices  52 us (52%)
  starting transfers between devices  23.8 us (24%)
  Pallas kernels  21.7 us (22%)
  other arithmetic  1.4 us (1%)
    all_to_all x1, waiting for transfers between devices, per_device(): lax.all_to_all(results.reshape(2 * EX, BLK, half // 2), ('expert', 'tenso...  34.8 us
    pallas_call x1, Pallas kernels, per_device(): call(expert_kernel, pltpu.HBM((EX, 2, BLK, half // 2), bf16), in_specs=[v...  9.28 us
    all_to_all x1, starting transfers between devices, per_device(): got = lax.all_to_all(outgoing, 'expert', 0, 0, tiled=True)  8.59 us
    all_to_all x1, waiting for transfers between devices, per_device(): got = lax.all_to_all(outgoing, 'expert', 0, 0, tiled=True)  6.61 us
    all_to_all x1, starting transfers between devices, per_device(): lax.all_to_all(results.reshape(2 * EX, BLK, half // 2), ('expert', 'tenso...  6.42 us
    ppermute x1, waiting for transfers between devices, per_device(): other_flags = lax.ppermute(flags, 'dp', swap)  5.13 us
    pallas_call x1, Pallas kernels, per_device(): call(weigh_kernel, (sds((TK, EX * MAIN), bf16), sds((TK, EX * 2 * REST),...  4.62 us
    ppermute x1, waiting for transfers between devices, per_device(): near = lax.ppermute(near, four, [(i, i ^ 2) for i in range(4)])  3.46 us
  transfers between devices with their start and end apart: 7, of which 6 were waited for; matrix products, arithmetic and copies ran while one was open for 1% of the time, Pallas kernels for 8%

profile of v7, /device:TPU:0, one launch (start us, length us, event | category | flops | bytes accessed | tf_op | source)
XLA Modules:
  0.0 99.7 jit_solution(8933786680081022799)
XLA Ops:
  0.0 3.2 %place.1 = bf16[32,40,1024]{2,1,0:T(8,128)(2,1)} custom-call(bf16[128,2048]{1,0:T(8,128)(2,1)} %tok_ref.1, f32[1,2048]{1,0:T(1,128)} %bitcast.18, s32[4,128]{1,0:T(4,128)} %bitcast.21), custom_call_target="tpu_custom_call" | custom-call | tf_op jit(solution)/shard_map/place/pallas_call | solution.py:279
  3.2 0.0 copy-start
  3.2 0.0 copy-start.4
  3.3 0.0 copy-start.1
  3.3 0.0 copy-start.3
  3.3 8.6 %all-to-all-start = ((bf16[32,40,1024]{2,1,0:T(8,128)(2,1)}), bf16[32,40,1024]{2,1,0:T(8,128)(2,1)S(1)}, u32[]{:S(2)}, u32[]{:S(2)}) async-start(bf16[32,40,1024]{2,1,0:T(8,128)(2,1)} %place.1), calls=%async_computation | async-start | bytes 5242880 | tf_op jit(solution)/shard_map/all_to_all | solution.py:294
  11.9 1.6 %collective-permute-start.1 = (bf16[128,2048]{1,0:T(8,128)(2,1)S(1)}, bf16[128,2048]{1,0:T(8,128)(2,1)}, u32[]{:S(2)}, u32[]{:S(2)}) collective-permute-start(bf16[128,2048]{1,0:T(8,128)(2,1)S(1)} %copy-done), channel_id=1, source_target_pairs={{0,64},{64,0},{1,65},{65,1},{2,66},{66,2},{3,67},{67,3},{4,68},{68... | collective-permute-start | bytes 1572872 | tf_op jit(solution)/shard_map/ppermute | solution.py:276
  13.5 0.5 collective-permute-start.2
  14.0 4.6 %weigh.1 = (bf16[128,512]{1,0:T(8,128)(2,1)S(1)}, bf16[128,256]{1,0:T(8,128)(2,1)S(1)}, f32[128,1024]{1,0:T(8,128)}, bf16[128,1024]{1,0:T(8,128)(2,1)}, bf16[2,1...) custom-call(s32[1]{0:T(128)} %bitcast.2.side_ref, ...), custom_call_target="tpu_custom_call" | custom-call | tf_op jit(solution)/shard_map/weigh/pallas_call | solution.py:300
  18.6 3.1 %collective-permute-start = (bf16[128,1024]{1,0:T(8,128)(2,1)}, bf16[128,1024]{1,0:T(8,128)(2,1)S(1)}, u32[]{:S(2)}, u32[]{:S(2)}) collective-permute-start(bf16[128,1024]{1,0:T(8,128)(2,1)} %get-tuple-element.24), channel_id=1, source_target_pairs={{0,1},{1,0},{64,65},{65,64},{2,3},{3,2},{66,67},{67,66},{4,5},{5,4... | collective-permute-start | bytes 786440 | tf_op jit(solution)/shard_map/ppermute | solution.py:319
  21.7 5.1 %collective-permute-done.2.flag_ref = s32[1,128]{1,0:T(1,128)S(1)} collective-permute-done((s32[1,128]{1,0:T(1,128)S(1)}, s32[1,128]{1,0:T(1,128)S(1)}, u32[]{:S(2)}, u32[]{:S(2)}) %collective-permute-start.2) | collective-permute-done | bytes 544 | tf_op jit(solution)/shard_map/ppermute | solution.py:277
  26.9 3.3 %shared.1 = (bf16[128,1024]{1,0:T(8,128)(2,1)}, bf16[128,1024]{1,0:T(8,128)(2,1)}) custom-call(s32[1]{0:T(128)} %bitcast.2.side_ref, bf16[128,2048]{1,0:T(8,128)(2,1)} %collective-permute-done.1.other_ref, f32[1,2048]{1,0:T(1,128)S(1)} %bitcast.20, s32[1,128]{1,0:T(1,128)S(1)} %collective-permute-done.2.flag_ref, ...), custom_call_target="tpu_custom_call" | custom-call | tf_op jit(solution)/shard_map/shared/pallas_call | solution.py:320
  30.2 1.5 %collective-permute-start.3 = (bf16[128,1024]{1,0:T(8,128)(2,1)}, bf16[128,1024]{1,0:T(8,128)(2,1)S(1)}, u32[]{:S(2)}, u32[]{:S(2)}) collective-permute-start(bf16[128,1024]{1,0:T(8,128)(2,1)} %get-tuple-element.28), channel_id=1, source_target_pairs={{0,64},{1,65},{64,0},{65,1},{2,66},{3,67},{66,2},{67,3},{4,68},{5,... | collective-permute-start | bytes 786440 | tf_op jit(solution)/shard_map/ppermute | solution.py:327
  31.6 2.1 %collective-permute-start.4 = (bf16[128,1024]{1,0:T(8,128)(2,1)}, bf16[128,1024]{1,0:T(8,128)(2,1)}, u32[]{:S(2)}, u32[]{:S(2)}) collective-permute-start(bf16[128,1024]{1,0:T(8,128)(2,1)} %get-tuple-element.29), channel_id=1, source_target_pairs={{0,65},{1,64},{64,1},{65,0},{2,67},{3,66},{66,3},{67,2},{4,69},{5,... | collective-permute-start | bytes 786440 | tf_op jit(solution)/shard_map/ppermute | solution.py:328
  33.7 0.2 collective-permute-done
  33.9 3.5 %collective-permute-done.3 = bf16[128,1024]{1,0:T(8,128)(2,1)S(1)} collective-permute-done((bf16[128,1024]{1,0:T(8,128)(2,1)}, bf16[128,1024]{1,0:T(8,128)(2,1)S(1)}, u32[]{:S(2)}, u32[]{:S(2)}) %collective-permute-start.3) | collective-permute-done | bytes 262176 | tf_op jit(solution)/shard_map/ppermute | solution.py:327
  37.4 0.7 copy-done.6
  38.1 1.8 %collective-permute-done.4 = bf16[128,1024]{1,0:T(8,128)(2,1)} collective-permute-done((bf16[128,1024]{1,0:T(8,128)(2,1)}, bf16[128,1024]{1,0:T(8,128)(2,1)}, u32[]{:S(2)}, u32[]{:S(2)}) %collective-permute-start.4) | collective-permute-done | bytes 262176 | tf_op jit(solution)/shard_map/ppermute | solution.py:328
  39.8 6.6 %all-to-all-done.got_ref = bf16[32,40,1024]{2,1,0:T(8,128)(2,1)S(1)} async-done(((bf16[32,40,1024]{2,1,0:T(8,128)(2,1)}), bf16[32,40,1024]{2,1,0:T(8,128)(2,1)S(1)}, u32[]{:S(2)}, u32[]{:S(2)}) %all-to-all-start) | async-done | bytes 2621472 | tf_op jit(solution)/shard_map/all_to_all | solution.py:294
  46.5 9.3 %expert.1 = bf16[32,2,40,512]{3,2,1,0:T(8,128)(2,1)} custom-call(bf16[32,40,1024]{2,1,0:T(8,128)(2,1)S(1)} %all-to-all-done.got_ref, bf16[704,2048]{1,0:T(8,128)(2,1)} %bitcast.26, bf16[704,2048]{1,0:T(8,128)(2,1)} %bitcast.27, bf16[704,2048]{1,0:T(8,128)(2,1)} %bitcast.28), custom_call_target="tpu_custom_call" | custom-call | tf_op jit(solution)/shard_map/expert/pallas_call | solution.py:336
  55.7 6.4 %all-to-all-start.1 = ((bf16[64,40,512]{2,1,0:T(8,128)(2,1)}), bf16[64,40,512]{2,1,0:T(8,128)(2,1)S(1)}, u32[]{:S(2)}, u32[]{:S(2)}) async-start(bf16[64,40,512]{2,1,0:T(8,128)(2,1)} %bitcast.25), calls=%async_computation.1 | async-start | bytes 5242880 | tf_op jit(solution)/shard_map/all_to_all | solution.py:354
  62.2 1.4 %convert_add_fusion.base_ref = f32[128,1024]{1,0:T(8,128)S(1)} fusion(bf16[128,1024]{1,0:T(8,128)(2,1)} %collective-permute-done.4, bf16[128,1024]{1,0:T(8,128)(2,1)} %copy-done.6, f32[128,1024]{1,0:T(8,128)} %get-tuple-element.33, bf16[128,1024]{1,0:T(8,128)(2,1)} %copy-done.5), kind=kLoop, calls=%fused_computation | loop fusion | flops 786432 | bytes 1835008 | tf_op jit(solution)/shard_map/add | solution.py:332
  63.6 34.8 %all-to-all-done.1 = bf16[64,40,512]{2,1,0:T(8,128)(2,1)S(1)} async-done(((bf16[64,40,512]{2,1,0:T(8,128)(2,1)}), bf16[64,40,512]{2,1,0:T(8,128)(2,1)S(1)}, u32[]{:S(2)}, u32[]{:S(2)}) %all-to-all-start.1) | async-done | bytes 2621472 | tf_op jit(solution)/shard_map/all_to_all | solution.py:354
  98.4 1.3 %combine.1 = bf16[128,1024]{1,0:T(8,128)(2,1)} custom-call(bf16[32,2,40,512]{3,2,1,0:T(8,128)(2,1)S(1)} %bitcast.16, bf16[128,512]{1,0:T(8,128)(2,1)S(1)} %get-tuple-element.31.main_ref, bf16[128,256]{1,0:T(8,128)(2,1)S(1)} %get-tuple-element.32.rest_ref, f32[128,1024]{1,0:T(8,128)S(1)} %convert_add_fusion.base_ref), custom_call_target="tpu_custom_call" | custom-call | tf_op jit(solution)/shard_map/combine/pallas_call | solution.py:357
  (10 shorter events, 0.0 us)
Async XLA Ops:
  3.2 8.7 %copy-start = (bf16[128,2048]{1,0:T(8,128)(2,1)S(1)}, bf16[128,2048]{1,0:T(8,128)(2,1)}, u32[]{:S(2)}) copy-start(bf16[128,2048]{1,0:T(8,128)(2,1)} %tok_ref.1) | copy-start | bytes 1572868
  3.2 10.2 %copy-start.4 = (s32[128]{0:T(128)S(1)}, s32[128]{0:T(128)}, u32[]{:S(2)}) copy-start(s32[128]{0:T(128)} %param.15) | copy-start | bytes 1540
  3.3 10.8 %copy-start.1 = (bf16[2048,32]{0,1:T(8,128)(2,1)S(1)}, bf16[2048,32]{0,1:T(8,128)(2,1)}, u32[]{:S(2)}) copy-start(bf16[2048,32]{0,1:T(8,128)(2,1)} %param.13) | copy-start | bytes 393220
  3.3 10.7 %copy-start.2 = (f32[2048]{0:T(1024)S(1)}, f32[2048]{0:T(1024)}, u32[]{:S(2)}) copy-start(f32[2048]{0:T(1024)} %param.12) | copy-start | bytes 24580
  3.3 10.7 %copy-start.3 = (s32[128,4]{0,1:T(4,128)S(1)}, s32[128,4]{0,1:T(4,128)}, u32[]{:S(2)}) copy-start(s32[128,4]{0,1:T(4,128)} %param.14) | copy-start | bytes 6148
  3.3 43.2 %all-to-all-start = ((bf16[32,40,1024]{2,1,0:T(8,128)(2,1)}), bf16[32,40,1024]{2,1,0:T(8,128)(2,1)S(1)}, u32[]{:S(2)}, u32[]{:S(2)}) async-start(bf16[32,40,1024]{2,1,0:T(8,128)(2,1)} %place.1), calls=%async_computation | async-start | bytes 5242880 | tf_op jit(solution)/shard_map/all_to_all | solution.py:294
  11.9 15.0 %collective-permute-start.1 = (bf16[128,2048]{1,0:T(8,128)(2,1)S(1)}, bf16[128,2048]{1,0:T(8,128)(2,1)}, u32[]{:S(2)}, u32[]{:S(2)}) collective-permute-start(bf16[128,2048]{1,0:T(8,128)(2,1)S(1)} %copy-done), channel_id=1, source_target_pairs={{0,64},{64,0},{1,65},{65,1},{2,66},{66,2},{3,67},{67,3},{4,68},{68... | collective-permute-start | bytes 1572872 | tf_op jit(solution)/shard_map/ppermute | solution.py:276
  13.5 13.4 %collective-permute-start.2 = (s32[1,128]{1,0:T(1,128)S(1)}, s32[1,128]{1,0:T(1,128)S(1)}, u32[]{:S(2)}, u32[]{:S(2)}) collective-permute-start(s32[1,128]{1,0:T(1,128)S(1)} %bitcast.23), channel_id=1, source_target_pairs={{0,64},{64,0},{1,65},{65,1},{2,66},{66,2},{3,67},{67,3},{4,68},{68... | collective-permute-start | bytes 1544 | tf_op jit(solution)/shard_map/ppermute | solution.py:277
  18.6 15.3 %collective-permute-start = (bf16[128,1024]{1,0:T(8,128)(2,1)}, bf16[128,1024]{1,0:T(8,128)(2,1)S(1)}, u32[]{:S(2)}, u32[]{:S(2)}) collective-permute-start(bf16[128,1024]{1,0:T(8,128)(2,1)} %get-tuple-element.24), channel_id=1, source_target_pairs={{0,1},{1,0},{64,65},{65,64},{2,3},{3,2},{66,67},{67,66},{4,5},{5,4... | collective-permute-start | bytes 786440 | tf_op jit(solution)/shard_map/ppermute | solution.py:319
  30.2 7.2 %collective-permute-start.3 = (bf16[128,1024]{1,0:T(8,128)(2,1)}, bf16[128,1024]{1,0:T(8,128)(2,1)S(1)}, u32[]{:S(2)}, u32[]{:S(2)}) collective-permute-start(bf16[128,1024]{1,0:T(8,128)(2,1)} %get-tuple-element.28), channel_id=1, source_target_pairs={{0,64},{1,65},{64,0},{65,1},{2,66},{3,67},{66,2},{67,3},{4,68},{5,... | collective-permute-start | bytes 786440 | tf_op jit(solution)/shard_map/ppermute | solution.py:327
  31.6 8.2 %collective-permute-start.4 = (bf16[128,1024]{1,0:T(8,128)(2,1)}, bf16[128,1024]{1,0:T(8,128)(2,1)}, u32[]{:S(2)}, u32[]{:S(2)}) collective-permute-start(bf16[128,1024]{1,0:T(8,128)(2,1)} %get-tuple-element.29), channel_id=1, source_target_pairs={{0,65},{1,64},{64,1},{65,0},{2,67},{3,66},{66,3},{67,2},{4,69},{5,... | collective-permute-start | bytes 786440 | tf_op jit(solution)/shard_map/ppermute | solution.py:328
  33.9 3.5 %copy-start.5 = (bf16[128,1024]{1,0:T(8,128)(2,1)}, bf16[128,1024]{1,0:T(8,128)(2,1)S(1)}, u32[]{:S(2)}) copy-start(bf16[128,1024]{1,0:T(8,128)(2,1)S(1)} %collective-permute-done) | copy-start | bytes 786436
  37.4 0.7 copy-start.6
  55.7 42.7 %all-to-all-start.1 = ((bf16[64,40,512]{2,1,0:T(8,128)(2,1)}), bf16[64,40,512]{2,1,0:T(8,128)(2,1)S(1)}, u32[]{:S(2)}, u32[]{:S(2)}) async-start(bf16[64,40,512]{2,1,0:T(8,128)(2,1)} %bitcast.25), calls=%async_computation.1 | async-start | bytes 5242880 | tf_op jit(solution)/shard_map/all_to_all | solution.py:354
